TPU v7x, 32 devices: a whole 2x2x4 slice. The times are simulated.
32 devices in a mesh: subj: 4 (over y, x), cortex: 8 (over z, core).
Axes of the slice: x: 2, y: 2, z: 4, core: 2. Of those that a mesh axis runs over, the one named last changes fastest.
Arguments:
- series: bfloat16 [8, 1024, 2048], P('subj', None, 'cortex'), may hold values from -6 to 6
- template: bfloat16 [1024, 2048], P(None, 'cortex'), may hold values from -6 to 6
- sl_blocks: int32 [16, 3], P('cortex'), may hold values from 0 to 15, as said below
Outputs:
- template_new: float32 [1024, 2048], P(None, 'cortex')
Inputs may be any that keep to these rules, and one draw needn't show every extreme that they name: sl_blocks[g, 0] = g; the other two entries of row g are distinct, differ from g, and lie between (g // 2 - 1) * 2 and (g // 2 + 2) * 2 - 1.
All inputs are finite; a program needn't handle non-finite values.
Results may differ from a plain program's by a relative error of at most 0.0024.
Values may be sent and summed in bfloat16 or wider, within the bound.
No kernel may reach another device: no remote copies, remote signals or barrier semaphores. Data moves between devices by JAX's collectives and lax.ppermute only.
A program may use at most 64 MiB of HBM per device.

v0:
```python
import functools

import jax
import jax.numpy as jnp
from jax import lax
from jax.experimental import pallas as pl
from jax.experimental.pallas import tpu as pltpu
from jax.sharding import PartitionSpec as P


BLOCK = 128
NS_STEPS = 8
RIDGE_SHIFT = 0.1
NORM_EPSILON = 1e-06
MIB = 1 << 20


def swap_near(value):
    count = lax.axis_size("cortex")
    return lax.ppermute(value, "cortex", [(i, i ^ 1) for i in range(count)])


def swap_far(value):
    count = lax.axis_size("cortex")
    route = [(0, 0), (count - 1, count - 1)]
    for i in range(1, count - 1, 2):
        route += [(i, i + 1), (i + 1, i)]
    return lax.ppermute(value, "cortex", route)


def swap_subj(value, distance):
    count = lax.axis_size("subj")
    return lax.ppermute(value, "subj", [(i, i ^ distance) for i in range(count)])


def vmem():
    return pl.BlockSpec(memory_space=pltpu.VMEM)


def smem():
    return pl.BlockSpec(memory_space=pltpu.SMEM)


def call(kernel, out_shape, in_specs, flops, limit, scratch=()):
    outs = jax.tree.leaves(out_shape)
    return pl.pallas_call(
        kernel,
        out_shape=out_shape,
        in_specs=in_specs,
        out_specs=jax.tree.map(lambda _: vmem(), out_shape),
        scratch_shapes=list(scratch),
        compiler_params=pltpu.CompilerParams(vmem_limit_bytes=limit * MIB),
        cost_estimate=pl.CostEstimate(
            flops=flops, bytes_accessed=sum(o.size * o.dtype.itemsize for o in outs), transcendentals=0
        ),
    )


def columns(ref, half):
    return ref[:, pl.ds(pl.multiple_of(half * BLOCK, BLOCK), BLOCK)]


def template_kernel(code_ref, own_ref, near_ref, far_ref, out_ref):
    lights, members = code_ref.shape
    for g in range(lights):
        for j in range(members):
            code = code_ref[g, j]
            for place, ref in enumerate((own_ref, near_ref, far_ref)):

                @pl.when(code // 2 == place)
                def _():
                    out_ref[g, j * BLOCK : (j + 1) * BLOCK, :] = columns(ref, code % 2).T


def newton_schulz(now):
    head = now.shape[0] - BLOCK
    top, low = now[:head], now[head:]
    over = (((1,), (1,)), ((), ()))
    corner = lax.dot_general(top, top, over, preferred_element_type=jnp.float32).astype(jnp.bfloat16)
    bottom = lax.dot_general(low, now, over, preferred_element_type=jnp.float32).astype(jnp.bfloat16)
    gram = jnp.concatenate([jnp.concatenate([corner, bottom[:, :head].T], axis=1), bottom], axis=0)
    product = jnp.dot(gram, now, preferred_element_type=jnp.float32)
    return (1.5 * now.astype(jnp.float32) - 0.5 * product).astype(jnp.bfloat16)


def polar_kernel(code_ref, tmpl_ref, own_ref, near_ref, far_ref, map_ref, cols_ref):
    lights, members = code_ref.shape
    width = members * BLOCK
    frames = own_ref.shape[0]
    for g in range(lights):
        for i in range(members):
            code = code_ref[g, i]
            lo = g * width + i * BLOCK
            for place, ref in enumerate((own_ref, near_ref, far_ref)):

                @pl.when(code // 2 == place)
                def _():
                    cols_ref[:, lo : lo + BLOCK] = columns(ref, code % 2)

    row = lax.broadcasted_iota(jnp.int32, (width, width), 0)
    col = lax.broadcasted_iota(jnp.int32, (width, width), 1)
    ridge = jnp.where(row == col, RIDGE_SHIFT, 0.0)
    for g in range(lights):
        cross = jnp.dot(
            tmpl_ref[g], cols_ref[:, g * width : (g + 1) * width], preferred_element_type=jnp.float32
        )
        cross = cross * (1.0 / frames) + ridge
        squares = jnp.sum(cross * cross, keepdims=True)
        map_ref[g] = (cross * (1.0 / jnp.sqrt(squares + NORM_EPSILON))).astype(jnp.bfloat16)

    for _ in range(NS_STEPS):
        for g in range(lights):
            map_ref[g] = newton_schulz(map_ref[g])


def map_kernel(subj_count, places, splits, code_ref, *refs):
    cols_refs = refs[:subj_count]
    map_refs = refs[subj_count : 2 * subj_count]
    weight_ref = refs[-1]
    out_refs = refs[2 * subj_count : -1]
    lights, members = code_ref.shape
    width = members * BLOCK
    for p, place in enumerate(places):
        for g in range(lights):
            pick = jnp.int32(0)
            found = code_ref[g, 0] == place
            for j in range(1, members):
                hit = code_ref[g, j] == place
                pick = jnp.where(hit, j, pick)
                found = jnp.logical_or(found, hit)
            rows = pl.ds(pl.multiple_of(pick * BLOCK, BLOCK), BLOCK)
            for s in range(subj_count):
                lo = (s * lights + g) * width
                piece = map_refs[s][g, rows, :]
                weight_ref[p * BLOCK : (p + 1) * BLOCK, lo : lo + width] = jnp.where(
                    found, piece, jnp.zeros_like(piece)
                )
    depth = lights * width
    step_cols = len(places) * BLOCK // len(splits)
    chunk = 256
    at = 0
    for n, pieces in enumerate(splits):
        first = n * step_cols
        weights = [
            weight_ref[first : first + step_cols, s * depth : (s + 1) * depth] for s in range(subj_count)
        ]
        rows = cols_refs[0].shape[0] // pieces
        for piece in range(pieces):
            for lo in range(0, rows, chunk):
                total = None
                for s in range(subj_count):
                    term = lax.dot_general(
                        cols_refs[s][piece * rows + lo : piece * rows + lo + chunk, :],
                        weights[s],
                        (((1,), (1,)), ((), ())),
                        preferred_element_type=jnp.float32,
                    )
                    total = term if total is None else total + term
                out_refs[at][lo : lo + chunk, :] = total.astype(out_refs[at].dtype)
            at += 1


def body(series, template, sl_blocks):
    subj_count, frames, width_dev = series.shape
    lights, members = sl_blocks.shape
    blk_dev = width_dev // BLOCK
    width = members * BLOCK
    count = lax.axis_size("cortex")
    position = lax.axis_index("cortex")
    odd = position % 2
    far_real = jnp.logical_and(position + 2 * odd - 1 >= 0, position + 2 * odd - 1 < count)

    tmpl_far = swap_far(template)
    tmpl_near = swap_near(template)
    parts = [series[s] for s in range(subj_count)]
    far, near = [], []
    for part in parts:
        far.append(swap_far(part))
        near.append(swap_near(part))
    lists_near = swap_near(sl_blocks)
    lists_far = swap_far(sl_blocks)

    window = sl_blocks - (position - 1) * blk_dev
    side = window // blk_dev
    place = jnp.where(side == 1, 0, jnp.where((side == 2) == (odd == 1), 2, 1))
    code = (place * blk_dev + window % blk_dev).astype(jnp.int32)

    mine = position * blk_dev + jnp.arange(blk_dev, dtype=jnp.int32)

    def counted(lists):
        return jnp.sum((lists.reshape(-1)[:, None] == mine[None, :]).astype(jnp.float32), axis=0)

    coverage = counted(sl_blocks) + counted(lists_near) + jnp.where(far_real, counted(lists_far), 0.0)
    per_vertex = jnp.repeat(coverage, BLOCK)

    tmpl_rows = call(
        template_kernel,
        jax.ShapeDtypeStruct((lights, width, frames), jnp.bfloat16),
        [smem(), vmem(), vmem(), vmem()],
        flops=10**9,
        limit=16,
    )(code, template, tmpl_near, tmpl_far)

    maps, cols = [], []
    for s in range(subj_count):
        if s == subj_count - 1:
            code, per_vertex = lax.optimization_barrier((code, per_vertex))
        polar, gathered = call(
            polar_kernel,
            (
                jax.ShapeDtypeStruct((lights, width, width), jnp.bfloat16),
                jax.ShapeDtypeStruct((frames, lights * width), jnp.bfloat16),
            ),
            [smem()] + [vmem()] * 4,
            flops=8 * 10**9,
            limit=24,
        )(code, tmpl_rows, parts[s], near[s], far[s])
        maps.append(polar)
        cols.append(gathered)

    def mapped(code, places, splits, types):
        shapes = [
            jax.ShapeDtypeStruct((frames // pieces, width_dev), kind)
            for pieces, kind in zip(splits, types)
            for _ in range(pieces)
        ]
        return call(
            functools.partial(map_kernel, subj_count, places, splits),
            shapes,
            [smem()] + [vmem()] * (2 * subj_count),
            flops=len(places) * 4 * 10**8,
            limit=24,
            scratch=[pltpu.VMEM((len(places) * BLOCK, subj_count * lights * width), jnp.bfloat16)],
        )(code, *cols, *maps)

    blocks = list(range(blk_dev))
    to_far = mapped(code, [2 * blk_dev + b for b in blocks], (2,), (jnp.bfloat16,))
    from_far = []
    for h in range(2):
        from_far.append(swap_far(to_far[h]))
    code, _ = lax.optimization_barrier((code, to_far[0]))
    to_near, *own = mapped(code, [blk_dev + b for b in blocks] + blocks, (1, 2), (jnp.bfloat16, jnp.float32))
    from_near = swap_near(to_near)
    keep = far_real.astype(jnp.float32)

    subj_size = lax.axis_size("subj")
    distances = []
    while 2 ** len(distances) < subj_size:
        distances.append(2 ** len(distances))
    rows = frames // 2
    halves = []
    for h in range(2):
        mine_h = own[h]
        if h > 0:
            mine_h, halves[0] = lax.optimization_barrier((mine_h, halves[0]))
        near_h = from_near[h * rows : (h + 1) * rows].astype(jnp.float32)
        halves.append((mine_h + near_h + keep * from_far[h].astype(jnp.float32)).astype(jnp.bfloat16))
    for step in range(len(distances)):
        for h in range(2):
            sent = halves[h].astype(jnp.bfloat16)
            got = swap_subj(sent, distances[(step + h) % len(distances)])
            halves[h] = sent.astype(jnp.float32) + got.astype(jnp.float32)
    total = jnp.concatenate(halves, axis=0)
    return total / per_vertex[None, :] / (subj_count * subj_size)


def solution(mesh):
    def step(series, template, sl_blocks):
        in_specs = (P("subj", None, "cortex"), P(None, "cortex"), P("cortex", None))
        out_specs = P(None, "cortex")
        placed = jax.shard_map(body, mesh=mesh, in_specs=in_specs, out_specs=out_specs, check_vma=False)
        return placed(series, template, sl_blocks)

    return step
```

profile of v0, /device:TPU:8, one launch (start us, length us, event | category | flops | bytes accessed | tf_op | source)
XLA Modules:
  0.0 73.4 jit_solution(9309866360420989566)
XLA Ops:
  0.0 2.0 %collective-permute-start.1 = (s32[2,3]{1,0:T(2,128)}, s32[2,3]{1,0:T(2,128)S(1)}, u32[]{:S(2)}, u32[]{:S(2)}) collective-permute-start(s32[2,3]{1,0:T(2,128)} %param.5), channel_id=1, source_target_pairs={{0,0},{7,7},{1,2},{2,1},{3,4},{4,3},{5,6},{6,5},{8,8},{15,15},{9,1... | collective-permute-start | bytes 80 | tf_op jit(solution)/shard_map/ppermute | solution.py:28
  2.1 1.7 %collective-permute-start = (s32[2,3]{1,0:T(2,128)}, s32[2,3]{1,0:T(2,128)S(1)}, u32[]{:S(2)}, u32[]{:S(2)}) collective-permute-start(s32[2,3]{1,0:T(2,128)} %param.5), channel_id=1, source_target_pairs={{0,1},{1,0},{2,3},{3,2},{4,5},{5,4},{6,7},{7,6},{8,9},{9,8},{10,11... | collective-permute-start | bytes 80 | tf_op jit(solution)/shard_map/ppermute | solution.py:20
  3.8 0.1 collective-permute-start.2
  3.9 2.4 %collective-permute-start.3 = (bf16[1024,256]{1,0:T(8,128)(2,1)}, bf16[1024,256]{1,0:T(8,128)(2,1)S(1)}, u32[]{:S(2)}, u32[]{:S(2)}) collective-permute-start(bf16[1024,256]{1,0:T(8,128)(2,1)} %own_ref.1), channel_id=1, source_target_pairs={{0,0},{7,7},{1,2},{2,1},{3,4},{4,3},{5,6},{6,5},{8,8},{15,15},{9,1... | collective-permute-start | bytes 1572872 | tf_op jit(solution)/shard_map/ppermute | solution.py:28
  6.3 1.3 %slice_bitcast_fusion = (bf16[1024,256]{1,0:T(8,128)(2,1)S(1)}, bf16[1024,256]{1,0:T(8,128)(2,1)S(1)}) fusion(bf16[2,1024,256]{2,1,0:T(8,128)(2,1)} %param.3), kind=kLoop, calls=%fused_computation.8 | loop fusion | bytes 2097152 | tf_op jit(solution)/shard_map/squeeze | solution.py:175
  7.5 3.2 %collective-permute-start.5 = (bf16[1024,256]{1,0:T(8,128)(2,1)S(1)}, bf16[1024,256]{1,0:T(8,128)(2,1)S(1)}, u32[]{:S(2)}, u32[]{:S(2)}) collective-permute-start(bf16[1024,256]{1,0:T(8,128)(2,1)S(1)} %get-tuple-element.37.own_ref), channel_id=1, source_target_pairs={{0,0},{7,7},{1,2},{2,1},{3,4},{4,3},{5,6},{6,5},{8,8},{15,15},{9,1... | collective-permute-start | bytes 1572872 | tf_op jit(solution)/shard_map/ppermute | solution.py:28
  10.7 0.1 eq.65
  10.8 0.0 collective-permute-done.1
  10.9 0.5 collective-permute-start.4
  11.3 0.1 eq.72
  11.4 0.0 collective-permute-done
  11.4 2.0 %collective-permute-start.7 = (bf16[1024,256]{1,0:T(8,128)(2,1)S(1)}, bf16[1024,256]{1,0:T(8,128)(2,1)}, u32[]{:S(2)}, u32[]{:S(2)}) collective-permute-start(bf16[1024,256]{1,0:T(8,128)(2,1)S(1)} %get-tuple-element.36.own_ref), channel_id=1, source_target_pairs={{0,0},{7,7},{1,2},{2,1},{3,4},{4,3},{5,6},{6,5},{8,8},{15,15},{9,1... | collective-permute-start | bytes 1572872 | tf_op jit(solution)/shard_map/ppermute | solution.py:28
  13.4 0.1 eq.69
  13.5 0.2 fusion.4
  13.7 0.1 broadcast_bitcast_fusion
  13.8 0.0 collective-permute-done.2.near_ref
  13.8 1.6 %collective-permute-start.6 = (bf16[1024,256]{1,0:T(8,128)(2,1)S(1)}, bf16[1024,256]{1,0:T(8,128)(2,1)S(1)}, u32[]{:S(2)}, u32[]{:S(2)}) collective-permute-start(bf16[1024,256]{1,0:T(8,128)(2,1)S(1)} %get-tuple-element.36.own_ref), channel_id=1, source_target_pairs={{0,1},{1,0},{2,3},{3,2},{4,5},{5,4},{6,7},{7,6},{8,9},{9,8},{10,11... | collective-permute-start | bytes 1572872 | tf_op jit(solution)/shard_map/ppermute | solution.py:20
  15.4 0.0 collective-permute-done.3.far_ref
  15.4 1.4 %shard_map.37.tmpl_ref = bf16[2,384,1024]{2,1,0:T(8,128)(2,1)S(1)} custom-call(s32[2,3]{1,0:T(2,128)S(1)} %fusion.2.code_ref, bf16[1024,256]{1,0:T(8,128)(2,1)S(1)} %copy-done, bf16[1024,256]{1,0:T(8,128)(2,1)S(1)} %collective-permute-done.2.near_ref, bf16[1024,256]{1,0:T(8,128)(2,1)S(1)} %collective-permute-done.3.far_ref), custom_call_target="tpu_custom_call" | custom-call | flops 1000000000 | bytes 1572864 | tf_op jit(solution)/shard_map/pallas_call | solution.py:196
  16.8 3.4 %collective-permute-done.5.far_ref = bf16[1024,256]{1,0:T(8,128)(2,1)S(1)} collective-permute-done((bf16[1024,256]{1,0:T(8,128)(2,1)S(1)}, bf16[1024,256]{1,0:T(8,128)(2,1)S(1)}, u32[]{:S(2)}, u32[]{:S(2)}) %collective-permute-start.5) | collective-permute-done | bytes 524320 | tf_op jit(solution)/shard_map/ppermute | solution.py:28
  20.2 0.0 collective-permute-done.4.near_ref
  20.2 8.9 %shard_map.38 = (bf16[2,384,384]{2,1,0:T(8,128)(2,1)S(1)}, bf16[1024,768]{1,0:T(8,128)(2,1)S(1)}) custom-call(s32[2,3]{1,0:T(2,128)S(1)} %fusion.2.code_ref, bf16[2,384,1024]{2,1,0:T(8,128)(2,1)S(1)} %shard_map.37.tmpl_ref, bf16[1024,256]{1,0:T(8,128)(2,1)S(1)} %get-tuple-element.37.own_ref, bf16[1024,256]{1,0:T(8,128)(2,1)} %collective-permute-done.4.near_ref, ...), custom_call_target="tpu_custom_call" | custom-call | flops 8000000000 | bytes 2162688 | tf_op jit(solution)/shard_map/pallas_call | solution.py:208
  29.1 0.0 collective-permute-done.7.far_ref
  29.1 0.0 collective-permute-done.6.near_ref
  29.1 9.0 %shard_map.39 = (bf16[2,384,384]{2,1,0:T(8,128)(2,1)S(1)}, bf16[1024,768]{1,0:T(8,128)(2,1)S(1)}) custom-call(s32[2,3]{1,0:T(2,128)S(1)} %fusion.2.code_ref, bf16[2,384,1024]{2,1,0:T(8,128)(2,1)S(1)} %shard_map.37.tmpl_ref, bf16[1024,256]{1,0:T(8,128)(2,1)S(1)} %get-tuple-element.36.own_ref, bf16[1024,256]{1,0:T(8,128)(2,1)S(1)} %collective-permute-done.6.near_ref, ...), custom_call_target="tpu_custom_call" | custom-call | flops 8000000000 | bytes 2162688 | tf_op jit(solution)/shard_map/pallas_call | solution.py:208
  38.2 1.6 %shard_map.40 = (bf16[512,256]{1,0:T(8,128)(2,1)S(1)}, bf16[512,256]{1,0:T(8,128)(2,1)S(1)}) custom-call(s32[2,3]{1,0:T(2,128)S(1)} %fusion.2.code_ref, bf16[1024,768]{1,0:T(8,128)(2,1)S(1)} %get-tuple-element.20.refs_0_, bf16[1024,768]{1,0:T(8,128)(2,1)S(1)} %get-tuple-element.21.refs_1_, bf16[2,384,384]{2,1,0:T(8,128)(2,1)S(1)} %get-tuple-element.22.refs_2_, ...), custom_call_target="tpu_custom_call" | custom-call | flops 800000000 | bytes 524288 | tf_op jit(solution)/shard_map/pallas_call | solution.py:227
  39.7 2.4 %shard_map.41 = (bf16[1024,256]{1,0:T(8,128)(2,1)S(1)}, f32[512,256]{1,0:T(8,128)S(1)}, f32[512,256]{1,0:T(8,128)S(1)}) custom-call(s32[2,3]{1,0:T(2,128)S(1)} %fusion.2.code_ref, bf16[1024,768]{1,0:T(8,128)(2,1)S(1)} %get-tuple-element.20.refs_0_, bf16[1024,768]{1,0:T(8,128)(2,1)S(1)} %get-tuple-element.21.refs_1_, ...), custom_call_target="tpu_custom_call" | custom-call | flops 1600000000 | bytes 1572864 | tf_op jit(solution)/shard_map/pallas_call | solution.py:227
  42.1 0.9 %collective-permute-start.8 = (bf16[1024,256]{1,0:T(8,128)(2,1)S(1)}, bf16[1024,256]{1,0:T(8,128)(2,1)S(1)}, u32[]{:S(2)}, u32[]{:S(2)}) collective-permute-start(bf16[1024,256]{1,0:T(8,128)(2,1)S(1)} %get-tuple-element.28), channel_id=1, source_target_pairs={{0,1},{1,0},{2,3},{3,2},{4,5},{5,4},{6,7},{7,6},{8,9},{9,8},{10,11... | collective-permute-start | bytes 1572872 | tf_op jit(solution)/shard_map/ppermute | solution.py:20
  43.0 1.9 %collective-permute-start.9 = (bf16[512,256]{1,0:T(8,128)(2,1)S(1)}, bf16[512,256]{1,0:T(8,128)(2,1)S(1)}, u32[]{:S(2)}, u32[]{:S(2)}) collective-permute-start(bf16[512,256]{1,0:T(8,128)(2,1)S(1)} %get-tuple-element.24), channel_id=1, source_target_pairs={{0,0},{7,7},{1,2},{2,1},{3,4},{4,3},{5,6},{6,5},{8,8},{15,15},{9,1... | collective-permute-start | bytes 786440 | tf_op jit(solution)/shard_map/ppermute | solution.py:28
  44.9 3.6 %collective-permute-start.12 = (bf16[512,256]{1,0:T(8,128)(2,1)S(1)}, bf16[512,256]{1,0:T(8,128)(2,1)S(1)}, u32[]{:S(2)}, u32[]{:S(2)}) collective-permute-start(bf16[512,256]{1,0:T(8,128)(2,1)S(1)} %get-tuple-element.31), channel_id=1, source_target_pairs={{0,0},{7,7},{1,2},{2,1},{3,4},{4,3},{5,6},{6,5},{8,8},{15,15},{9,1... | collective-permute-start | bytes 786440 | tf_op jit(solution)/shard_map/ppermute | solution.py:28
  48.6 2.1 %collective-permute-done.9 = bf16[512,256]{1,0:T(8,128)(2,1)S(1)} collective-permute-done((bf16[512,256]{1,0:T(8,128)(2,1)S(1)}, bf16[512,256]{1,0:T(8,128)(2,1)S(1)}, u32[]{:S(2)}, u32[]{:S(2)}) %collective-permute-start.9) | collective-permute-done | bytes 262176 | tf_op jit(solution)/shard_map/ppermute | solution.py:28
  50.7 0.0 collective-permute-done.8
  50.7 0.1 add_convert_fusion.3
  50.8 2.7 %collective-permute-done.12 = bf16[512,256]{1,0:T(8,128)(2,1)S(1)} collective-permute-done((bf16[512,256]{1,0:T(8,128)(2,1)S(1)}, bf16[512,256]{1,0:T(8,128)(2,1)S(1)}, u32[]{:S(2)}, u32[]{:S(2)}) %collective-permute-start.12) | collective-permute-done | bytes 262176 | tf_op jit(solution)/shard_map/ppermute | solution.py:28
  53.5 0.1 add_convert_fusion.1
  53.6 1.6 %collective-permute-start.13 = (bf16[512,256]{1,0:T(8,128)(2,1)S(1)}, bf16[512,256]{1,0:T(8,128)(2,1)S(1)}, u32[]{:S(2)}, u32[]{:S(2)}) collective-permute-start(bf16[512,256]{1,0:T(8,128)(2,1)S(1)} %add_convert_fusion.1), channel_id=1, source_target_pairs={{0,16},{8,24},{16,0},{24,8},{1,17},{9,25},{17,1},{25,9},{2,18},{10... | collective-permute-start | bytes 786440 | tf_op jit(solution)/shard_map/ppermute | solution.py:33
  55.2 1.5 %collective-permute-start.10 = (bf16[512,256]{1,0:T(8,128)(2,1)S(1)}, bf16[512,256]{1,0:T(8,128)(2,1)S(1)}, u32[]{:S(2)}, u32[]{:S(2)}) collective-permute-start(bf16[512,256]{1,0:T(8,128)(2,1)S(1)} %add_convert_fusion.3), channel_id=1, source_target_pairs={{0,8},{8,0},{16,24},{24,16},{1,9},{9,1},{17,25},{25,17},{2,10},{10... | collective-permute-start | bytes 786440 | tf_op jit(solution)/shard_map/ppermute | solution.py:33
  56.7 6.0 %collective-permute-done.13 = bf16[512,256]{1,0:T(8,128)(2,1)S(1)} collective-permute-done((bf16[512,256]{1,0:T(8,128)(2,1)S(1)}, bf16[512,256]{1,0:T(8,128)(2,1)S(1)}, u32[]{:S(2)}, u32[]{:S(2)}) %collective-permute-start.13) | collective-permute-done | bytes 262176 | tf_op jit(solution)/shard_map/ppermute | solution.py:33
  62.7 0.1 add_convert_fusion
  62.8 1.5 %collective-permute-start.14 = (bf16[512,256]{1,0:T(8,128)(2,1)S(1)}, bf16[512,256]{1,0:T(8,128)(2,1)S(1)}, u32[]{:S(2)}, u32[]{:S(2)}) collective-permute-start(bf16[512,256]{1,0:T(8,128)(2,1)S(1)} %add_convert_fusion), channel_id=1, source_target_pairs={{0,8},{8,0},{16,24},{24,16},{1,9},{9,1},{17,25},{25,17},{2,10},{10... | collective-permute-start | bytes 786440 | tf_op jit(solution)/shard_map/ppermute | solution.py:33
  64.3 0.0 collective-permute-done.10
  64.3 0.1 add_convert_fusion.2
  64.4 1.6 %collective-permute-start.11 = (bf16[512,256]{1,0:T(8,128)(2,1)S(1)}, bf16[512,256]{1,0:T(8,128)(2,1)S(1)}, u32[]{:S(2)}, u32[]{:S(2)}) collective-permute-start(bf16[512,256]{1,0:T(8,128)(2,1)S(1)} %add_convert_fusion.2), channel_id=1, source_target_pairs={{0,16},{8,24},{16,0},{24,8},{1,17},{9,25},{17,1},{25,9},{2,18},{10... | collective-permute-start | bytes 786440 | tf_op jit(solution)/shard_map/ppermute | solution.py:33
  66.0 5.0 %collective-permute-done.14 = bf16[512,256]{1,0:T(8,128)(2,1)S(1)} collective-permute-done((bf16[512,256]{1,0:T(8,128)(2,1)S(1)}, bf16[512,256]{1,0:T(8,128)(2,1)S(1)}, u32[]{:S(2)}, u32[]{:S(2)}) %collective-permute-start.14) | collective-permute-done | bytes 262176 | tf_op jit(solution)/shard_map/ppermute | solution.py:33
  71.0 0.1 convert_add_fusion
  71.1 1.3 %collective-permute-done.11 = bf16[512,256]{1,0:T(8,128)(2,1)S(1)} collective-permute-done((bf16[512,256]{1,0:T(8,128)(2,1)S(1)}, bf16[512,256]{1,0:T(8,128)(2,1)S(1)}, u32[]{:S(2)}, u32[]{:S(2)}) %collective-permute-start.11) | collective-permute-done | bytes 262176 | tf_op jit(solution)/shard_map/ppermute | solution.py:33
  72.3 0.1 convert_add_fusion.1
  72.4 1.1 %fusion = f32[1024,256]{1,0:T(8,128)} fusion(f32[512,256]{1,0:T(8,128)S(1)} %convert_add_fusion, f32[512,256]{1,0:T(8,128)S(1)} %convert_add_fusion.1, f32[256]{0:T(256)S(1)} %broadcast_bitcast_fusion), kind=kLoop, calls=%fused_computation.1 | loop fusion | flops 786432 | bytes 2098176 | tf_op jit(solution)/shard_map/div | solution.py:264
  (7 shorter events, 0.0 us)
Async XLA Ops:
  0.0 10.7 %copy-start.1 = (s32[2,3]{1,0:T(2,128)S(1)}, s32[2,3]{1,0:T(2,128)}, u32[]{:S(2)}) copy-start(s32[2,3]{1,0:T(2,128)} %param.5) | copy-start | bytes 76
  0.0 15.4 %copy-start = (bf16[1024,256]{1,0:T(8,128)(2,1)S(1)}, bf16[1024,256]{1,0:T(8,128)(2,1)}, u32[]{:S(2)}) copy-start(bf16[1024,256]{1,0:T(8,128)(2,1)} %own_ref.1) | copy-start | bytes 1572868
  0.0 10.8 %collective-permute-start.1 = (s32[2,3]{1,0:T(2,128)}, s32[2,3]{1,0:T(2,128)S(1)}, u32[]{:S(2)}, u32[]{:S(2)}) collective-permute-start(s32[2,3]{1,0:T(2,128)} %param.5), channel_id=1, source_target_pairs={{0,0},{7,7},{1,2},{2,1},{3,4},{4,3},{5,6},{6,5},{8,8},{15,15},{9,1... | collective-permute-start | bytes 80 | tf_op jit(solution)/shard_map/ppermute | solution.py:28
  2.1 9.4 %collective-permute-start = (s32[2,3]{1,0:T(2,128)}, s32[2,3]{1,0:T(2,128)S(1)}, u32[]{:S(2)}, u32[]{:S(2)}) collective-permute-start(s32[2,3]{1,0:T(2,128)} %param.5), channel_id=1, source_target_pairs={{0,1},{1,0},{2,3},{3,2},{4,5},{5,4},{6,7},{7,6},{8,9},{9,8},{10,11... | collective-permute-start | bytes 80 | tf_op jit(solution)/shard_map/ppermute | solution.py:20
  3.8 10.0 %collective-permute-start.2 = (bf16[1024,256]{1,0:T(8,128)(2,1)}, bf16[1024,256]{1,0:T(8,128)(2,1)S(1)}, u32[]{:S(2)}, u32[]{:S(2)}) collective-permute-start(bf16[1024,256]{1,0:T(8,128)(2,1)} %own_ref.1), channel_id=1, source_target_pairs={{0,1},{1,0},{2,3},{3,2},{4,5},{5,4},{6,7},{7,6},{8,9},{9,8},{10,11... | collective-permute-start | bytes 1572872 | tf_op jit(solution)/shard_map/ppermute | solution.py:20
  3.9 11.5 %collective-permute-start.3 = (bf16[1024,256]{1,0:T(8,128)(2,1)}, bf16[1024,256]{1,0:T(8,128)(2,1)S(1)}, u32[]{:S(2)}, u32[]{:S(2)}) collective-permute-start(bf16[1024,256]{1,0:T(8,128)(2,1)} %own_ref.1), channel_id=1, source_target_pairs={{0,0},{7,7},{1,2},{2,1},{3,4},{4,3},{5,6},{6,5},{8,8},{15,15},{9,1... | collective-permute-start | bytes 1572872 | tf_op jit(solution)/shard_map/ppermute | solution.py:28
  7.5 12.7 %collective-permute-start.5 = (bf16[1024,256]{1,0:T(8,128)(2,1)S(1)}, bf16[1024,256]{1,0:T(8,128)(2,1)S(1)}, u32[]{:S(2)}, u32[]{:S(2)}) collective-permute-start(bf16[1024,256]{1,0:T(8,128)(2,1)S(1)} %get-tuple-element.37.own_ref), channel_id=1, source_target_pairs={{0,0},{7,7},{1,2},{2,1},{3,4},{4,3},{5,6},{6,5},{8,8},{15,15},{9,1... | collective-permute-start | bytes 1572872 | tf_op jit(solution)/shard_map/ppermute | solution.py:28
  10.9 9.3 %collective-permute-start.4 = (bf16[1024,256]{1,0:T(8,128)(2,1)S(1)}, bf16[1024,256]{1,0:T(8,128)(2,1)}, u32[]{:S(2)}, u32[]{:S(2)}) collective-permute-start(bf16[1024,256]{1,0:T(8,128)(2,1)S(1)} %get-tuple-element.37.own_ref), channel_id=1, source_target_pairs={{0,1},{1,0},{2,3},{3,2},{4,5},{5,4},{6,7},{7,6},{8,9},{9,8},{10,11... | collective-permute-start | bytes 1572872 | tf_op jit(solution)/shard_map/ppermute | solution.py:20
  11.4 17.6 %collective-permute-start.7 = (bf16[1024,256]{1,0:T(8,128)(2,1)S(1)}, bf16[1024,256]{1,0:T(8,128)(2,1)}, u32[]{:S(2)}, u32[]{:S(2)}) collective-permute-start(bf16[1024,256]{1,0:T(8,128)(2,1)S(1)} %get-tuple-element.36.own_ref), channel_id=1, source_target_pairs={{0,0},{7,7},{1,2},{2,1},{3,4},{4,3},{5,6},{6,5},{8,8},{15,15},{9,1... | collective-permute-start | bytes 1572872 | tf_op jit(solution)/shard_map/ppermute | solution.py:28
  13.8 15.3 %collective-permute-start.6 = (bf16[1024,256]{1,0:T(8,128)(2,1)S(1)}, bf16[1024,256]{1,0:T(8,128)(2,1)S(1)}, u32[]{:S(2)}, u32[]{:S(2)}) collective-permute-start(bf16[1024,256]{1,0:T(8,128)(2,1)S(1)} %get-tuple-element.36.own_ref), channel_id=1, source_target_pairs={{0,1},{1,0},{2,3},{3,2},{4,5},{5,4},{6,7},{7,6},{8,9},{9,8},{10,11... | collective-permute-start | bytes 1572872 | tf_op jit(solution)/shard_map/ppermute | solution.py:20
  42.1 8.6 %collective-permute-start.8 = (bf16[1024,256]{1,0:T(8,128)(2,1)S(1)}, bf16[1024,256]{1,0:T(8,128)(2,1)S(1)}, u32[]{:S(2)}, u32[]{:S(2)}) collective-permute-start(bf16[1024,256]{1,0:T(8,128)(2,1)S(1)} %get-tuple-element.28), channel_id=1, source_target_pairs={{0,1},{1,0},{2,3},{3,2},{4,5},{5,4},{6,7},{7,6},{8,9},{9,8},{10,11... | collective-permute-start | bytes 1572872 | tf_op jit(solution)/shard_map/ppermute | solution.py:20
  43.0 7.7 %collective-permute-start.9 = (bf16[512,256]{1,0:T(8,128)(2,1)S(1)}, bf16[512,256]{1,0:T(8,128)(2,1)S(1)}, u32[]{:S(2)}, u32[]{:S(2)}) collective-permute-start(bf16[512,256]{1,0:T(8,128)(2,1)S(1)} %get-tuple-element.24), channel_id=1, source_target_pairs={{0,0},{7,7},{1,2},{2,1},{3,4},{4,3},{5,6},{6,5},{8,8},{15,15},{9,1... | collective-permute-start | bytes 786440 | tf_op jit(solution)/shard_map/ppermute | solution.py:28
  44.9 8.6 %collective-permute-start.12 = (bf16[512,256]{1,0:T(8,128)(2,1)S(1)}, bf16[512,256]{1,0:T(8,128)(2,1)S(1)}, u32[]{:S(2)}, u32[]{:S(2)}) collective-permute-start(bf16[512,256]{1,0:T(8,128)(2,1)S(1)} %get-tuple-element.31), channel_id=1, source_target_pairs={{0,0},{7,7},{1,2},{2,1},{3,4},{4,3},{5,6},{6,5},{8,8},{15,15},{9,1... | collective-permute-start | bytes 786440 | tf_op jit(solution)/shard_map/ppermute | solution.py:28
  53.6 9.1 %collective-permute-start.13 = (bf16[512,256]{1,0:T(8,128)(2,1)S(1)}, bf16[512,256]{1,0:T(8,128)(2,1)S(1)}, u32[]{:S(2)}, u32[]{:S(2)}) collective-permute-start(bf16[512,256]{1,0:T(8,128)(2,1)S(1)} %add_convert_fusion.1), channel_id=1, source_target_pairs={{0,16},{8,24},{16,0},{24,8},{1,17},{9,25},{17,1},{25,9},{2,18},{10... | collective-permute-start | bytes 786440 | tf_op jit(solution)/shard_map/ppermute | solution.py:33
  55.2 9.1 %collective-permute-start.10 = (bf16[512,256]{1,0:T(8,128)(2,1)S(1)}, bf16[512,256]{1,0:T(8,128)(2,1)S(1)}, u32[]{:S(2)}, u32[]{:S(2)}) collective-permute-start(bf16[512,256]{1,0:T(8,128)(2,1)S(1)} %add_convert_fusion.3), channel_id=1, source_target_pairs={{0,8},{8,0},{16,24},{24,16},{1,9},{9,1},{17,25},{25,17},{2,10},{10... | collective-permute-start | bytes 786440 | tf_op jit(solution)/shard_map/ppermute | solution.py:33
  62.8 8.2 %collective-permute-start.14 = (bf16[512,256]{1,0:T(8,128)(2,1)S(1)}, bf16[512,256]{1,0:T(8,128)(2,1)S(1)}, u32[]{:S(2)}, u32[]{:S(2)}) collective-permute-start(bf16[512,256]{1,0:T(8,128)(2,1)S(1)} %add_convert_fusion), channel_id=1, source_target_pairs={{0,8},{8,0},{16,24},{24,16},{1,9},{9,1},{17,25},{25,17},{2,10},{10... | collective-permute-start | bytes 786440 | tf_op jit(solution)/shard_map/ppermute | solution.py:33
  64.4 7.9 %collective-permute-start.11 = (bf16[512,256]{1,0:T(8,128)(2,1)S(1)}, bf16[512,256]{1,0:T(8,128)(2,1)S(1)}, u32[]{:S(2)}, u32[]{:S(2)}) collective-permute-start(bf16[512,256]{1,0:T(8,128)(2,1)S(1)} %add_convert_fusion.2), channel_id=1, source_target_pairs={{0,16},{8,24},{16,0},{24,8},{1,17},{9,25},{17,1},{25,9},{2,18},{10... | collective-permute-start | bytes 786440 | tf_op jit(solution)/shard_map/ppermute | solution.py:33
where the time goes:
time: 73.8 us; the launch traced here: 73.4 us
  starting transfers between devices  26.1 us (35%)
  Pallas kernels  23.3 us (32%)
  waiting for transfers between devices  20.5 us (28%)
  other arithmetic  1.76 us (2%)
  local copies, waits for them, and re-layouts  1.59 us (2%)
    pallas_call x2, Pallas kernels, body(): call(polar_kernel, (jax.ShapeDtypeStruct((lights, width, width), jnp.bflo...  17.9 us
    ppermute x6, starting transfers between devices, swap_far(): return lax.ppermute(value, 'cortex', route)  15.1 us
    ppermute x4, waiting for transfers between devices, swap_subj(): lax.ppermute(value, 'subj', [(i, i ^ distance) for i in range(count)])  12.3 us
    ppermute x6, waiting for transfers between devices, swap_far(): return lax.ppermute(value, 'cortex', route)  8.2 us
    ppermute x4, starting transfers between devices, swap_subj(): lax.ppermute(value, 'subj', [(i, i ^ distance) for i in range(count)])  6.19 us
    ppermute x5, starting transfers between devices, swap_near(): return lax.ppermute(value, 'cortex', [(i, i ^ 1) for i in range(count)])  4.83 us
    pallas_call x2, Pallas kernels, mapped(): call(functools.partial(map_kernel, subj_count, places, splits), shapes, [...  3.95 us
  transfers between devices with their start and end apart: 15, of which 6 were waited for; matrix products, arithmetic and copies ran while one was open for 3% of the time, Pallas kernels for 14%

commit v1 on v0

--- a/solution.py
+++ b/solution.py
@@ -12,7 +12,9 @@
 NS_STEPS = 8
 RIDGE_SHIFT = 0.1
 NORM_EPSILON = 1e-06
+COUNT_ROWS = 16
 MIB = 1 << 20
+LIMIT = 24
 
 
 def swap_near(value):
@@ -83,7 +85,7 @@
     return (1.5 * now.astype(jnp.float32) - 0.5 * product).astype(jnp.bfloat16)
 
 
-def polar_kernel(code_ref, tmpl_ref, own_ref, near_ref, far_ref, map_ref, cols_ref):
+def polar_kernel(subject, code_ref, tmpl_ref, own_ref, near_ref, far_ref, map_ref, cols_ref):
     lights, members = code_ref.shape
     width = members * BLOCK
     frames = own_ref.shape[0]
@@ -91,7 +93,7 @@
         for i in range(members):
             code = code_ref[g, i]
             lo = g * width + i * BLOCK
-            for place, ref in enumerate((own_ref, near_ref, far_ref)):
+            for place, ref in enumerate((own_ref, near_ref.at[subject], far_ref)):
 
                 @pl.when(code // 2 == place)
                 def _():
@@ -120,7 +122,9 @@
     out_refs = refs[2 * subj_count : -1]
     lights, members = code_ref.shape
     width = members * BLOCK
+    counts = []
     for p, place in enumerate(places):
+        total = jnp.int32(0)
         for g in range(lights):
             pick = jnp.int32(0)
             found = code_ref[g, 0] == place
@@ -128,6 +132,7 @@
                 hit = code_ref[g, j] == place
                 pick = jnp.where(hit, j, pick)
                 found = jnp.logical_or(found, hit)
+            total = total + found.astype(jnp.int32)
             rows = pl.ds(pl.multiple_of(pick * BLOCK, BLOCK), BLOCK)
             for s in range(subj_count):
                 lo = (s * lights + g) * width
@@ -135,8 +140,10 @@
                 weight_ref[p * BLOCK : (p + 1) * BLOCK, lo : lo + width] = jnp.where(
                     found, piece, jnp.zeros_like(piece)
                 )
+        counts.append(total)
     depth = lights * width
-    step_cols = len(places) * BLOCK // len(splits)
+    group = len(places) // len(splits)
+    step_cols = group * BLOCK
     chunk = 256
     at = 0
     for n, pieces in enumerate(splits):
@@ -158,6 +165,11 @@
                     total = term if total is None else total + term
                 out_refs[at][lo : lo + chunk, :] = total.astype(out_refs[at].dtype)
             at += 1
+        for b in range(group):
+            tally = jnp.full((COUNT_ROWS, BLOCK), counts[n * group + b], jnp.int32)
+            out_refs[at - 1][rows:, b * BLOCK : (b + 1) * BLOCK] = tally.astype(jnp.float32).astype(
+                out_refs[at - 1].dtype
+            )
 
 
 def body(series, template, sl_blocks):
@@ -173,95 +185,81 @@
     tmpl_far = swap_far(template)
     tmpl_near = swap_near(template)
     parts = [series[s] for s in range(subj_count)]
-    far, near = [], []
+    far = []
     for part in parts:
         far.append(swap_far(part))
-        near.append(swap_near(part))
-    lists_near = swap_near(sl_blocks)
-    lists_far = swap_far(sl_blocks)
+    near = swap_near(series)
 
     window = sl_blocks - (position - 1) * blk_dev
     side = window // blk_dev
     place = jnp.where(side == 1, 0, jnp.where((side == 2) == (odd == 1), 2, 1))
     code = (place * blk_dev + window % blk_dev).astype(jnp.int32)
-
-    mine = position * blk_dev + jnp.arange(blk_dev, dtype=jnp.int32)
-
-    def counted(lists):
-        return jnp.sum((lists.reshape(-1)[:, None] == mine[None, :]).astype(jnp.float32), axis=0)
-
-    coverage = counted(sl_blocks) + counted(lists_near) + jnp.where(far_real, counted(lists_far), 0.0)
-    per_vertex = jnp.repeat(coverage, BLOCK)
 
     tmpl_rows = call(
         template_kernel,
         jax.ShapeDtypeStruct((lights, width, frames), jnp.bfloat16),
         [smem(), vmem(), vmem(), vmem()],
         flops=10**9,
-        limit=16,
+        limit=LIMIT,
     )(code, template, tmpl_near, tmpl_far)
 
     maps, cols = [], []
     for s in range(subj_count):
-        if s == subj_count - 1:
-            code, per_vertex = lax.optimization_barrier((code, per_vertex))
         polar, gathered = call(
-            polar_kernel,
+            functools.partial(polar_kernel, s),
             (
                 jax.ShapeDtypeStruct((lights, width, width), jnp.bfloat16),
                 jax.ShapeDtypeStruct((frames, lights * width), jnp.bfloat16),
             ),
             [smem()] + [vmem()] * 4,
             flops=8 * 10**9,
-            limit=24,
-        )(code, tmpl_rows, parts[s], near[s], far[s])
+            limit=LIMIT,
+        )(code, tmpl_rows, parts[s], near, far[s])
         maps.append(polar)
         cols.append(gathered)
 
-    def mapped(code, places, splits, types):
+    def mapped(places, splits, types):
         shapes = [
-            jax.ShapeDtypeStruct((frames // pieces, width_dev), kind)
+            jax.ShapeDtypeStruct(
+                (frames // pieces + (COUNT_ROWS if piece == pieces - 1 else 0), width_dev), kind
+            )
             for pieces, kind in zip(splits, types)
-            for _ in range(pieces)
+            for piece in range(pieces)
         ]
         return call(
             functools.partial(map_kernel, subj_count, places, splits),
             shapes,
             [smem()] + [vmem()] * (2 * subj_count),
             flops=len(places) * 4 * 10**8,
-            limit=24,
+            limit=LIMIT,
             scratch=[pltpu.VMEM((len(places) * BLOCK, subj_count * lights * width), jnp.bfloat16)],
         )(code, *cols, *maps)
 
     blocks = list(range(blk_dev))
-    to_far = mapped(code, [2 * blk_dev + b for b in blocks], (2,), (jnp.bfloat16,))
-    from_far = []
-    for h in range(2):
-        from_far.append(swap_far(to_far[h]))
-    code, _ = lax.optimization_barrier((code, to_far[0]))
-    to_near, *own = mapped(code, [blk_dev + b for b in blocks] + blocks, (1, 2), (jnp.bfloat16, jnp.float32))
+    (to_far,) = mapped([2 * blk_dev + b for b in blocks], (1,), (jnp.bfloat16,))
+    from_far = swap_far(to_far)
+    code, _ = lax.optimization_barrier((code, to_far))
+    to_near, *own = mapped([blk_dev + b for b in blocks] + blocks, (1, 2), (jnp.bfloat16, jnp.float32))
     from_near = swap_near(to_near)
     keep = far_real.astype(jnp.float32)
 
+    def joined(mine, lo, hi):
+        return mine + from_near[lo:hi].astype(jnp.float32) + keep * from_far[lo:hi].astype(jnp.float32)
+
+    rows = frames // 2
+    per_vertex = joined(own[1][rows : rows + 1], frames, frames + 1)
+    halves = [joined(own[h][:rows], h * rows, (h + 1) * rows) for h in range(2)]
     subj_size = lax.axis_size("subj")
     distances = []
     while 2 ** len(distances) < subj_size:
         distances.append(2 ** len(distances))
-    rows = frames // 2
-    halves = []
-    for h in range(2):
-        mine_h = own[h]
-        if h > 0:
-            mine_h, halves[0] = lax.optimization_barrier((mine_h, halves[0]))
-        near_h = from_near[h * rows : (h + 1) * rows].astype(jnp.float32)
-        halves.append((mine_h + near_h + keep * from_far[h].astype(jnp.float32)).astype(jnp.bfloat16))
     for step in range(len(distances)):
         for h in range(2):
             sent = halves[h].astype(jnp.bfloat16)
             got = swap_subj(sent, distances[(step + h) % len(distances)])
             halves[h] = sent.astype(jnp.float32) + got.astype(jnp.float32)
     total = jnp.concatenate(halves, axis=0)
-    return total / per_vertex[None, :] / (subj_count * subj_size)
+    return total / per_vertex / (subj_count * subj_size)
 
 
 def solution(mesh):

time: 73.8 us -> 68.8 us (0.932)
  the two profiles are of different devices: /device:TPU:8 before, /device:TPU:18 now
where the time goes in v1:
time: 68.8 us; the launch traced here: 68.3 us
  waiting for transfers between devices  26.9 us (39%)
  Pallas kernels  23.4 us (34%)
  starting transfers between devices  15 us (22%)
  other arithmetic  1.59 us (2%)
  local copies, waits for them, and re-layouts  1.28 us (2%)
    pallas_call x2, Pallas kernels, body(): call(functools.partial(polar_kernel, s), (jax.ShapeDtypeStruct((lights, w...  17.4 us
    ppermute x4, waiting for transfers between devices, swap_far(): return lax.ppermute(value, 'cortex', route)  13.8 us
    ppermute x4, waiting for transfers between devices, swap_subj(): lax.ppermute(value, 'subj', [(i, i ^ distance) for i in range(count)])  13.1 us
    ppermute x4, starting transfers between devices, swap_far(): return lax.ppermute(value, 'cortex', route)  9.81 us
    ppermute x4, starting transfers between devices, swap_subj(): lax.ppermute(value, 'subj', [(i, i ^ distance) for i in range(count)])  4.34 us
    pallas_call x2, Pallas kernels, mapped(): call(functools.partial(map_kernel, subj_count, places, splits), shapes, [...  3.95 us
    pallas_call x1, Pallas kernels, body(): call(template_kernel, jax.ShapeDtypeStruct((lights, width, frames), jnp.b...  2.05 us
  transfers between devices with their start and end apart: 11, of which 6 were waited for; matrix products, arithmetic and copies ran while one was open for 2% of the time, Pallas kernels for 16%

profile of v1, /device:TPU:18, one launch (start us, length us, event | category | flops | bytes accessed | tf_op | source)
XLA Modules:
  0.0 68.3 jit_solution(3853002834221460557)
XLA Ops:
  0.0 0.0 copy-start
  0.0 0.0 copy-start.1
  0.0 0.0 collective-permute-start.2
  0.0 0.5 collective-permute-start
  0.5 2.0 %collective-permute-start.1 = (bf16[1024,256]{1,0:T(8,128)(2,1)}, bf16[1024,256]{1,0:T(8,128)(2,1)}, u32[]{:S(2)}, u32[]{:S(2)}) collective-permute-start(bf16[1024,256]{1,0:T(8,128)(2,1)} %own_ref.1), channel_id=1, source_target_pairs={{0,0},{7,7},{1,2},{2,1},{3,4},{4,3},{5,6},{6,5},{8,8},{15,15},{9,1... | collective-permute-start | bytes 1572872 | tf_op jit(solution)/shard_map/ppermute | solution.py:30
  2.5 1.3 %slice_bitcast_fusion = (bf16[1024,256]{1,0:T(8,128)(2,1)S(1)}, bf16[1024,256]{1,0:T(8,128)(2,1)S(1)}) fusion(bf16[2,1024,256]{2,1,0:T(8,128)(2,1)} %param.3), kind=kLoop, calls=%fused_computation.8 | loop fusion | bytes 2097152 | tf_op jit(solution)/shard_map/squeeze | solution.py:187
  3.8 3.5 %collective-permute-start.4 = (bf16[1024,256]{1,0:T(8,128)(2,1)S(1)}, bf16[1024,256]{1,0:T(8,128)(2,1)}, u32[]{:S(2)}, u32[]{:S(2)}) collective-permute-start(bf16[1024,256]{1,0:T(8,128)(2,1)S(1)} %get-tuple-element.23.own_ref), channel_id=1, source_target_pairs={{0,0},{7,7},{1,2},{2,1},{3,4},{4,3},{5,6},{6,5},{8,8},{15,15},{9,1... | collective-permute-start | bytes 1572872 | tf_op jit(solution)/shard_map/ppermute | solution.py:30
  7.4 2.0 %collective-permute-start.3 = (bf16[1024,256]{1,0:T(8,128)(2,1)S(1)}, bf16[1024,256]{1,0:T(8,128)(2,1)S(1)}, u32[]{:S(2)}, u32[]{:S(2)}) collective-permute-start(bf16[1024,256]{1,0:T(8,128)(2,1)S(1)} %get-tuple-element.24.own_ref), channel_id=1, source_target_pairs={{0,0},{7,7},{1,2},{2,1},{3,4},{4,3},{5,6},{6,5},{8,8},{15,15},{9,1... | collective-permute-start | bytes 1572872 | tf_op jit(solution)/shard_map/ppermute | solution.py:30
  9.4 0.0 copy-done.1
  9.4 0.0 collective-permute-done.near_ref
  9.5 1.9 %collective-permute-done.1.far_ref = bf16[1024,256]{1,0:T(8,128)(2,1)} collective-permute-done((bf16[1024,256]{1,0:T(8,128)(2,1)}, bf16[1024,256]{1,0:T(8,128)(2,1)}, u32[]{:S(2)}, u32[]{:S(2)}) %collective-permute-start.1) | collective-permute-done | bytes 524320 | tf_op jit(solution)/shard_map/ppermute | solution.py:30
  11.3 0.0 copy-done
  11.3 2.0 %shard_map.37.tmpl_ref = bf16[2,384,1024]{2,1,0:T(8,128)(2,1)S(1)} custom-call(s32[2,3]{1,0:T(2,128)S(1)} %fusion.2.code_ref, bf16[1024,256]{1,0:T(8,128)(2,1)S(1)} %copy-done, bf16[1024,256]{1,0:T(8,128)(2,1)} %collective-permute-done.near_ref, bf16[1024,256]{1,0:T(8,128)(2,1)} %collective-permute-done.1.far_ref), custom_call_target="tpu_custom_call" | custom-call | flops 1000000000 | bytes 1572864 | tf_op jit(solution)/shard_map/pallas_call | solution.py:198
  13.4 3.6 %collective-permute-done.4.far_ref = bf16[1024,256]{1,0:T(8,128)(2,1)} collective-permute-done((bf16[1024,256]{1,0:T(8,128)(2,1)S(1)}, bf16[1024,256]{1,0:T(8,128)(2,1)}, u32[]{:S(2)}, u32[]{:S(2)}) %collective-permute-start.4) | collective-permute-done | bytes 524320 | tf_op jit(solution)/shard_map/ppermute | solution.py:30
  16.9 0.0 collective-permute-done.2.near_ref
  16.9 8.9 %shard_map.39 = (bf16[2,384,384]{2,1,0:T(8,128)(2,1)S(1)}, bf16[1024,768]{1,0:T(8,128)(2,1)S(1)}) custom-call(s32[2,3]{1,0:T(2,128)S(1)} %fusion.2.code_ref, bf16[2,384,1024]{2,1,0:T(8,128)(2,1)S(1)} %shard_map.37.tmpl_ref, bf16[1024,256]{1,0:T(8,128)(2,1)S(1)} %get-tuple-element.23.own_ref, bf16[2,1024,256]{2,1,0:T(8,128)(2,1)S(1)} %collective-permute-done.2.near_ref, ...), custom_call_target="tpu_custom_call" | custom-call | flops 8000000000 | bytes 2162688 | tf_op jit(solution)/shard_map/pallas_call | solution.py:208
  25.8 0.0 collective-permute-done.3.far_ref
  25.8 8.6 %shard_map.38 = (bf16[2,384,384]{2,1,0:T(8,128)(2,1)S(1)}, bf16[1024,768]{1,0:T(8,128)(2,1)S(1)}) custom-call(s32[2,3]{1,0:T(2,128)S(1)} %fusion.2.code_ref, bf16[2,384,1024]{2,1,0:T(8,128)(2,1)S(1)} %shard_map.37.tmpl_ref, bf16[1024,256]{1,0:T(8,128)(2,1)S(1)} %get-tuple-element.24.own_ref, bf16[2,1024,256]{2,1,0:T(8,128)(2,1)S(1)} %collective-permute-done.2.near_ref, ...), custom_call_target="tpu_custom_call" | custom-call | flops 8000000000 | bytes 2162688 | tf_op jit(solution)/shard_map/pallas_call | solution.py:208
  34.4 1.6 %shard_map.40 = bf16[1040,256]{1,0:T(8,128)(2,1)S(1)} custom-call(s32[2,3]{1,0:T(2,128)S(1)} %fusion.2.code_ref, bf16[1024,768]{1,0:T(8,128)(2,1)S(1)} %get-tuple-element.13.refs_0_, bf16[1024,768]{1,0:T(8,128)(2,1)S(1)} %get-tuple-element.14.refs_1_, bf16[2,384,384]{2,1,0:T(8,128)(2,1)S(1)} %get-tuple-element.15.refs_2_, ...), custom_call_target="tpu_custom_call" | custom-call | flops 800000000 | bytes 532480 | tf_op jit(solution)/shard_map/pallas_call | solution.py:229
  36.0 2.4 %shard_map.41 = (bf16[1040,256]{1,0:T(8,128)(2,1)S(1)}, f32[512,256]{1,0:T(8,128)S(1)}, f32[528,256]{1,0:T(8,128)S(1)}) custom-call(s32[2,3]{1,0:T(2,128)S(1)} %fusion.2.code_ref, bf16[1024,768]{1,0:T(8,128)(2,1)S(1)} %get-tuple-element.13.refs_0_, bf16[1024,768]{1,0:T(8,128)(2,1)S(1)} %get-tuple-element.14.refs_1_, ...), custom_call_target="tpu_custom_call" | custom-call | flops 1600000000 | bytes 1597440 | tf_op jit(solution)/shard_map/pallas_call | solution.py:229
  38.3 0.3 collective-permute-start.5
  38.7 2.2 %collective-permute-start.6 = (bf16[1040,256]{1,0:T(8,128)(2,1)S(1)}, bf16[1040,256]{1,0:T(8,128)(2,1)S(1)}, u32[]{:S(2)}, u32[]{:S(2)}) collective-permute-start(bf16[1040,256]{1,0:T(8,128)(2,1)S(1)} %shard_map.40), channel_id=1, source_target_pairs={{0,0},{7,7},{1,2},{2,1},{3,4},{4,3},{5,6},{6,5},{8,8},{15,15},{9,1... | collective-permute-start | bytes 1597448 | tf_op jit(solution)/shard_map/ppermute | solution.py:30
  40.9 0.0 collective-permute-done.5
  40.9 8.3 %collective-permute-done.6 = bf16[1040,256]{1,0:T(8,128)(2,1)S(1)} collective-permute-done((bf16[1040,256]{1,0:T(8,128)(2,1)S(1)}, bf16[1040,256]{1,0:T(8,128)(2,1)S(1)}, u32[]{:S(2)}, u32[]{:S(2)}) %collective-permute-start.6) | collective-permute-done | bytes 532512 | tf_op jit(solution)/shard_map/ppermute | solution.py:30
  49.2 0.2 add_convert_fusion.3
  49.5 0.6 collective-permute-start.7
  50.1 1.5 %collective-permute-start.9 = (bf16[512,256]{1,0:T(8,128)(2,1)S(1)}, bf16[512,256]{1,0:T(8,128)(2,1)S(1)}, u32[]{:S(2)}, u32[]{:S(2)}) collective-permute-start(bf16[512,256]{1,0:T(8,128)(2,1)S(1)} %get-tuple-element.22), channel_id=1, source_target_pairs={{0,16},{8,24},{16,0},{24,8},{1,17},{9,25},{17,1},{25,9},{2,18},{10... | collective-permute-start | bytes 786440 | tf_op jit(solution)/shard_map/ppermute | solution.py:35
  51.6 6.4 %collective-permute-done.7 = bf16[512,256]{1,0:T(8,128)(2,1)S(1)} collective-permute-done((bf16[512,256]{1,0:T(8,128)(2,1)S(1)}, bf16[512,256]{1,0:T(8,128)(2,1)S(1)}, u32[]{:S(2)}, u32[]{:S(2)}) %collective-permute-start.7) | collective-permute-done | bytes 262176 | tf_op jit(solution)/shard_map/ppermute | solution.py:35
  58.0 0.1 add_convert_fusion.2
  58.1 1.6 %collective-permute-start.8 = (bf16[512,256]{1,0:T(8,128)(2,1)S(1)}, bf16[512,256]{1,0:T(8,128)(2,1)S(1)}, u32[]{:S(2)}, u32[]{:S(2)}) collective-permute-start(bf16[512,256]{1,0:T(8,128)(2,1)S(1)} %add_convert_fusion.2), channel_id=1, source_target_pairs={{0,16},{8,24},{16,0},{24,8},{1,17},{9,25},{17,1},{25,9},{2,18},{10... | collective-permute-start | bytes 786440 | tf_op jit(solution)/shard_map/ppermute | solution.py:35
  59.7 0.0 collective-permute-done.9
  59.7 0.1 add_convert_fusion
  59.8 0.6 collective-permute-start.10
  60.4 5.4 %collective-permute-done.8 = bf16[512,256]{1,0:T(8,128)(2,1)S(1)} collective-permute-done((bf16[512,256]{1,0:T(8,128)(2,1)S(1)}, bf16[512,256]{1,0:T(8,128)(2,1)S(1)}, u32[]{:S(2)}, u32[]{:S(2)}) %collective-permute-start.8) | collective-permute-done | bytes 262176 | tf_op jit(solution)/shard_map/ppermute | solution.py:35
  65.8 0.1 convert_add_fusion.1
  65.8 1.3 %collective-permute-done.10 = bf16[512,256]{1,0:T(8,128)(2,1)S(1)} collective-permute-done((bf16[512,256]{1,0:T(8,128)(2,1)S(1)}, bf16[512,256]{1,0:T(8,128)(2,1)S(1)}, u32[]{:S(2)}, u32[]{:S(2)}) %collective-permute-start.10) | collective-permute-done | bytes 262176 | tf_op jit(solution)/shard_map/ppermute | solution.py:35
  67.2 0.1 convert_add_fusion
  67.2 1.1 %fusion = f32[1024,256]{1,0:T(8,128)} fusion(f32[512,256]{1,0:T(8,128)S(1)} %convert_add_fusion, f32[512,256]{1,0:T(8,128)S(1)} %convert_add_fusion.1, f32[256]{0:T(256)S(1)} %bitcast.5), kind=kLoop, calls=%fused_computation.1 | loop fusion | flops 786432 | bytes 2098176 | tf_op jit(solution)/shard_map/div | solution.py:262
  (2 shorter events, 0.0 us)
Async XLA Ops:
  0.0 11.3 %copy-start = (bf16[1024,256]{1,0:T(8,128)(2,1)S(1)}, bf16[1024,256]{1,0:T(8,128)(2,1)}, u32[]{:S(2)}) copy-start(bf16[1024,256]{1,0:T(8,128)(2,1)} %own_ref.1) | copy-start | bytes 1572868
  0.0 9.4 %copy-start.1 = (s32[2,3]{1,0:T(2,128)S(1)}, s32[2,3]{1,0:T(2,128)}, u32[]{:S(2)}) copy-start(s32[2,3]{1,0:T(2,128)} %param.5) | copy-start | bytes 76
  0.0 16.9 %collective-permute-start.2 = (bf16[2,1024,256]{2,1,0:T(8,128)(2,1)}, bf16[2,1024,256]{2,1,0:T(8,128)(2,1)S(1)}, u32[]{:S(2)}, u32[]{:S(2)}) collective-permute-start(bf16[2,1024,256]{2,1,0:T(8,128)(2,1)} %param.3), channel_id=1, source_target_pairs={{0,1},{1,0},{2,3},{3,2},{4,5},{5,4},{6,7},{7,6},{8,9},{9,8},{10,11... | collective-permute-start | bytes 3145736 | tf_op jit(solution)/shard_map/ppermute | solution.py:22
  0.0 9.4 %collective-permute-start = (bf16[1024,256]{1,0:T(8,128)(2,1)}, bf16[1024,256]{1,0:T(8,128)(2,1)}, u32[]{:S(2)}, u32[]{:S(2)}) collective-permute-start(bf16[1024,256]{1,0:T(8,128)(2,1)} %own_ref.1), channel_id=1, source_target_pairs={{0,1},{1,0},{2,3},{3,2},{4,5},{5,4},{6,7},{7,6},{8,9},{9,8},{10,11... | collective-permute-start | bytes 1572872 | tf_op jit(solution)/shard_map/ppermute | solution.py:22
  0.5 10.8 %collective-permute-start.1 = (bf16[1024,256]{1,0:T(8,128)(2,1)}, bf16[1024,256]{1,0:T(8,128)(2,1)}, u32[]{:S(2)}, u32[]{:S(2)}) collective-permute-start(bf16[1024,256]{1,0:T(8,128)(2,1)} %own_ref.1), channel_id=1, source_target_pairs={{0,0},{7,7},{1,2},{2,1},{3,4},{4,3},{5,6},{6,5},{8,8},{15,15},{9,1... | collective-permute-start | bytes 1572872 | tf_op jit(solution)/shard_map/ppermute | solution.py:30
  3.8 13.1 %collective-permute-start.4 = (bf16[1024,256]{1,0:T(8,128)(2,1)S(1)}, bf16[1024,256]{1,0:T(8,128)(2,1)}, u32[]{:S(2)}, u32[]{:S(2)}) collective-permute-start(bf16[1024,256]{1,0:T(8,128)(2,1)S(1)} %get-tuple-element.23.own_ref), channel_id=1, source_target_pairs={{0,0},{7,7},{1,2},{2,1},{3,4},{4,3},{5,6},{6,5},{8,8},{15,15},{9,1... | collective-permute-start | bytes 1572872 | tf_op jit(solution)/shard_map/ppermute | solution.py:30
  7.4 18.5 %collective-permute-start.3 = (bf16[1024,256]{1,0:T(8,128)(2,1)S(1)}, bf16[1024,256]{1,0:T(8,128)(2,1)S(1)}, u32[]{:S(2)}, u32[]{:S(2)}) collective-permute-start(bf16[1024,256]{1,0:T(8,128)(2,1)S(1)} %get-tuple-element.24.own_ref), channel_id=1, source_target_pairs={{0,0},{7,7},{1,2},{2,1},{3,4},{4,3},{5,6},{6,5},{8,8},{15,15},{9,1... | collective-permute-start | bytes 1572872 | tf_op jit(solution)/shard_map/ppermute | solution.py:30
  38.3 2.6 %collective-permute-start.5 = (bf16[1040,256]{1,0:T(8,128)(2,1)S(1)}, bf16[1040,256]{1,0:T(8,128)(2,1)S(1)}, u32[]{:S(2)}, u32[]{:S(2)}) collective-permute-start(bf16[1040,256]{1,0:T(8,128)(2,1)S(1)} %get-tuple-element.19), channel_id=1, source_target_pairs={{0,1},{1,0},{2,3},{3,2},{4,5},{5,4},{6,7},{7,6},{8,9},{9,8},{10,11... | collective-permute-start | bytes 1597448 | tf_op jit(solution)/shard_map/ppermute | solution.py:22
  38.7 10.6 %collective-permute-start.6 = (bf16[1040,256]{1,0:T(8,128)(2,1)S(1)}, bf16[1040,256]{1,0:T(8,128)(2,1)S(1)}, u32[]{:S(2)}, u32[]{:S(2)}) collective-permute-start(bf16[1040,256]{1,0:T(8,128)(2,1)S(1)} %shard_map.40), channel_id=1, source_target_pairs={{0,0},{7,7},{1,2},{2,1},{3,4},{4,3},{5,6},{6,5},{8,8},{15,15},{9,1... | collective-permute-start | bytes 1597448 | tf_op jit(solution)/shard_map/ppermute | solution.py:30
  49.5 8.5 %collective-permute-start.7 = (bf16[512,256]{1,0:T(8,128)(2,1)S(1)}, bf16[512,256]{1,0:T(8,128)(2,1)S(1)}, u32[]{:S(2)}, u32[]{:S(2)}) collective-permute-start(bf16[512,256]{1,0:T(8,128)(2,1)S(1)} %get-tuple-element.21), channel_id=1, source_target_pairs={{0,8},{8,0},{16,24},{24,16},{1,9},{9,1},{17,25},{25,17},{2,10},{10... | collective-permute-start | bytes 786440 | tf_op jit(solution)/shard_map/ppermute | solution.py:35
  50.1 9.6 %collective-permute-start.9 = (bf16[512,256]{1,0:T(8,128)(2,1)S(1)}, bf16[512,256]{1,0:T(8,128)(2,1)S(1)}, u32[]{:S(2)}, u32[]{:S(2)}) collective-permute-start(bf16[512,256]{1,0:T(8,128)(2,1)S(1)} %get-tuple-element.22), channel_id=1, source_target_pairs={{0,16},{8,24},{16,0},{24,8},{1,17},{9,25},{17,1},{25,9},{2,18},{10... | collective-permute-start | bytes 786440 | tf_op jit(solution)/shard_map/ppermute | solution.py:35
  58.1 7.7 %collective-permute-start.8 = (bf16[512,256]{1,0:T(8,128)(2,1)S(1)}, bf16[512,256]{1,0:T(8,128)(2,1)S(1)}, u32[]{:S(2)}, u32[]{:S(2)}) collective-permute-start(bf16[512,256]{1,0:T(8,128)(2,1)S(1)} %add_convert_fusion.2), channel_id=1, source_target_pairs={{0,16},{8,24},{16,0},{24,8},{1,17},{9,25},{17,1},{25,9},{2,18},{10... | collective-permute-start | bytes 786440 | tf_op jit(solution)/shard_map/ppermute | solution.py:35
  59.8 7.4 %collective-permute-start.10 = (bf16[512,256]{1,0:T(8,128)(2,1)S(1)}, bf16[512,256]{1,0:T(8,128)(2,1)S(1)}, u32[]{:S(2)}, u32[]{:S(2)}) collective-permute-start(bf16[512,256]{1,0:T(8,128)(2,1)S(1)} %add_convert_fusion), channel_id=1, source_target_pairs={{0,8},{8,0},{16,24},{24,16},{1,9},{9,1},{17,25},{25,17},{2,10},{10... | collective-permute-start | bytes 786440 | tf_op jit(solution)/shard_map/ppermute | solution.py:35

commit v2 on v1

--- a/solution.py
+++ b/solution.py
@@ -15,6 +15,7 @@
 COUNT_ROWS = 16
 MIB = 1 << 20
 LIMIT = 24
+PIECES = 4
 
 
 def swap_near(value):
@@ -37,10 +38,6 @@
 
 def vmem():
     return pl.BlockSpec(memory_space=pltpu.VMEM)
-
-
-def smem():
-    return pl.BlockSpec(memory_space=pltpu.SMEM)
 
 
 def call(kernel, out_shape, in_specs, flops, limit, scratch=()):
@@ -74,18 +71,25 @@
                     out_ref[g, j * BLOCK : (j + 1) * BLOCK, :] = columns(ref, code % 2).T
 
 
-def newton_schulz(now):
-    head = now.shape[0] - BLOCK
-    top, low = now[:head], now[head:]
+def newton_schulz(now_ref, next_ref, gram_ref):
+    lights, width, _ = now_ref.shape
+    head = width - BLOCK
     over = (((1,), (1,)), ((), ()))
-    corner = lax.dot_general(top, top, over, preferred_element_type=jnp.float32).astype(jnp.bfloat16)
-    bottom = lax.dot_general(low, now, over, preferred_element_type=jnp.float32).astype(jnp.bfloat16)
-    gram = jnp.concatenate([jnp.concatenate([corner, bottom[:, :head].T], axis=1), bottom], axis=0)
-    product = jnp.dot(gram, now, preferred_element_type=jnp.float32)
-    return (1.5 * now.astype(jnp.float32) - 0.5 * product).astype(jnp.bfloat16)
-
-
-def polar_kernel(subject, code_ref, tmpl_ref, own_ref, near_ref, far_ref, map_ref, cols_ref):
+    for g in range(lights):
+        top = now_ref[g, :head]
+        corner = lax.dot_general(top, top, over, preferred_element_type=jnp.float32)
+        gram_ref[g, :head, :head] = corner.astype(jnp.bfloat16)
+        low = lax.dot_general(now_ref[g, head:], now_ref[g], over, preferred_element_type=jnp.float32)
+        low = low.astype(jnp.bfloat16)
+        gram_ref[g, head:, :] = low
+        gram_ref[g, :head, head:] = low[:, :head].T
+    for g in range(lights):
+        now = now_ref[g]
+        product = jnp.dot(gram_ref[g], now, preferred_element_type=jnp.float32)
+        next_ref[g] = (1.5 * now.astype(jnp.float32) - 0.5 * product).astype(jnp.bfloat16)
+
+
+def polar_kernel(subject, code_ref, tmpl_ref, own_ref, near_ref, far_ref, map_ref, cols_ref, odd_ref, gram_ref):
     lights, members = code_ref.shape
     width = members * BLOCK
     frames = own_ref.shape[0]
@@ -99,6 +103,7 @@
                 def _():
                     cols_ref[:, lo : lo + BLOCK] = columns(ref, code % 2)
 
+    first_ref = map_ref if NS_STEPS % 2 == 0 else odd_ref
     row = lax.broadcasted_iota(jnp.int32, (width, width), 0)
     col = lax.broadcasted_iota(jnp.int32, (width, width), 1)
     ridge = jnp.where(row == col, RIDGE_SHIFT, 0.0)
@@ -108,11 +113,11 @@
         )
         cross = cross * (1.0 / frames) + ridge
         squares = jnp.sum(cross * cross, keepdims=True)
-        map_ref[g] = (cross * (1.0 / jnp.sqrt(squares + NORM_EPSILON))).astype(jnp.bfloat16)
-
-    for _ in range(NS_STEPS):
-        for g in range(lights):
-            map_ref[g] = newton_schulz(map_ref[g])
+        first_ref[g] = (cross * (1.0 / jnp.sqrt(squares + NORM_EPSILON))).astype(jnp.bfloat16)
+
+    turns = (first_ref, odd_ref if first_ref is map_ref else map_ref)
+    for step in range(NS_STEPS):
+        newton_schulz(turns[step % 2], turns[1 - step % 2], gram_ref)
 
 
 def map_kernel(subj_count, places, splits, code_ref, *refs):
@@ -198,7 +203,7 @@
     tmpl_rows = call(
         template_kernel,
         jax.ShapeDtypeStruct((lights, width, frames), jnp.bfloat16),
-        [smem(), vmem(), vmem(), vmem()],
+        [vmem()] * 4,
         flops=10**9,
         limit=LIMIT,
     )(code, template, tmpl_near, tmpl_far)
@@ -211,9 +216,10 @@
                 jax.ShapeDtypeStruct((lights, width, width), jnp.bfloat16),
                 jax.ShapeDtypeStruct((frames, lights * width), jnp.bfloat16),
             ),
-            [smem()] + [vmem()] * 4,
+            [vmem()] * 5,
             flops=8 * 10**9,
             limit=LIMIT,
+            scratch=[pltpu.VMEM((lights, width, width), jnp.bfloat16)] * 2,
         )(code, tmpl_rows, parts[s], near, far[s])
         maps.append(polar)
         cols.append(gathered)
@@ -229,7 +235,7 @@
         return call(
             functools.partial(map_kernel, subj_count, places, splits),
             shapes,
-            [smem()] + [vmem()] * (2 * subj_count),
+            [vmem()] * (1 + 2 * subj_count),
             flops=len(places) * 4 * 10**8,
             limit=LIMIT,
             scratch=[pltpu.VMEM((len(places) * BLOCK, subj_count * lights * width), jnp.bfloat16)],
@@ -239,22 +245,22 @@
     (to_far,) = mapped([2 * blk_dev + b for b in blocks], (1,), (jnp.bfloat16,))
     from_far = swap_far(to_far)
     code, _ = lax.optimization_barrier((code, to_far))
-    to_near, *own = mapped([blk_dev + b for b in blocks] + blocks, (1, 2), (jnp.bfloat16, jnp.float32))
+    to_near, *own = mapped([blk_dev + b for b in blocks] + blocks, (1, PIECES), (jnp.bfloat16, jnp.float32))
     from_near = swap_near(to_near)
     keep = far_real.astype(jnp.float32)
 
     def joined(mine, lo, hi):
         return mine + from_near[lo:hi].astype(jnp.float32) + keep * from_far[lo:hi].astype(jnp.float32)
 
-    rows = frames // 2
-    per_vertex = joined(own[1][rows : rows + 1], frames, frames + 1)
-    halves = [joined(own[h][:rows], h * rows, (h + 1) * rows) for h in range(2)]
+    rows = frames // PIECES
+    per_vertex = joined(own[-1][rows : rows + 1], frames, frames + 1)
+    halves = [joined(own[h][:rows], h * rows, (h + 1) * rows) for h in range(PIECES)]
     subj_size = lax.axis_size("subj")
     distances = []
     while 2 ** len(distances) < subj_size:
         distances.append(2 ** len(distances))
     for step in range(len(distances)):
-        for h in range(2):
+        for h in range(PIECES):
             sent = halves[h].astype(jnp.bfloat16)
             got = swap_subj(sent, distances[(step + h) % len(distances)])
             halves[h] = sent.astype(jnp.float32) + got.astype(jnp.float32)

time: 68.8 us -> 65.3 us (0.949)
  the two profiles are of different devices: /device:TPU:18 before, /device:TPU:8 now
where the time goes in v2:
time: 65.3 us; the launch traced here: 64.8 us
  Pallas kernels  22.1 us (34%)
  waiting for transfers between devices  19.9 us (30%)
  starting transfers between devices  19.7 us (30%)
  other arithmetic  1.58 us (2%)
  local copies, waits for them, and re-layouts  1.28 us (2%)
    pallas_call x2, Pallas kernels, body(): call(functools.partial(polar_kernel, s), (jax.ShapeDtypeStruct((lights, w...  16.5 us
    ppermute x4, waiting for transfers between devices, swap_far(): return lax.ppermute(value, 'cortex', route)  13.7 us
    ppermute x8, starting transfers between devices, swap_subj(): lax.ppermute(value, 'subj', [(i, i ^ distance) for i in range(count)])  9.54 us
    ppermute x4, starting transfers between devices, swap_far(): return lax.ppermute(value, 'cortex', route)  9.38 us
    ppermute x8, waiting for transfers between devices, swap_subj(): lax.ppermute(value, 'subj', [(i, i ^ distance) for i in range(count)])  6.15 us
    pallas_call x2, Pallas kernels, mapped(): call(functools.partial(map_kernel, subj_count, places, splits), shapes, [...  3.11 us
    pallas_call x1, Pallas kernels, body(): call(template_kernel, jax.ShapeDtypeStruct((lights, width, frames), jnp.b...  2.49 us
  transfers between devices with their start and end apart: 15, of which 9 were waited for; matrix products, arithmetic and copies ran while one was open for 2% of the time, Pallas kernels for 17%

profile of v2, /device:TPU:8, one launch (start us, length us, event | category | flops | bytes accessed | tf_op | source)
XLA Modules:
  0.0 64.8 jit_solution(17403712380967927529)
XLA Ops:
  0.0 0.0 copy-start
  0.0 0.0 copy-start.1
  0.0 0.0 collective-permute-start.2
  0.0 0.5 collective-permute-start
  0.5 1.9 %collective-permute-start.1 = (bf16[1024,256]{1,0:T(8,128)(2,1)}, bf16[1024,256]{1,0:T(8,128)(2,1)}, u32[]{:S(2)}, u32[]{:S(2)}) collective-permute-start(bf16[1024,256]{1,0:T(8,128)(2,1)} %own_ref.1), channel_id=1, source_target_pairs={{0,0},{7,7},{1,2},{2,1},{3,4},{4,3},{5,6},{6,5},{8,8},{15,15},{9,1... | collective-permute-start | bytes 1572872 | tf_op jit(solution)/shard_map/ppermute | solution.py:31
  2.4 1.3 %slice_bitcast_fusion = (bf16[1024,256]{1,0:T(8,128)(2,1)S(1)}, bf16[1024,256]{1,0:T(8,128)(2,1)S(1)}) fusion(bf16[2,1024,256]{2,1,0:T(8,128)(2,1)} %param.3), kind=kLoop, calls=%fused_computation.2 | loop fusion | bytes 2097152 | tf_op jit(solution)/shard_map/squeeze | solution.py:192
  3.7 3.6 %collective-permute-start.4 = (bf16[1024,256]{1,0:T(8,128)(2,1)S(1)}, bf16[1024,256]{1,0:T(8,128)(2,1)}, u32[]{:S(2)}, u32[]{:S(2)}) collective-permute-start(bf16[1024,256]{1,0:T(8,128)(2,1)S(1)} %get-tuple-element.29.own_ref), channel_id=1, source_target_pairs={{0,0},{7,7},{1,2},{2,1},{3,4},{4,3},{5,6},{6,5},{8,8},{15,15},{9,1... | collective-permute-start | bytes 1572872 | tf_op jit(solution)/shard_map/ppermute | solution.py:31
  7.4 1.9 %collective-permute-start.3 = (bf16[1024,256]{1,0:T(8,128)(2,1)S(1)}, bf16[1024,256]{1,0:T(8,128)(2,1)S(1)}, u32[]{:S(2)}, u32[]{:S(2)}) collective-permute-start(bf16[1024,256]{1,0:T(8,128)(2,1)S(1)} %get-tuple-element.30.own_ref), channel_id=1, source_target_pairs={{0,0},{7,7},{1,2},{2,1},{3,4},{4,3},{5,6},{6,5},{8,8},{15,15},{9,1... | collective-permute-start | bytes 1572872 | tf_op jit(solution)/shard_map/ppermute | solution.py:31
  9.3 0.0 copy-done.1
  9.3 0.0 collective-permute-done.near_ref
  9.3 2.0 %collective-permute-done.1.far_ref = bf16[1024,256]{1,0:T(8,128)(2,1)} collective-permute-done((bf16[1024,256]{1,0:T(8,128)(2,1)}, bf16[1024,256]{1,0:T(8,128)(2,1)}, u32[]{:S(2)}, u32[]{:S(2)}) %collective-permute-start.1) | collective-permute-done | bytes 524320 | tf_op jit(solution)/shard_map/ppermute | solution.py:31
  11.3 0.0 copy-done
  11.3 2.5 %shard_map.37.tmpl_ref = bf16[2,384,1024]{2,1,0:T(8,128)(2,1)S(1)} custom-call(s32[2,3]{1,0:T(2,128)S(1)} %fusion.2.code_ref, bf16[1024,256]{1,0:T(8,128)(2,1)S(1)} %copy-done, bf16[1024,256]{1,0:T(8,128)(2,1)} %collective-permute-done.near_ref, bf16[1024,256]{1,0:T(8,128)(2,1)} %collective-permute-done.1.far_ref), custom_call_target="tpu_custom_call" | custom-call | flops 1000000000 | bytes 1572864 | tf_op jit(solution)/shard_map/pallas_call | solution.py:203
  13.8 3.1 %collective-permute-done.4.far_ref = bf16[1024,256]{1,0:T(8,128)(2,1)} collective-permute-done((bf16[1024,256]{1,0:T(8,128)(2,1)S(1)}, bf16[1024,256]{1,0:T(8,128)(2,1)}, u32[]{:S(2)}, u32[]{:S(2)}) %collective-permute-start.4) | collective-permute-done | bytes 524320 | tf_op jit(solution)/shard_map/ppermute | solution.py:31
  16.9 0.0 collective-permute-done.2.near_ref
  16.9 8.7 %shard_map.39 = (bf16[2,384,384]{2,1,0:T(8,128)(2,1)S(1)}, bf16[1024,768]{1,0:T(8,128)(2,1)S(1)}) custom-call(s32[2,3]{1,0:T(2,128)S(1)} %fusion.2.code_ref, bf16[2,384,1024]{2,1,0:T(8,128)(2,1)S(1)} %shard_map.37.tmpl_ref, bf16[1024,256]{1,0:T(8,128)(2,1)S(1)} %get-tuple-element.29.own_ref, bf16[2,1024,256]{2,1,0:T(8,128)(2,1)S(1)} %collective-permute-done.2.near_ref, ...), custom_call_target="tpu_custom_call" | custom-call | flops 8000000000 | bytes 2162688 | tf_op jit(solution)/shard_map/pallas_call | solution.py:213
  25.6 0.0 collective-permute-done.3.far_ref
  25.6 7.8 %shard_map.38 = (bf16[2,384,384]{2,1,0:T(8,128)(2,1)S(1)}, bf16[1024,768]{1,0:T(8,128)(2,1)S(1)}) custom-call(s32[2,3]{1,0:T(2,128)S(1)} %fusion.2.code_ref, bf16[2,384,1024]{2,1,0:T(8,128)(2,1)S(1)} %shard_map.37.tmpl_ref, bf16[1024,256]{1,0:T(8,128)(2,1)S(1)} %get-tuple-element.30.own_ref, bf16[2,1024,256]{2,1,0:T(8,128)(2,1)S(1)} %collective-permute-done.2.near_ref, ...), custom_call_target="tpu_custom_call" | custom-call | flops 8000000000 | bytes 2162688 | tf_op jit(solution)/shard_map/pallas_call | solution.py:213
  33.5 1.1 %shard_map.40 = bf16[1040,256]{1,0:T(8,128)(2,1)S(1)} custom-call(s32[2,3]{1,0:T(2,128)S(1)} %fusion.2.code_ref, bf16[1024,768]{1,0:T(8,128)(2,1)S(1)} %get-tuple-element.15.refs_0_, bf16[1024,768]{1,0:T(8,128)(2,1)S(1)} %get-tuple-element.16.refs_1_, bf16[2,384,384]{2,1,0:T(8,128)(2,1)S(1)} %get-tuple-element.17.refs_2_, ...), custom_call_target="tpu_custom_call" | custom-call | flops 800000000 | bytes 532480 | tf_op jit(solution)/shard_map/pallas_call | solution.py:235
  34.6 2.0 %shard_map.41 = (bf16[1040,256]{1,0:T(8,128)(2,1)S(1)}, f32[256,256]{1,0:T(8,128)S(1)}, f32[256,256]{1,0:T(8,128)S(1)}, f32[256,256]{1,0:T(8,128)S(1)}, f32[272,256]{1,0:T(8,128)S(1)}) custom-call(s32[2,3]{1,0:T(2,128)S(1)} %fusion.2.code_ref, bf16[1024,768]{1,0:T(8,128)(2,1)S(1)} %get-tuple-element.15.refs_0_, ...), custom_call_target="tpu_custom_call" | custom-call | flops 1600000000 | bytes 1597440 | tf_op jit(solution)/shard_map/pallas_call | solution.py:235
  36.6 0.3 collective-permute-start.5
  36.9 1.9 %collective-permute-start.6 = (bf16[1040,256]{1,0:T(8,128)(2,1)S(1)}, bf16[1040,256]{1,0:T(8,128)(2,1)S(1)}, u32[]{:S(2)}, u32[]{:S(2)}) collective-permute-start(bf16[1040,256]{1,0:T(8,128)(2,1)S(1)} %shard_map.40), channel_id=1, source_target_pairs={{0,0},{7,7},{1,2},{2,1},{3,4},{4,3},{5,6},{6,5},{8,8},{15,15},{9,1... | collective-permute-start | bytes 1597448 | tf_op jit(solution)/shard_map/ppermute | solution.py:31
  38.9 0.0 collective-permute-done.5
  38.9 8.6 %collective-permute-done.6 = bf16[1040,256]{1,0:T(8,128)(2,1)S(1)} collective-permute-done((bf16[1040,256]{1,0:T(8,128)(2,1)S(1)}, bf16[1040,256]{1,0:T(8,128)(2,1)S(1)}, u32[]{:S(2)}, u32[]{:S(2)}) %collective-permute-start.6) | collective-permute-done | bytes 532512 | tf_op jit(solution)/shard_map/ppermute | solution.py:31
  47.5 0.2 add_convert_fusion.7
  47.8 1.6 %collective-permute-start.7 = (bf16[256,256]{1,0:T(8,128)(2,1)S(1)}, bf16[256,256]{1,0:T(8,128)(2,1)S(1)}, u32[]{:S(2)}, u32[]{:S(2)}) collective-permute-start(bf16[256,256]{1,0:T(8,128)(2,1)S(1)} %get-tuple-element.25), channel_id=1, source_target_pairs={{0,8},{8,0},{16,24},{24,16},{1,9},{9,1},{17,25},{25,17},{2,10},{10... | collective-permute-start | bytes 393224 | tf_op jit(solution)/shard_map/ppermute | solution.py:36
  49.3 1.5 %collective-permute-start.13 = (bf16[256,256]{1,0:T(8,128)(2,1)S(1)}, bf16[256,256]{1,0:T(8,128)(2,1)S(1)}, u32[]{:S(2)}, u32[]{:S(2)}) collective-permute-start(bf16[256,256]{1,0:T(8,128)(2,1)S(1)} %get-tuple-element.26), channel_id=1, source_target_pairs={{0,16},{8,24},{16,0},{24,8},{1,17},{9,25},{17,1},{25,9},{2,18},{10... | collective-permute-start | bytes 393224 | tf_op jit(solution)/shard_map/ppermute | solution.py:36
  50.8 0.5 collective-permute-start.11
  51.4 0.5 collective-permute-start.9
  51.9 2.0 %collective-permute-done.7 = bf16[256,256]{1,0:T(8,128)(2,1)S(1)} collective-permute-done((bf16[256,256]{1,0:T(8,128)(2,1)S(1)}, bf16[256,256]{1,0:T(8,128)(2,1)S(1)}, u32[]{:S(2)}, u32[]{:S(2)}) %collective-permute-start.7) | collective-permute-done | bytes 131104 | tf_op jit(solution)/shard_map/ppermute | solution.py:36
  53.9 1.9 %collective-permute-start.8 = (bf16[256,256]{1,0:T(8,128)(2,1)S(1)}, bf16[256,256]{1,0:T(8,128)(2,1)S(1)}, u32[]{:S(2)}, u32[]{:S(2)}) collective-permute-start(bf16[256,256]{1,0:T(8,128)(2,1)S(1)} %add_convert_fusion.6), channel_id=1, source_target_pairs={{0,16},{8,24},{16,0},{24,8},{1,17},{9,25},{17,1},{25,9},{2,18},{10... | collective-permute-start | bytes 393224 | tf_op jit(solution)/shard_map/ppermute | solution.py:36
  55.8 0.0 collective-permute-done.13
  55.9 1.6 %collective-permute-start.14 = (bf16[256,256]{1,0:T(8,128)(2,1)S(1)}, bf16[256,256]{1,0:T(8,128)(2,1)S(1)}, u32[]{:S(2)}, u32[]{:S(2)}) collective-permute-start(bf16[256,256]{1,0:T(8,128)(2,1)S(1)} %add_convert_fusion), channel_id=1, source_target_pairs={{0,8},{8,0},{16,24},{24,16},{1,9},{9,1},{17,25},{25,17},{2,10},{10... | collective-permute-start | bytes 393224 | tf_op jit(solution)/shard_map/ppermute | solution.py:36
  57.4 0.0 collective-permute-done.11
  57.5 0.6 collective-permute-start.12
  58.0 0.5 collective-permute-done.9
  58.5 1.4 %collective-permute-start.10 = (bf16[256,256]{1,0:T(8,128)(2,1)S(1)}, bf16[256,256]{1,0:T(8,128)(2,1)S(1)}, u32[]{:S(2)}, u32[]{:S(2)}) collective-permute-start(bf16[256,256]{1,0:T(8,128)(2,1)S(1)} %add_convert_fusion.4), channel_id=1, source_target_pairs={{0,8},{8,0},{16,24},{24,16},{1,9},{9,1},{17,25},{25,17},{2,10},{10... | collective-permute-start | bytes 393224 | tf_op jit(solution)/shard_map/ppermute | solution.py:36
  59.9 1.4 %collective-permute-done.8 = bf16[256,256]{1,0:T(8,128)(2,1)S(1)} collective-permute-done((bf16[256,256]{1,0:T(8,128)(2,1)S(1)}, bf16[256,256]{1,0:T(8,128)(2,1)S(1)}, u32[]{:S(2)}, u32[]{:S(2)}) %collective-permute-start.8) | collective-permute-done | bytes 131104 | tf_op jit(solution)/shard_map/ppermute | solution.py:36
  61.3 0.7 %collective-permute-done.14 = bf16[256,256]{1,0:T(8,128)(2,1)S(1)} collective-permute-done((bf16[256,256]{1,0:T(8,128)(2,1)S(1)}, bf16[256,256]{1,0:T(8,128)(2,1)S(1)}, u32[]{:S(2)}, u32[]{:S(2)}) %collective-permute-start.14) | collective-permute-done | bytes 131104 | tf_op jit(solution)/shard_map/ppermute | solution.py:36
  62.1 1.0 %collective-permute-done.12 = bf16[256,256]{1,0:T(8,128)(2,1)S(1)} collective-permute-done((bf16[256,256]{1,0:T(8,128)(2,1)S(1)}, bf16[256,256]{1,0:T(8,128)(2,1)S(1)}, u32[]{:S(2)}, u32[]{:S(2)}) %collective-permute-start.12) | collective-permute-done | bytes 131104 | tf_op jit(solution)/shard_map/ppermute | solution.py:36
  63.2 0.6 collective-permute-done.10
  63.7 1.1 %fusion = f32[1024,256]{1,0:T(8,128)} fusion(f32[256,256]{1,0:T(8,128)S(1)} %convert_add_fusion, f32[256,256]{1,0:T(8,128)S(1)} %convert_add_fusion.1, f32[256,256]{1,0:T(8,128)S(1)} %convert_add_fusion.2, f32[256,256]{1,0:T(8,128)S(1)} %convert_add_fusion.3, f32[256]{0:T(256)S(1)} %bitcast.5), kind=kLoop, calls=%fused_computation.1 | loop fusion | flops 1310720 | bytes 2098176 | tf_op jit(solution)/shard_map/div | solution.py:268
  (10 shorter events, 0.3 us)
Async XLA Ops:
  0.0 11.3 %copy-start = (bf16[1024,256]{1,0:T(8,128)(2,1)S(1)}, bf16[1024,256]{1,0:T(8,128)(2,1)}, u32[]{:S(2)}) copy-start(bf16[1024,256]{1,0:T(8,128)(2,1)} %own_ref.1) | copy-start | bytes 1572868
  0.0 9.3 %copy-start.1 = (s32[2,3]{1,0:T(2,128)S(1)}, s32[2,3]{1,0:T(2,128)}, u32[]{:S(2)}) copy-start(s32[2,3]{1,0:T(2,128)} %param.5) | copy-start | bytes 76
  0.0 16.9 %collective-permute-start.2 = (bf16[2,1024,256]{2,1,0:T(8,128)(2,1)}, bf16[2,1024,256]{2,1,0:T(8,128)(2,1)S(1)}, u32[]{:S(2)}, u32[]{:S(2)}) collective-permute-start(bf16[2,1024,256]{2,1,0:T(8,128)(2,1)} %param.3), channel_id=1, source_target_pairs={{0,1},{1,0},{2,3},{3,2},{4,5},{5,4},{6,7},{7,6},{8,9},{9,8},{10,11... | collective-permute-start | bytes 3145736 | tf_op jit(solution)/shard_map/ppermute | solution.py:23
  0.0 9.3 %collective-permute-start = (bf16[1024,256]{1,0:T(8,128)(2,1)}, bf16[1024,256]{1,0:T(8,128)(2,1)}, u32[]{:S(2)}, u32[]{:S(2)}) collective-permute-start(bf16[1024,256]{1,0:T(8,128)(2,1)} %own_ref.1), channel_id=1, source_target_pairs={{0,1},{1,0},{2,3},{3,2},{4,5},{5,4},{6,7},{7,6},{8,9},{9,8},{10,11... | collective-permute-start | bytes 1572872 | tf_op jit(solution)/shard_map/ppermute | solution.py:23
  0.5 10.8 %collective-permute-start.1 = (bf16[1024,256]{1,0:T(8,128)(2,1)}, bf16[1024,256]{1,0:T(8,128)(2,1)}, u32[]{:S(2)}, u32[]{:S(2)}) collective-permute-start(bf16[1024,256]{1,0:T(8,128)(2,1)} %own_ref.1), channel_id=1, source_target_pairs={{0,0},{7,7},{1,2},{2,1},{3,4},{4,3},{5,6},{6,5},{8,8},{15,15},{9,1... | collective-permute-start | bytes 1572872 | tf_op jit(solution)/shard_map/ppermute | solution.py:31
  3.7 13.2 %collective-permute-start.4 = (bf16[1024,256]{1,0:T(8,128)(2,1)S(1)}, bf16[1024,256]{1,0:T(8,128)(2,1)}, u32[]{:S(2)}, u32[]{:S(2)}) collective-permute-start(bf16[1024,256]{1,0:T(8,128)(2,1)S(1)} %get-tuple-element.29.own_ref), channel_id=1, source_target_pairs={{0,0},{7,7},{1,2},{2,1},{3,4},{4,3},{5,6},{6,5},{8,8},{15,15},{9,1... | collective-permute-start | bytes 1572872 | tf_op jit(solution)/shard_map/ppermute | solution.py:31
  7.4 18.3 %collective-permute-start.3 = (bf16[1024,256]{1,0:T(8,128)(2,1)S(1)}, bf16[1024,256]{1,0:T(8,128)(2,1)S(1)}, u32[]{:S(2)}, u32[]{:S(2)}) collective-permute-start(bf16[1024,256]{1,0:T(8,128)(2,1)S(1)} %get-tuple-element.30.own_ref), channel_id=1, source_target_pairs={{0,0},{7,7},{1,2},{2,1},{3,4},{4,3},{5,6},{6,5},{8,8},{15,15},{9,1... | collective-permute-start | bytes 1572872 | tf_op jit(solution)/shard_map/ppermute | solution.py:31
  36.6 2.3 %collective-permute-start.5 = (bf16[1040,256]{1,0:T(8,128)(2,1)S(1)}, bf16[1040,256]{1,0:T(8,128)(2,1)S(1)}, u32[]{:S(2)}, u32[]{:S(2)}) collective-permute-start(bf16[1040,256]{1,0:T(8,128)(2,1)S(1)} %get-tuple-element.21), channel_id=1, source_target_pairs={{0,1},{1,0},{2,3},{3,2},{4,5},{5,4},{6,7},{7,6},{8,9},{9,8},{10,11... | collective-permute-start | bytes 1597448 | tf_op jit(solution)/shard_map/ppermute | solution.py:23
  36.9 10.6 %collective-permute-start.6 = (bf16[1040,256]{1,0:T(8,128)(2,1)S(1)}, bf16[1040,256]{1,0:T(8,128)(2,1)S(1)}, u32[]{:S(2)}, u32[]{:S(2)}) collective-permute-start(bf16[1040,256]{1,0:T(8,128)(2,1)S(1)} %shard_map.40), channel_id=1, source_target_pairs={{0,0},{7,7},{1,2},{2,1},{3,4},{4,3},{5,6},{6,5},{8,8},{15,15},{9,1... | collective-permute-start | bytes 1597448 | tf_op jit(solution)/shard_map/ppermute | solution.py:31
  47.8 6.1 %collective-permute-start.7 = (bf16[256,256]{1,0:T(8,128)(2,1)S(1)}, bf16[256,256]{1,0:T(8,128)(2,1)S(1)}, u32[]{:S(2)}, u32[]{:S(2)}) collective-permute-start(bf16[256,256]{1,0:T(8,128)(2,1)S(1)} %get-tuple-element.25), channel_id=1, source_target_pairs={{0,8},{8,0},{16,24},{24,16},{1,9},{9,1},{17,25},{25,17},{2,10},{10... | collective-permute-start | bytes 393224 | tf_op jit(solution)/shard_map/ppermute | solution.py:36
  49.3 6.5 %collective-permute-start.13 = (bf16[256,256]{1,0:T(8,128)(2,1)S(1)}, bf16[256,256]{1,0:T(8,128)(2,1)S(1)}, u32[]{:S(2)}, u32[]{:S(2)}) collective-permute-start(bf16[256,256]{1,0:T(8,128)(2,1)S(1)} %get-tuple-element.26), channel_id=1, source_target_pairs={{0,16},{8,24},{16,0},{24,8},{1,17},{9,25},{17,1},{25,9},{2,18},{10... | collective-permute-start | bytes 393224 | tf_op jit(solution)/shard_map/ppermute | solution.py:36
  50.8 6.6 %collective-permute-start.11 = (bf16[256,256]{1,0:T(8,128)(2,1)S(1)}, bf16[256,256]{1,0:T(8,128)(2,1)S(1)}, u32[]{:S(2)}, u32[]{:S(2)}) collective-permute-start(bf16[256,256]{1,0:T(8,128)(2,1)S(1)} %get-tuple-element.27), channel_id=1, source_target_pairs={{0,8},{8,0},{16,24},{24,16},{1,9},{9,1},{17,25},{25,17},{2,10},{10... | collective-permute-start | bytes 393224 | tf_op jit(solution)/shard_map/ppermute | solution.py:36
  51.4 7.1 %collective-permute-start.9 = (bf16[256,256]{1,0:T(8,128)(2,1)S(1)}, bf16[256,256]{1,0:T(8,128)(2,1)S(1)}, u32[]{:S(2)}, u32[]{:S(2)}) collective-permute-start(bf16[256,256]{1,0:T(8,128)(2,1)S(1)} %get-tuple-element.28), channel_id=1, source_target_pairs={{0,16},{8,24},{16,0},{24,8},{1,17},{9,25},{17,1},{25,9},{2,18},{10... | collective-permute-start | bytes 393224 | tf_op jit(solution)/shard_map/ppermute | solution.py:36
  53.9 7.4 %collective-permute-start.8 = (bf16[256,256]{1,0:T(8,128)(2,1)S(1)}, bf16[256,256]{1,0:T(8,128)(2,1)S(1)}, u32[]{:S(2)}, u32[]{:S(2)}) collective-permute-start(bf16[256,256]{1,0:T(8,128)(2,1)S(1)} %add_convert_fusion.6), channel_id=1, source_target_pairs={{0,16},{8,24},{16,0},{24,8},{1,17},{9,25},{17,1},{25,9},{2,18},{10... | collective-permute-start | bytes 393224 | tf_op jit(solution)/shard_map/ppermute | solution.py:36
  55.9 6.2 %collective-permute-start.14 = (bf16[256,256]{1,0:T(8,128)(2,1)S(1)}, bf16[256,256]{1,0:T(8,128)(2,1)S(1)}, u32[]{:S(2)}, u32[]{:S(2)}) collective-permute-start(bf16[256,256]{1,0:T(8,128)(2,1)S(1)} %add_convert_fusion), channel_id=1, source_target_pairs={{0,8},{8,0},{16,24},{24,16},{1,9},{9,1},{17,25},{25,17},{2,10},{10... | collective-permute-start | bytes 393224 | tf_op jit(solution)/shard_map/ppermute | solution.py:36
  57.5 5.7 %collective-permute-start.12 = (bf16[256,256]{1,0:T(8,128)(2,1)S(1)}, bf16[256,256]{1,0:T(8,128)(2,1)S(1)}, u32[]{:S(2)}, u32[]{:S(2)}) collective-permute-start(bf16[256,256]{1,0:T(8,128)(2,1)S(1)} %add_convert_fusion.2), channel_id=1, source_target_pairs={{0,16},{8,24},{16,0},{24,8},{1,17},{9,25},{17,1},{25,9},{2,18},{10... | collective-permute-start | bytes 393224 | tf_op jit(solution)/shard_map/ppermute | solution.py:36
  58.5 5.2 %collective-permute-start.10 = (bf16[256,256]{1,0:T(8,128)(2,1)S(1)}, bf16[256,256]{1,0:T(8,128)(2,1)S(1)}, u32[]{:S(2)}, u32[]{:S(2)}) collective-permute-start(bf16[256,256]{1,0:T(8,128)(2,1)S(1)} %add_convert_fusion.4), channel_id=1, source_target_pairs={{0,8},{8,0},{16,24},{24,16},{1,9},{9,1},{17,25},{25,17},{2,10},{10... | collective-permute-start | bytes 393224 | tf_op jit(solution)/shard_map/ppermute | solution.py:36

commit v3 on v2

--- a/solution.py
+++ b/solution.py
@@ -85,23 +85,37 @@
         gram_ref[g, :head, head:] = low[:, :head].T
     for g in range(lights):
         now = now_ref[g]
-        product = jnp.dot(gram_ref[g], now, preferred_element_type=jnp.float32)
+        product = jnp.dot(gram_ref[g, :, :head], now[:head], preferred_element_type=jnp.float32)
+        product += jnp.dot(gram_ref[g, :, head:], now[head:], preferred_element_type=jnp.float32)
         next_ref[g] = (1.5 * now.astype(jnp.float32) - 0.5 * product).astype(jnp.bfloat16)
 
 
-def polar_kernel(subject, code_ref, tmpl_ref, own_ref, near_ref, far_ref, map_ref, cols_ref, odd_ref, gram_ref):
+def polar_kernel(subject, code_ref, tmpl_ref, own_ref, near_ref, far_ref, map_ref, cols_ref, odd_ref, gram_ref, *stage):
     lights, members = code_ref.shape
     width = members * BLOCK
     frames = own_ref.shape[0]
-    for g in range(lights):
-        for i in range(members):
-            code = code_ref[g, i]
-            lo = g * width + i * BLOCK
-            for place, ref in enumerate((own_ref, near_ref.at[subject], far_ref)):
-
-                @pl.when(code // 2 == place)
-                def _():
-                    cols_ref[:, lo : lo + BLOCK] = columns(ref, code % 2)
+    arrival = None
+    if stage:
+        staged_ref, arrived = stage
+        arrival = pltpu.make_async_copy(far_ref, staged_ref, arrived)
+        arrival.start()
+        far_ref = staged_ref
+
+    def gather(sources):
+        for g in range(lights):
+            for i in range(members):
+                code = code_ref[g, i]
+                lo = g * width + i * BLOCK
+                for place, ref in sources:
+
+                    @pl.when(code // 2 == place)
+                    def _():
+                        cols_ref[:, lo : lo + BLOCK] = columns(ref, code % 2)
+
+    gather(((0, own_ref), (1, near_ref.at[subject])))
+    if arrival is not None:
+        arrival.wait()
+    gather(((2, far_ref),))
 
     first_ref = map_ref if NS_STEPS % 2 == 0 else odd_ref
     row = lax.broadcasted_iota(jnp.int32, (width, width), 0)
@@ -156,25 +170,26 @@
         weights = [
             weight_ref[first : first + step_cols, s * depth : (s + 1) * depth] for s in range(subj_count)
         ]
-        rows = cols_refs[0].shape[0] // pieces
-        for piece in range(pieces):
+        for b in range(group):
+            tally = jnp.full((COUNT_ROWS, BLOCK), counts[n * group + b], jnp.int32)
+            out_refs[at][pieces[0] :, b * BLOCK : (b + 1) * BLOCK] = tally.astype(jnp.float32).astype(
+                out_refs[at].dtype
+            )
+        above = 0
+        for rows in pieces:
             for lo in range(0, rows, chunk):
                 total = None
                 for s in range(subj_count):
                     term = lax.dot_general(
-                        cols_refs[s][piece * rows + lo : piece * rows + lo + chunk, :],
+                        cols_refs[s][above + lo : above + lo + chunk, :],
                         weights[s],
                         (((1,), (1,)), ((), ())),
                         preferred_element_type=jnp.float32,
                     )
                     total = term if total is None else total + term
                 out_refs[at][lo : lo + chunk, :] = total.astype(out_refs[at].dtype)
+            above += rows
             at += 1
-        for b in range(group):
-            tally = jnp.full((COUNT_ROWS, BLOCK), counts[n * group + b], jnp.int32)
-            out_refs[at - 1][rows:, b * BLOCK : (b + 1) * BLOCK] = tally.astype(jnp.float32).astype(
-                out_refs[at - 1].dtype
-            )
 
 
 def body(series, template, sl_blocks):
@@ -216,21 +231,20 @@
                 jax.ShapeDtypeStruct((lights, width, width), jnp.bfloat16),
                 jax.ShapeDtypeStruct((frames, lights * width), jnp.bfloat16),
             ),
-            [vmem()] * 5,
+            [vmem()] * 4 + [pl.BlockSpec(memory_space=pl.ANY) if s > 0 else vmem()],
             flops=8 * 10**9,
             limit=LIMIT,
-            scratch=[pltpu.VMEM((lights, width, width), jnp.bfloat16)] * 2,
+            scratch=[pltpu.VMEM((lights, width, width), jnp.bfloat16)] * 2
+            + ([pltpu.VMEM((frames, width_dev), jnp.bfloat16), pltpu.SemaphoreType.DMA] if s > 0 else []),
         )(code, tmpl_rows, parts[s], near, far[s])
         maps.append(polar)
         cols.append(gathered)
 
     def mapped(places, splits, types):
         shapes = [
-            jax.ShapeDtypeStruct(
-                (frames // pieces + (COUNT_ROWS if piece == pieces - 1 else 0), width_dev), kind
-            )
+            jax.ShapeDtypeStruct((rows + (COUNT_ROWS if n == 0 else 0), width_dev), kind)
             for pieces, kind in zip(splits, types)
-            for piece in range(pieces)
+            for n, rows in enumerate(pieces)
         ]
         return call(
             functools.partial(map_kernel, subj_count, places, splits),
@@ -241,31 +255,47 @@
             scratch=[pltpu.VMEM((len(places) * BLOCK, subj_count * lights * width), jnp.bfloat16)],
         )(code, *cols, *maps)
 
+    subj_size = lax.axis_size("subj")
+    distances = subject_distances(subj_size)
+    rows = frames // PIECES
+    late = frames - rows
     blocks = list(range(blk_dev))
-    (to_far,) = mapped([2 * blk_dev + b for b in blocks], (1,), (jnp.bfloat16,))
+
+    def swapped(value, step, turn):
+        got = swap_subj(value, distances[(step + turn) % len(distances)])
+        return value.astype(jnp.float32) + got.astype(jnp.float32)
+
+    to_far, early_far = mapped([2 * blk_dev + b for b in blocks], ((late, rows),), (jnp.bfloat16,))
     from_far = swap_far(to_far)
     code, _ = lax.optimization_barrier((code, to_far))
-    to_near, *own = mapped([blk_dev + b for b in blocks] + blocks, (1, PIECES), (jnp.bfloat16, jnp.float32))
+    to_near, *own = mapped(
+        [blk_dev + b for b in blocks] + blocks, ((frames,), (rows,) * PIECES), (jnp.bfloat16, jnp.float32)
+    )
     from_near = swap_near(to_near)
+    early_own = own[-1] + from_near[late:frames].astype(jnp.float32)
+    early_own, from_near = lax.optimization_barrier((early_own.astype(jnp.bfloat16), from_near))
     keep = far_real.astype(jnp.float32)
 
-    def joined(mine, lo, hi):
-        return mine + from_near[lo:hi].astype(jnp.float32) + keep * from_far[lo:hi].astype(jnp.float32)
-
-    rows = frames // PIECES
-    per_vertex = joined(own[-1][rows : rows + 1], frames, frames + 1)
-    halves = [joined(own[h][:rows], h * rows, (h + 1) * rows) for h in range(PIECES)]
-    subj_size = lax.axis_size("subj")
+    def joined(mine, lo, far_lo, size):
+        near_rows = from_near[lo : lo + size].astype(jnp.float32)
+        return mine + near_rows + keep * from_far[far_lo : far_lo + size].astype(jnp.float32)
+
+    per_vertex = joined(own[0][rows : rows + 1], frames, late, 1)
+    parts = [joined(own[h][:rows], h * rows, h * rows, rows) for h in range(PIECES - 1)]
+    for step in range(len(distances)):
+        early_own = swapped(early_own.astype(jnp.bfloat16), step, 1)
+        early_far = swapped(early_far.astype(jnp.bfloat16), step, 0)
+        parts = [swapped(p.astype(jnp.bfloat16), step, h) for h, p in enumerate(parts)]
+    early_back = swap_far(early_far.astype(jnp.bfloat16))
+    parts.append(early_own + keep * early_back.astype(jnp.float32))
+    return jnp.concatenate(parts, axis=0) / per_vertex / (subj_count * subj_size)
+
+
+def subject_distances(size):
     distances = []
-    while 2 ** len(distances) < subj_size:
+    while 2 ** len(distances) < size:
         distances.append(2 ** len(distances))
-    for step in range(len(distances)):
-        for h in range(PIECES):
-            sent = halves[h].astype(jnp.bfloat16)
-            got = swap_subj(sent, distances[(step + h) % len(distances)])
-            halves[h] = sent.astype(jnp.float32) + got.astype(jnp.float32)
-    total = jnp.concatenate(halves, axis=0)
-    return total / per_vertex / (subj_count * subj_size)
+    return distances
 
 
 def solution(mesh):

time: 65.3 us -> 69.6 us (1.066)
  starting transfers between devices: 19.7 us -> 23.6 us
    ppermute x8 -> x10, waiting for transfers between devices: 6.15 us -> 11.9 us  [swap_subj(): lax.ppermute(value, 'subj', [(i, i ^ distance) for i in range(count)])]
    ppermute x4 -> x5, waiting for transfers between devices: 13.7 us -> 8.61 us  [swap_far(): return lax.ppermute(value, 'cortex', route)]
    ppermute x4 -> x5, starting transfers between devices: 9.38 us -> 11.5 us  [swap_far(): return lax.ppermute(value, 'cortex', route)]
    ppermute x8 -> x10, starting transfers between devices: 9.54 us -> 11.5 us  [swap_subj(): lax.ppermute(value, 'subj', [(i, i ^ distance) for i in range(count)])]
  transfers between devices with their start and end apart: 15 -> 18, of which waited for: 9 -> 11; matrix products, arithmetic and copies ran while one was open for 2% -> 3% of each run, Pallas kernels for 17% -> 18%
where the time goes in v3:
time: 69.6 us; the launch traced here: 69.1 us
  starting transfers between devices  23.6 us (34%)
  Pallas kernels  21.9 us (31%)
  waiting for transfers between devices  20.5 us (29%)
  other arithmetic  1.6 us (2%)
  local copies, waits for them, and re-layouts  1.28 us (2%)
    pallas_call x2, Pallas kernels, body(): call(functools.partial(polar_kernel, s), (jax.ShapeDtypeStruct((lights, w...  16.3 us
    ppermute x10, waiting for transfers between devices, swap_subj(): lax.ppermute(value, 'subj', [(i, i ^ distance) for i in range(count)])  11.9 us
    ppermute x10, starting transfers between devices, swap_subj(): lax.ppermute(value, 'subj', [(i, i ^ distance) for i in range(count)])  11.5 us
    ppermute x5, starting transfers between devices, swap_far(): return lax.ppermute(value, 'cortex', route)  11.5 us
    ppermute x5, waiting for transfers between devices, swap_far(): return lax.ppermute(value, 'cortex', route)  8.61 us
    pallas_call x2, Pallas kernels, mapped(): call(functools.partial(map_kernel, subj_count, places, splits), shapes, [...  3.11 us
    pallas_call x1, Pallas kernels, body(): call(template_kernel, jax.ShapeDtypeStruct((lights, width, frames), jnp.b...  2.49 us
  transfers between devices with their start and end apart: 18, of which 11 were waited for; matrix products, arithmetic and copies ran while one was open for 3% of the time, Pallas kernels for 18%

profile of v3, /device:TPU:8, one launch (start us, length us, event | category | flops | bytes accessed | tf_op | source)
XLA Modules:
  0.0 69.1 jit_solution(7913439736049525244)
XLA Ops:
  0.0 0.0 copy-start
  0.0 0.0 collective-permute-start.2
  0.0 0.5 collective-permute-start
  0.5 1.9 %collective-permute-start.1 = (bf16[1024,256]{1,0:T(8,128)(2,1)}, bf16[1024,256]{1,0:T(8,128)(2,1)}, u32[]{:S(2)}, u32[]{:S(2)}) collective-permute-start(bf16[1024,256]{1,0:T(8,128)(2,1)} %own_ref.1), channel_id=1, source_target_pairs={{0,0},{7,7},{1,2},{2,1},{3,4},{4,3},{5,6},{6,5},{8,8},{15,15},{9,1... | collective-permute-start | bytes 1572872 | tf_op jit(solution)/shard_map/ppermute | solution.py:31
  2.4 1.3 %slice_bitcast_fusion = (bf16[1024,256]{1,0:T(8,128)(2,1)S(1)}, bf16[1024,256]{1,0:T(8,128)(2,1)S(1)}) fusion(bf16[2,1024,256]{2,1,0:T(8,128)(2,1)} %param.3), kind=kLoop, calls=%fused_computation.2 | loop fusion | bytes 2097152 | tf_op jit(solution)/shard_map/squeeze | solution.py:207
  3.7 3.6 %collective-permute-start.4 = (bf16[1024,256]{1,0:T(8,128)(2,1)S(1)}, bf16[1024,256]{1,0:T(8,128)(2,1)}, u32[]{:S(2)}, u32[]{:S(2)}) collective-permute-start(bf16[1024,256]{1,0:T(8,128)(2,1)S(1)} %get-tuple-element.33.own_ref), channel_id=1, source_target_pairs={{0,0},{7,7},{1,2},{2,1},{3,4},{4,3},{5,6},{6,5},{8,8},{15,15},{9,1... | collective-permute-start | bytes 1572872 | tf_op jit(solution)/shard_map/ppermute | solution.py:31
  7.4 1.9 %collective-permute-start.3 = (bf16[1024,256]{1,0:T(8,128)(2,1)S(1)}, bf16[1024,256]{1,0:T(8,128)(2,1)S(1)}, u32[]{:S(2)}, u32[]{:S(2)}) collective-permute-start(bf16[1024,256]{1,0:T(8,128)(2,1)S(1)} %get-tuple-element.34.own_ref), channel_id=1, source_target_pairs={{0,0},{7,7},{1,2},{2,1},{3,4},{4,3},{5,6},{6,5},{8,8},{15,15},{9,1... | collective-permute-start | bytes 1572872 | tf_op jit(solution)/shard_map/ppermute | solution.py:31
  9.3 0.0 copy-done.1
  9.3 0.0 collective-permute-done.near_ref
  9.3 2.0 %collective-permute-done.1.far_ref = bf16[1024,256]{1,0:T(8,128)(2,1)} collective-permute-done((bf16[1024,256]{1,0:T(8,128)(2,1)}, bf16[1024,256]{1,0:T(8,128)(2,1)}, u32[]{:S(2)}, u32[]{:S(2)}) %collective-permute-start.1) | collective-permute-done | bytes 524320 | tf_op jit(solution)/shard_map/ppermute | solution.py:31
  11.3 0.0 copy-done
  11.3 2.5 %shard_map.37.tmpl_ref = bf16[2,384,1024]{2,1,0:T(8,128)(2,1)S(1)} custom-call(s32[2,3]{1,0:T(2,128)S(1)} %fusion.2.code_ref, bf16[1024,256]{1,0:T(8,128)(2,1)S(1)} %copy-done, bf16[1024,256]{1,0:T(8,128)(2,1)} %collective-permute-done.near_ref, bf16[1024,256]{1,0:T(8,128)(2,1)} %collective-permute-done.1.far_ref), custom_call_target="tpu_custom_call" | custom-call | flops 1000000000 | bytes 1572864 | tf_op jit(solution)/shard_map/pallas_call | solution.py:218
  13.8 3.1 %collective-permute-done.4.far_ref = bf16[1024,256]{1,0:T(8,128)(2,1)} collective-permute-done((bf16[1024,256]{1,0:T(8,128)(2,1)S(1)}, bf16[1024,256]{1,0:T(8,128)(2,1)}, u32[]{:S(2)}, u32[]{:S(2)}) %collective-permute-start.4) | collective-permute-done | bytes 524320 | tf_op jit(solution)/shard_map/ppermute | solution.py:31
  16.9 0.0 collective-permute-done.2.near_ref
  16.9 8.2 %shard_map.39 = (bf16[2,384,384]{2,1,0:T(8,128)(2,1)S(1)}, bf16[1024,768]{1,0:T(8,128)(2,1)S(1)}) custom-call(s32[2,3]{1,0:T(2,128)S(1)} %fusion.2.code_ref, bf16[2,384,1024]{2,1,0:T(8,128)(2,1)S(1)} %shard_map.37.tmpl_ref, bf16[1024,256]{1,0:T(8,128)(2,1)S(1)} %get-tuple-element.33.own_ref, bf16[2,1024,256]{2,1,0:T(8,128)(2,1)S(1)} %collective-permute-done.2.near_ref, ...), custom_call_target="tpu_custom_call" | custom-call | flops 8000000000 | bytes 2162688 | tf_op jit(solution)/shard_map/pallas_call | solution.py:228
  25.2 0.0 collective-permute-done.3.far_ref
  25.2 8.1 %shard_map.38 = (bf16[2,384,384]{2,1,0:T(8,128)(2,1)S(1)}, bf16[1024,768]{1,0:T(8,128)(2,1)S(1)}) custom-call(s32[2,3]{1,0:T(2,128)S(1)} %fusion.2.code_ref, bf16[2,384,1024]{2,1,0:T(8,128)(2,1)S(1)} %shard_map.37.tmpl_ref, bf16[1024,256]{1,0:T(8,128)(2,1)S(1)} %get-tuple-element.34.own_ref, bf16[2,1024,256]{2,1,0:T(8,128)(2,1)S(1)} %collective-permute-done.2.near_ref, ...), custom_call_target="tpu_custom_call" | custom-call | flops 8000000000 | bytes 2162688 | tf_op jit(solution)/shard_map/pallas_call | solution.py:228
  33.3 1.1 %shard_map.40 = (bf16[784,256]{1,0:T(8,128)(2,1)S(1)}, bf16[256,256]{1,0:T(8,128)(2,1)S(1)}) custom-call(s32[2,3]{1,0:T(2,128)S(1)} %fusion.2.code_ref, bf16[1024,768]{1,0:T(8,128)(2,1)S(1)} %get-tuple-element.19.refs_0_, bf16[1024,768]{1,0:T(8,128)(2,1)S(1)} %get-tuple-element.20.refs_1_, bf16[2,384,384]{2,1,0:T(8,128)(2,1)S(1)} %get-tuple-element.21.refs_2_, ...), custom_call_target="tpu_custom_call" | custom-call | flops 800000000 | bytes 532480 | tf_op jit(solution)/shard_map/pallas_call | solution.py:249
  34.4 1.6 %collective-permute-start.15 = (bf16[256,256]{1,0:T(8,128)(2,1)S(1)}, bf16[256,256]{1,0:T(8,128)(2,1)S(1)}, u32[]{:S(2)}, u32[]{:S(2)}) collective-permute-start(bf16[256,256]{1,0:T(8,128)(2,1)S(1)} %get-tuple-element.32), channel_id=1, source_target_pairs={{0,8},{8,0},{16,24},{24,16},{1,9},{9,1},{17,25},{25,17},{2,10},{10... | collective-permute-start | bytes 393224 | tf_op jit(solution)/shard_map/ppermute | solution.py:36
  36.0 2.0 %shard_map.41 = (bf16[1040,256]{1,0:T(8,128)(2,1)S(1)}, f32[272,256]{1,0:T(8,128)S(1)}, f32[256,256]{1,0:T(8,128)S(1)}, f32[256,256]{1,0:T(8,128)S(1)}, f32[256,256]{1,0:T(8,128)S(1)}) custom-call(s32[2,3]{1,0:T(2,128)S(1)} %fusion.2.code_ref, bf16[1024,768]{1,0:T(8,128)(2,1)S(1)} %get-tuple-element.19.refs_0_, ...), custom_call_target="tpu_custom_call" | custom-call | flops 1600000000 | bytes 1597440 | tf_op jit(solution)/shard_map/pallas_call | solution.py:249
  38.0 0.1 collective-permute-start.5
  38.1 2.1 %collective-permute-done.15 = bf16[256,256]{1,0:T(8,128)(2,1)S(1)} collective-permute-done((bf16[256,256]{1,0:T(8,128)(2,1)S(1)}, bf16[256,256]{1,0:T(8,128)(2,1)S(1)}, u32[]{:S(2)}, u32[]{:S(2)}) %collective-permute-start.15) | collective-permute-done | bytes 131104 | tf_op jit(solution)/shard_map/ppermute | solution.py:36
  40.2 1.6 %collective-permute-start.16 = (bf16[256,256]{1,0:T(8,128)(2,1)S(1)}, bf16[256,256]{1,0:T(8,128)(2,1)S(1)}, u32[]{:S(2)}, u32[]{:S(2)}) collective-permute-start(bf16[256,256]{1,0:T(8,128)(2,1)S(1)} %add_convert_fusion.1), channel_id=1, source_target_pairs={{0,16},{8,24},{16,0},{24,8},{1,17},{9,25},{17,1},{25,9},{2,18},{10... | collective-permute-start | bytes 393224 | tf_op jit(solution)/shard_map/ppermute | solution.py:36
  41.8 1.9 %collective-permute-start.6 = (bf16[784,256]{1,0:T(8,128)(2,1)S(1)}, bf16[784,256]{1,0:T(8,128)(2,1)S(1)}, u32[]{:S(2)}, u32[]{:S(2)}) collective-permute-start(bf16[784,256]{1,0:T(8,128)(2,1)S(1)} %get-tuple-element.23), channel_id=1, source_target_pairs={{0,0},{7,7},{1,2},{2,1},{3,4},{4,3},{5,6},{6,5},{8,8},{15,15},{9,1... | collective-permute-start | bytes 1204232 | tf_op jit(solution)/shard_map/ppermute | solution.py:31
  43.7 1.5 %collective-permute-done.16 = bf16[256,256]{1,0:T(8,128)(2,1)S(1)} collective-permute-done((bf16[256,256]{1,0:T(8,128)(2,1)S(1)}, bf16[256,256]{1,0:T(8,128)(2,1)S(1)}, u32[]{:S(2)}, u32[]{:S(2)}) %collective-permute-start.16) | collective-permute-done | bytes 131104 | tf_op jit(solution)/shard_map/ppermute | solution.py:36
  45.3 2.1 %collective-permute-start.17 = (bf16[256,256]{1,0:T(8,128)(2,1)S(1)}, bf16[256,256]{1,0:T(8,128)(2,1)S(1)}, u32[]{:S(2)}, u32[]{:S(2)}) collective-permute-start(bf16[256,256]{1,0:T(8,128)(2,1)S(1)} %add_convert_fusion), channel_id=1, source_target_pairs={{0,0},{7,7},{1,2},{2,1},{3,4},{4,3},{5,6},{6,5},{8,8},{15,15},{9,1... | collective-permute-start | bytes 393224 | tf_op jit(solution)/shard_map/ppermute | solution.py:31
  47.4 0.0 collective-permute-done.5
  47.5 3.5 %collective-permute-done.6 = bf16[784,256]{1,0:T(8,128)(2,1)S(1)} collective-permute-done((bf16[784,256]{1,0:T(8,128)(2,1)S(1)}, bf16[784,256]{1,0:T(8,128)(2,1)S(1)}, u32[]{:S(2)}, u32[]{:S(2)}) %collective-permute-start.6) | collective-permute-done | bytes 401440 | tf_op jit(solution)/shard_map/ppermute | solution.py:31
  51.0 0.1 add_convert_fusion.8
  51.1 1.6 %collective-permute-start.7 = (bf16[256,256]{1,0:T(8,128)(2,1)S(1)}, bf16[256,256]{1,0:T(8,128)(2,1)S(1)}, u32[]{:S(2)}, u32[]{:S(2)}) collective-permute-start(bf16[256,256]{1,0:T(8,128)(2,1)S(1)} %get-tuple-element.35), channel_id=1, source_target_pairs={{0,8},{8,0},{16,24},{24,16},{1,9},{9,1},{17,25},{25,17},{2,10},{10... | collective-permute-start | bytes 393224 | tf_op jit(solution)/shard_map/ppermute | solution.py:36
  52.7 0.5 collective-permute-start.11
  53.2 0.5 collective-permute-start.9
  53.7 1.5 %collective-permute-start.13 = (bf16[256,256]{1,0:T(8,128)(2,1)S(1)}, bf16[256,256]{1,0:T(8,128)(2,1)S(1)}, u32[]{:S(2)}, u32[]{:S(2)}) collective-permute-start(bf16[256,256]{1,0:T(8,128)(2,1)S(1)} %add_convert_fusion.9), channel_id=1, source_target_pairs={{0,16},{8,24},{16,0},{24,8},{1,17},{9,25},{17,1},{25,9},{2,18},{10... | collective-permute-start | bytes 393224 | tf_op jit(solution)/shard_map/ppermute | solution.py:36
  55.2 2.3 %collective-permute-done.7 = bf16[256,256]{1,0:T(8,128)(2,1)S(1)} collective-permute-done((bf16[256,256]{1,0:T(8,128)(2,1)S(1)}, bf16[256,256]{1,0:T(8,128)(2,1)S(1)}, u32[]{:S(2)}, u32[]{:S(2)}) %collective-permute-start.7) | collective-permute-done | bytes 131104 | tf_op jit(solution)/shard_map/ppermute | solution.py:36
  57.6 0.6 collective-permute-start.8
  58.2 1.6 %collective-permute-done.11 = bf16[256,256]{1,0:T(8,128)(2,1)S(1)} collective-permute-done((bf16[256,256]{1,0:T(8,128)(2,1)S(1)}, bf16[256,256]{1,0:T(8,128)(2,1)S(1)}, u32[]{:S(2)}, u32[]{:S(2)}) %collective-permute-start.11) | collective-permute-done | bytes 131104 | tf_op jit(solution)/shard_map/ppermute | solution.py:36
  59.8 0.6 collective-permute-start.12
  60.4 0.0 collective-permute-done.9
  60.4 1.6 %collective-permute-start.10 = (bf16[256,256]{1,0:T(8,128)(2,1)S(1)}, bf16[256,256]{1,0:T(8,128)(2,1)S(1)}, u32[]{:S(2)}, u32[]{:S(2)}) collective-permute-start(bf16[256,256]{1,0:T(8,128)(2,1)S(1)} %add_convert_fusion.5), channel_id=1, source_target_pairs={{0,8},{8,0},{16,24},{24,16},{1,9},{9,1},{17,25},{25,17},{2,10},{10... | collective-permute-start | bytes 393224 | tf_op jit(solution)/shard_map/ppermute | solution.py:36
  62.0 0.4 collective-permute-done.13
  62.4 1.6 %collective-permute-start.14 = (bf16[256,256]{1,0:T(8,128)(2,1)S(1)}, bf16[256,256]{1,0:T(8,128)(2,1)S(1)}, u32[]{:S(2)}, u32[]{:S(2)}) collective-permute-start(bf16[256,256]{1,0:T(8,128)(2,1)S(1)} %add_convert_fusion.2), channel_id=1, source_target_pairs={{0,8},{8,0},{16,24},{24,16},{1,9},{9,1},{17,25},{25,17},{2,10},{10... | collective-permute-start | bytes 393224 | tf_op jit(solution)/shard_map/ppermute | solution.py:36
  64.0 1.2 %collective-permute-done.8 = bf16[256,256]{1,0:T(8,128)(2,1)S(1)} collective-permute-done((bf16[256,256]{1,0:T(8,128)(2,1)S(1)}, bf16[256,256]{1,0:T(8,128)(2,1)S(1)}, u32[]{:S(2)}, u32[]{:S(2)}) %collective-permute-start.8) | collective-permute-done | bytes 131104 | tf_op jit(solution)/shard_map/ppermute | solution.py:36
  65.2 1.6 %collective-permute-done.12 = bf16[256,256]{1,0:T(8,128)(2,1)S(1)} collective-permute-done((bf16[256,256]{1,0:T(8,128)(2,1)S(1)}, bf16[256,256]{1,0:T(8,128)(2,1)S(1)}, u32[]{:S(2)}, u32[]{:S(2)}) %collective-permute-start.12) | collective-permute-done | bytes 131104 | tf_op jit(solution)/shard_map/ppermute | solution.py:36
  66.9 0.0 collective-permute-done.10
  67.0 0.0 collective-permute-done.17
  67.0 1.0 %collective-permute-done.14 = bf16[256,256]{1,0:T(8,128)(2,1)S(1)} collective-permute-done((bf16[256,256]{1,0:T(8,128)(2,1)S(1)}, bf16[256,256]{1,0:T(8,128)(2,1)S(1)}, u32[]{:S(2)}, u32[]{:S(2)}) %collective-permute-start.14) | collective-permute-done | bytes 131104 | tf_op jit(solution)/shard_map/ppermute | solution.py:36
  68.0 0.1 multiply_add_fusion
  68.0 1.1 %fusion = f32[1024,256]{1,0:T(8,128)} fusion(f32[256,256]{1,0:T(8,128)S(1)} %multiply_add_fusion, f32[256,256]{1,0:T(8,128)S(1)} %convert_add_fusion, f32[256,256]{1,0:T(8,128)S(1)} %convert_add_fusion.1, f32[256,256]{1,0:T(8,128)S(1)} %convert_add_fusion.2, f32[256]{0:T(256)S(1)} %bitcast.5), kind=kLoop, calls=%fused_computation.1 | loop fusion | flops 1310720 | bytes 2098176 | tf_op jit(solution)/shard_map/div | solution.py:291
  (13 shorter events, 0.3 us)
Async XLA Ops:
  0.0 11.3 %copy-start = (bf16[1024,256]{1,0:T(8,128)(2,1)S(1)}, bf16[1024,256]{1,0:T(8,128)(2,1)}, u32[]{:S(2)}) copy-start(bf16[1024,256]{1,0:T(8,128)(2,1)} %own_ref.1) | copy-start | bytes 1572868
  0.0 9.3 %copy-start.1 = (s32[2,3]{1,0:T(2,128)S(1)}, s32[2,3]{1,0:T(2,128)}, u32[]{:S(2)}) copy-start(s32[2,3]{1,0:T(2,128)} %param.5) | copy-start | bytes 76
  0.0 16.9 %collective-permute-start.2 = (bf16[2,1024,256]{2,1,0:T(8,128)(2,1)}, bf16[2,1024,256]{2,1,0:T(8,128)(2,1)S(1)}, u32[]{:S(2)}, u32[]{:S(2)}) collective-permute-start(bf16[2,1024,256]{2,1,0:T(8,128)(2,1)} %param.3), channel_id=1, source_target_pairs={{0,1},{1,0},{2,3},{3,2},{4,5},{5,4},{6,7},{7,6},{8,9},{9,8},{10,11... | collective-permute-start | bytes 3145736 | tf_op jit(solution)/shard_map/ppermute | solution.py:23
  0.0 9.3 %collective-permute-start = (bf16[1024,256]{1,0:T(8,128)(2,1)}, bf16[1024,256]{1,0:T(8,128)(2,1)}, u32[]{:S(2)}, u32[]{:S(2)}) collective-permute-start(bf16[1024,256]{1,0:T(8,128)(2,1)} %own_ref.1), channel_id=1, source_target_pairs={{0,1},{1,0},{2,3},{3,2},{4,5},{5,4},{6,7},{7,6},{8,9},{9,8},{10,11... | collective-permute-start | bytes 1572872 | tf_op jit(solution)/shard_map/ppermute | solution.py:23
  0.5 10.8 %collective-permute-start.1 = (bf16[1024,256]{1,0:T(8,128)(2,1)}, bf16[1024,256]{1,0:T(8,128)(2,1)}, u32[]{:S(2)}, u32[]{:S(2)}) collective-permute-start(bf16[1024,256]{1,0:T(8,128)(2,1)} %own_ref.1), channel_id=1, source_target_pairs={{0,0},{7,7},{1,2},{2,1},{3,4},{4,3},{5,6},{6,5},{8,8},{15,15},{9,1... | collective-permute-start | bytes 1572872 | tf_op jit(solution)/shard_map/ppermute | solution.py:31
  3.7 13.2 %collective-permute-start.4 = (bf16[1024,256]{1,0:T(8,128)(2,1)S(1)}, bf16[1024,256]{1,0:T(8,128)(2,1)}, u32[]{:S(2)}, u32[]{:S(2)}) collective-permute-start(bf16[1024,256]{1,0:T(8,128)(2,1)S(1)} %get-tuple-element.33.own_ref), channel_id=1, source_target_pairs={{0,0},{7,7},{1,2},{2,1},{3,4},{4,3},{5,6},{6,5},{8,8},{15,15},{9,1... | collective-permute-start | bytes 1572872 | tf_op jit(solution)/shard_map/ppermute | solution.py:31
  7.4 17.8 %collective-permute-start.3 = (bf16[1024,256]{1,0:T(8,128)(2,1)S(1)}, bf16[1024,256]{1,0:T(8,128)(2,1)S(1)}, u32[]{:S(2)}, u32[]{:S(2)}) collective-permute-start(bf16[1024,256]{1,0:T(8,128)(2,1)S(1)} %get-tuple-element.34.own_ref), channel_id=1, source_target_pairs={{0,0},{7,7},{1,2},{2,1},{3,4},{4,3},{5,6},{6,5},{8,8},{15,15},{9,1... | collective-permute-start | bytes 1572872 | tf_op jit(solution)/shard_map/ppermute | solution.py:31
  34.4 5.7 %collective-permute-start.15 = (bf16[256,256]{1,0:T(8,128)(2,1)S(1)}, bf16[256,256]{1,0:T(8,128)(2,1)S(1)}, u32[]{:S(2)}, u32[]{:S(2)}) collective-permute-start(bf16[256,256]{1,0:T(8,128)(2,1)S(1)} %get-tuple-element.32), channel_id=1, source_target_pairs={{0,8},{8,0},{16,24},{24,16},{1,9},{9,1},{17,25},{25,17},{2,10},{10... | collective-permute-start | bytes 393224 | tf_op jit(solution)/shard_map/ppermute | solution.py:36
  38.0 9.4 %collective-permute-start.5 = (bf16[1040,256]{1,0:T(8,128)(2,1)S(1)}, bf16[1040,256]{1,0:T(8,128)(2,1)S(1)}, u32[]{:S(2)}, u32[]{:S(2)}) collective-permute-start(bf16[1040,256]{1,0:T(8,128)(2,1)S(1)} %get-tuple-element.27), channel_id=1, source_target_pairs={{0,1},{1,0},{2,3},{3,2},{4,5},{5,4},{6,7},{7,6},{8,9},{9,8},{10,11... | collective-permute-start | bytes 1597448 | tf_op jit(solution)/shard_map/ppermute | solution.py:23
  40.2 5.0 %collective-permute-start.16 = (bf16[256,256]{1,0:T(8,128)(2,1)S(1)}, bf16[256,256]{1,0:T(8,128)(2,1)S(1)}, u32[]{:S(2)}, u32[]{:S(2)}) collective-permute-start(bf16[256,256]{1,0:T(8,128)(2,1)S(1)} %add_convert_fusion.1), channel_id=1, source_target_pairs={{0,16},{8,24},{16,0},{24,8},{1,17},{9,25},{17,1},{25,9},{2,18},{10... | collective-permute-start | bytes 393224 | tf_op jit(solution)/shard_map/ppermute | solution.py:36
  41.8 9.2 %collective-permute-start.6 = (bf16[784,256]{1,0:T(8,128)(2,1)S(1)}, bf16[784,256]{1,0:T(8,128)(2,1)S(1)}, u32[]{:S(2)}, u32[]{:S(2)}) collective-permute-start(bf16[784,256]{1,0:T(8,128)(2,1)S(1)} %get-tuple-element.23), channel_id=1, source_target_pairs={{0,0},{7,7},{1,2},{2,1},{3,4},{4,3},{5,6},{6,5},{8,8},{15,15},{9,1... | collective-permute-start | bytes 1204232 | tf_op jit(solution)/shard_map/ppermute | solution.py:31
  45.3 21.7 %collective-permute-start.17 = (bf16[256,256]{1,0:T(8,128)(2,1)S(1)}, bf16[256,256]{1,0:T(8,128)(2,1)S(1)}, u32[]{:S(2)}, u32[]{:S(2)}) collective-permute-start(bf16[256,256]{1,0:T(8,128)(2,1)S(1)} %add_convert_fusion), channel_id=1, source_target_pairs={{0,0},{7,7},{1,2},{2,1},{3,4},{4,3},{5,6},{6,5},{8,8},{15,15},{9,1... | collective-permute-start | bytes 393224 | tf_op jit(solution)/shard_map/ppermute | solution.py:31
  51.1 6.4 %collective-permute-start.7 = (bf16[256,256]{1,0:T(8,128)(2,1)S(1)}, bf16[256,256]{1,0:T(8,128)(2,1)S(1)}, u32[]{:S(2)}, u32[]{:S(2)}) collective-permute-start(bf16[256,256]{1,0:T(8,128)(2,1)S(1)} %get-tuple-element.35), channel_id=1, source_target_pairs={{0,8},{8,0},{16,24},{24,16},{1,9},{9,1},{17,25},{25,17},{2,10},{10... | collective-permute-start | bytes 393224 | tf_op jit(solution)/shard_map/ppermute | solution.py:36
  52.7 7.1 %collective-permute-start.11 = (bf16[256,256]{1,0:T(8,128)(2,1)S(1)}, bf16[256,256]{1,0:T(8,128)(2,1)S(1)}, u32[]{:S(2)}, u32[]{:S(2)}) collective-permute-start(bf16[256,256]{1,0:T(8,128)(2,1)S(1)} %get-tuple-element.36), channel_id=1, source_target_pairs={{0,8},{8,0},{16,24},{24,16},{1,9},{9,1},{17,25},{25,17},{2,10},{10... | collective-permute-start | bytes 393224 | tf_op jit(solution)/shard_map/ppermute | solution.py:36
  53.2 7.2 %collective-permute-start.9 = (bf16[256,256]{1,0:T(8,128)(2,1)S(1)}, bf16[256,256]{1,0:T(8,128)(2,1)S(1)}, u32[]{:S(2)}, u32[]{:S(2)}) collective-permute-start(bf16[256,256]{1,0:T(8,128)(2,1)S(1)} %get-tuple-element.37), channel_id=1, source_target_pairs={{0,16},{8,24},{16,0},{24,8},{1,17},{9,25},{17,1},{25,9},{2,18},{10... | collective-permute-start | bytes 393224 | tf_op jit(solution)/shard_map/ppermute | solution.py:36
  53.7 8.7 %collective-permute-start.13 = (bf16[256,256]{1,0:T(8,128)(2,1)S(1)}, bf16[256,256]{1,0:T(8,128)(2,1)S(1)}, u32[]{:S(2)}, u32[]{:S(2)}) collective-permute-start(bf16[256,256]{1,0:T(8,128)(2,1)S(1)} %add_convert_fusion.9), channel_id=1, source_target_pairs={{0,16},{8,24},{16,0},{24,8},{1,17},{9,25},{17,1},{25,9},{2,18},{10... | collective-permute-start | bytes 393224 | tf_op jit(solution)/shard_map/ppermute | solution.py:36
  57.6 7.6 %collective-permute-start.8 = (bf16[256,256]{1,0:T(8,128)(2,1)S(1)}, bf16[256,256]{1,0:T(8,128)(2,1)S(1)}, u32[]{:S(2)}, u32[]{:S(2)}) collective-permute-start(bf16[256,256]{1,0:T(8,128)(2,1)S(1)} %add_convert_fusion.7), channel_id=1, source_target_pairs={{0,16},{8,24},{16,0},{24,8},{1,17},{9,25},{17,1},{25,9},{2,18},{10... | collective-permute-start | bytes 393224 | tf_op jit(solution)/shard_map/ppermute | solution.py:36
  59.8 7.0 %collective-permute-start.12 = (bf16[256,256]{1,0:T(8,128)(2,1)S(1)}, bf16[256,256]{1,0:T(8,128)(2,1)S(1)}, u32[]{:S(2)}, u32[]{:S(2)}) collective-permute-start(bf16[256,256]{1,0:T(8,128)(2,1)S(1)} %add_convert_fusion.3), channel_id=1, source_target_pairs={{0,16},{8,24},{16,0},{24,8},{1,17},{9,25},{17,1},{25,9},{2,18},{10... | collective-permute-start | bytes 393224 | tf_op jit(solution)/shard_map/ppermute | solution.py:36
  60.4 6.5 %collective-permute-start.10 = (bf16[256,256]{1,0:T(8,128)(2,1)S(1)}, bf16[256,256]{1,0:T(8,128)(2,1)S(1)}, u32[]{:S(2)}, u32[]{:S(2)}) collective-permute-start(bf16[256,256]{1,0:T(8,128)(2,1)S(1)} %add_convert_fusion.5), channel_id=1, source_target_pairs={{0,8},{8,0},{16,24},{24,16},{1,9},{9,1},{17,25},{25,17},{2,10},{10... | collective-permute-start | bytes 393224 | tf_op jit(solution)/shard_map/ppermute | solution.py:36
  62.4 5.5 %collective-permute-start.14 = (bf16[256,256]{1,0:T(8,128)(2,1)S(1)}, bf16[256,256]{1,0:T(8,128)(2,1)S(1)}, u32[]{:S(2)}, u32[]{:S(2)}) collective-permute-start(bf16[256,256]{1,0:T(8,128)(2,1)S(1)} %add_convert_fusion.2), channel_id=1, source_target_pairs={{0,8},{8,0},{16,24},{24,16},{1,9},{9,1},{17,25},{25,17},{2,10},{10... | collective-permute-start | bytes 393224 | tf_op jit(solution)/shard_map/ppermute | solution.py:36

commit v4 on v3

--- a/solution.py
+++ b/solution.py
@@ -55,15 +55,21 @@
     )
 
 
+def read_codes(code_ref):
+    lights, members = code_ref.shape
+    return [[code_ref[g, j] for j in range(members)] for g in range(lights)]
+
+
 def columns(ref, half):
     return ref[:, pl.ds(pl.multiple_of(half * BLOCK, BLOCK), BLOCK)]
 
 
 def template_kernel(code_ref, own_ref, near_ref, far_ref, out_ref):
     lights, members = code_ref.shape
+    codes = read_codes(code_ref)
     for g in range(lights):
         for j in range(members):
-            code = code_ref[g, j]
+            code = codes[g][j]
             for place, ref in enumerate((own_ref, near_ref, far_ref)):
 
                 @pl.when(code // 2 == place)
@@ -94,6 +100,7 @@
     lights, members = code_ref.shape
     width = members * BLOCK
     frames = own_ref.shape[0]
+    codes = read_codes(code_ref)
     arrival = None
     if stage:
         staged_ref, arrived = stage
@@ -104,7 +111,7 @@
     def gather(sources):
         for g in range(lights):
             for i in range(members):
-                code = code_ref[g, i]
+                code = codes[g][i]
                 lo = g * width + i * BLOCK
                 for place, ref in sources:
 
@@ -141,14 +148,15 @@
     out_refs = refs[2 * subj_count : -1]
     lights, members = code_ref.shape
     width = members * BLOCK
+    codes = read_codes(code_ref)
     counts = []
     for p, place in enumerate(places):
         total = jnp.int32(0)
         for g in range(lights):
             pick = jnp.int32(0)
-            found = code_ref[g, 0] == place
+            found = codes[g][0] == place
             for j in range(1, members):
-                hit = code_ref[g, j] == place
+                hit = codes[g][j] == place
                 pick = jnp.where(hit, j, pick)
                 found = jnp.logical_or(found, hit)
             total = total + found.astype(jnp.int32)
@@ -192,6 +200,26 @@
             at += 1
 
 
+def finish_kernel(subjects, sent_ref, got_ref, cover_ref, *rest):
+    total = sent_ref[...].astype(jnp.float32) + got_ref[...].astype(jnp.float32)
+    rest[-1][...] = total / cover_ref[...] / subjects
+
+
+def finished(result, piece, pair, cover, subjects):
+    rows, cols = pair[0].shape
+    placed = [] if result is None else [result]
+    return pl.pallas_call(
+        functools.partial(finish_kernel, subjects),
+        out_shape=jax.ShapeDtypeStruct((rows * PIECES, cols), jnp.float32),
+        in_specs=[vmem()] * 3 + [pl.BlockSpec(memory_space=pl.ANY)] * len(placed),
+        out_specs=pl.BlockSpec((rows, cols), lambda i: (piece, 0)),
+        grid=(1,),
+        input_output_aliases={3: 0} if placed else {},
+        compiler_params=pltpu.CompilerParams(vmem_limit_bytes=LIMIT * MIB),
+        name="finish",
+    )(*pair, cover, *placed)
+
+
 def body(series, template, sl_blocks):
     subj_count, frames, width_dev = series.shape
     lights, members = sl_blocks.shape
@@ -255,47 +283,40 @@
             scratch=[pltpu.VMEM((len(places) * BLOCK, subj_count * lights * width), jnp.bfloat16)],
         )(code, *cols, *maps)
 
-    subj_size = lax.axis_size("subj")
-    distances = subject_distances(subj_size)
-    rows = frames // PIECES
-    late = frames - rows
     blocks = list(range(blk_dev))
-
-    def swapped(value, step, turn):
-        got = swap_subj(value, distances[(step + turn) % len(distances)])
-        return value.astype(jnp.float32) + got.astype(jnp.float32)
-
-    to_far, early_far = mapped([2 * blk_dev + b for b in blocks], ((late, rows),), (jnp.bfloat16,))
+    (to_far,) = mapped([2 * blk_dev + b for b in blocks], ((frames,),), (jnp.bfloat16,))
     from_far = swap_far(to_far)
     code, _ = lax.optimization_barrier((code, to_far))
     to_near, *own = mapped(
-        [blk_dev + b for b in blocks] + blocks, ((frames,), (rows,) * PIECES), (jnp.bfloat16, jnp.float32)
+        [blk_dev + b for b in blocks] + blocks, ((frames,), (frames // PIECES,) * PIECES), (jnp.bfloat16, jnp.float32)
     )
     from_near = swap_near(to_near)
-    early_own = own[-1] + from_near[late:frames].astype(jnp.float32)
-    early_own, from_near = lax.optimization_barrier((early_own.astype(jnp.bfloat16), from_near))
     keep = far_real.astype(jnp.float32)
 
-    def joined(mine, lo, far_lo, size):
-        near_rows = from_near[lo : lo + size].astype(jnp.float32)
-        return mine + near_rows + keep * from_far[far_lo : far_lo + size].astype(jnp.float32)
-
-    per_vertex = joined(own[0][rows : rows + 1], frames, late, 1)
-    parts = [joined(own[h][:rows], h * rows, h * rows, rows) for h in range(PIECES - 1)]
+    def joined(mine, lo, hi):
+        return mine + from_near[lo:hi].astype(jnp.float32) + keep * from_far[lo:hi].astype(jnp.float32)
+
+    rows = frames // PIECES
+    per_vertex = joined(own[0][rows : rows + 1], frames, frames + 1)
+    halves = [joined(own[h][:rows], h * rows, (h + 1) * rows) for h in range(PIECES)]
+    subj_size = lax.axis_size("subj")
+    distances = []
+    while 2 ** len(distances) < subj_size:
+        distances.append(2 ** len(distances))
+    pairs = []
     for step in range(len(distances)):
-        early_own = swapped(early_own.astype(jnp.bfloat16), step, 1)
-        early_far = swapped(early_far.astype(jnp.bfloat16), step, 0)
-        parts = [swapped(p.astype(jnp.bfloat16), step, h) for h, p in enumerate(parts)]
-    early_back = swap_far(early_far.astype(jnp.bfloat16))
-    parts.append(early_own + keep * early_back.astype(jnp.float32))
-    return jnp.concatenate(parts, axis=0) / per_vertex / (subj_count * subj_size)
-
-
-def subject_distances(size):
-    distances = []
-    while 2 ** len(distances) < size:
-        distances.append(2 ** len(distances))
-    return distances
+        pairs = []
+        for h in range(PIECES):
+            sent = halves[h].astype(jnp.bfloat16)
+            got = swap_subj(sent, distances[(step + h) % len(distances)])
+            halves[h] = sent.astype(jnp.float32) + got.astype(jnp.float32)
+            pairs.append((sent, got))
+    if not pairs:
+        return jnp.concatenate(halves, axis=0) / per_vertex / (subj_count * subj_size)
+    result = None
+    for h, pair in enumerate(pairs):
+        result = finished(result, h, pair, per_vertex, subj_count * subj_size)
+    return result
 
 
 def solution(mesh):

time: 69.6 us -> 63.6 us (0.914)
  the two profiles are of different devices: /device:TPU:8 before, /device:TPU:20 now
where the time goes in v4:
time: 63.6 us; the launch traced here: 63.1 us
  Pallas kernels  23.2 us (36%)
  waiting for transfers between devices  20.4 us (32%)
  starting transfers between devices  17.6 us (28%)
  local copies, waits for them, and re-layouts  1.28 us (2%)
    pallas_call x2, Pallas kernels, body(): call(functools.partial(polar_kernel, s), (jax.ShapeDtypeStruct((lights, w...  15 us
    ppermute x4, waiting for transfers between devices, swap_far(): return lax.ppermute(value, 'cortex', route)  13.9 us
    ppermute x4, starting transfers between devices, swap_far(): return lax.ppermute(value, 'cortex', route)  9.64 us
    ppermute x8, starting transfers between devices, swap_subj(): lax.ppermute(value, 'subj', [(i, i ^ distance) for i in range(count)])  7.07 us
    ppermute x8, waiting for transfers between devices, swap_subj(): lax.ppermute(value, 'subj', [(i, i ^ distance) for i in range(count)])  6.53 us
    pallas_call x2, Pallas kernels, mapped(): call(functools.partial(map_kernel, subj_count, places, splits), shapes, [...  3.13 us
    pallas_call x4, Pallas kernels, finished(): pl.pallas_call(functools.partial(finish_kernel, subjects), out_shape=jax....  3 us
    pallas_call x1, Pallas kernels, body(): call(template_kernel, jax.ShapeDtypeStruct((lights, width, frames), jnp.b...  2.12 us
  transfers between devices with their start and end apart: 15, of which 8 were waited for; matrix products, arithmetic and copies ran while one was open for 2% of the time, Pallas kernels for 19%

profile of v4, /device:TPU:20, one launch (start us, length us, event | category | flops | bytes accessed | tf_op | source)
XLA Modules:
  0.0 63.1 jit_solution(9908493756119747373)
XLA Ops:
  0.0 0.0 copy-start
  0.0 0.0 copy-start.1
  0.0 0.0 collective-permute-start.2
  0.0 0.5 collective-permute-start
  0.5 2.0 %collective-permute-start.1 = (bf16[1024,256]{1,0:T(8,128)(2,1)}, bf16[1024,256]{1,0:T(8,128)(2,1)}, u32[]{:S(2)}, u32[]{:S(2)}) collective-permute-start(bf16[1024,256]{1,0:T(8,128)(2,1)} %own_ref.1), channel_id=1, source_target_pairs={{0,0},{7,7},{1,2},{2,1},{3,4},{4,3},{5,6},{6,5},{8,8},{15,15},{9,1... | collective-permute-start | bytes 1572872 | tf_op jit(solution)/shard_map/ppermute | solution.py:31
  2.5 1.3 %slice_bitcast_fusion = (bf16[1024,256]{1,0:T(8,128)(2,1)S(1)}, bf16[1024,256]{1,0:T(8,128)(2,1)S(1)}) fusion(bf16[2,1024,256]{2,1,0:T(8,128)(2,1)} %param.3), kind=kLoop, calls=%fused_computation | loop fusion | bytes 2097152 | tf_op jit(solution)/shard_map/squeeze | solution.py:235
  3.8 3.5 %collective-permute-start.4 = (bf16[1024,256]{1,0:T(8,128)(2,1)S(1)}, bf16[1024,256]{1,0:T(8,128)(2,1)}, u32[]{:S(2)}, u32[]{:S(2)}) collective-permute-start(bf16[1024,256]{1,0:T(8,128)(2,1)S(1)} %get-tuple-element.29.own_ref), channel_id=1, source_target_pairs={{0,0},{7,7},{1,2},{2,1},{3,4},{4,3},{5,6},{6,5},{8,8},{15,15},{9,1... | collective-permute-start | bytes 1572872 | tf_op jit(solution)/shard_map/ppermute | solution.py:31
  7.4 2.0 %collective-permute-start.3 = (bf16[1024,256]{1,0:T(8,128)(2,1)S(1)}, bf16[1024,256]{1,0:T(8,128)(2,1)S(1)}, u32[]{:S(2)}, u32[]{:S(2)}) collective-permute-start(bf16[1024,256]{1,0:T(8,128)(2,1)S(1)} %get-tuple-element.30.own_ref), channel_id=1, source_target_pairs={{0,0},{7,7},{1,2},{2,1},{3,4},{4,3},{5,6},{6,5},{8,8},{15,15},{9,1... | collective-permute-start | bytes 1572872 | tf_op jit(solution)/shard_map/ppermute | solution.py:31
  9.4 0.0 copy-done.1
  9.4 0.0 collective-permute-done.near_ref
  9.5 1.9 %collective-permute-done.1.far_ref = bf16[1024,256]{1,0:T(8,128)(2,1)} collective-permute-done((bf16[1024,256]{1,0:T(8,128)(2,1)}, bf16[1024,256]{1,0:T(8,128)(2,1)}, u32[]{:S(2)}, u32[]{:S(2)}) %collective-permute-start.1) | collective-permute-done | bytes 524320 | tf_op jit(solution)/shard_map/ppermute | solution.py:31
  11.3 0.0 copy-done
  11.3 2.1 %shard_map.37.tmpl_ref = bf16[2,384,1024]{2,1,0:T(8,128)(2,1)S(1)} custom-call(s32[2,3]{1,0:T(2,128)S(1)} %fusion.1.code_ref, bf16[1024,256]{1,0:T(8,128)(2,1)S(1)} %copy-done, bf16[1024,256]{1,0:T(8,128)(2,1)} %collective-permute-done.near_ref, bf16[1024,256]{1,0:T(8,128)(2,1)} %collective-permute-done.1.far_ref), custom_call_target="tpu_custom_call" | custom-call | flops 1000000000 | bytes 1572864 | tf_op jit(solution)/shard_map/pallas_call | solution.py:246
  13.4 3.5 %collective-permute-done.4.far_ref = bf16[1024,256]{1,0:T(8,128)(2,1)} collective-permute-done((bf16[1024,256]{1,0:T(8,128)(2,1)S(1)}, bf16[1024,256]{1,0:T(8,128)(2,1)}, u32[]{:S(2)}, u32[]{:S(2)}) %collective-permute-start.4) | collective-permute-done | bytes 524320 | tf_op jit(solution)/shard_map/ppermute | solution.py:31
  16.9 0.0 collective-permute-done.2.near_ref
  16.9 7.7 %shard_map.39 = (bf16[2,384,384]{2,1,0:T(8,128)(2,1)S(1)}, bf16[1024,768]{1,0:T(8,128)(2,1)S(1)}) custom-call(s32[2,3]{1,0:T(2,128)S(1)} %fusion.1.code_ref, bf16[2,384,1024]{2,1,0:T(8,128)(2,1)S(1)} %shard_map.37.tmpl_ref, bf16[1024,256]{1,0:T(8,128)(2,1)S(1)} %get-tuple-element.29.own_ref, bf16[2,1024,256]{2,1,0:T(8,128)(2,1)S(1)} %collective-permute-done.2.near_ref, ...), custom_call_target="tpu_custom_call" | custom-call | flops 8000000000 | bytes 2162688 | tf_op jit(solution)/shard_map/pallas_call | solution.py:256
  24.7 0.0 collective-permute-done.3.far_ref
  24.7 7.2 %shard_map.38 = (bf16[2,384,384]{2,1,0:T(8,128)(2,1)S(1)}, bf16[1024,768]{1,0:T(8,128)(2,1)S(1)}) custom-call(s32[2,3]{1,0:T(2,128)S(1)} %fusion.1.code_ref, bf16[2,384,1024]{2,1,0:T(8,128)(2,1)S(1)} %shard_map.37.tmpl_ref, bf16[1024,256]{1,0:T(8,128)(2,1)S(1)} %get-tuple-element.30.own_ref, bf16[2,1024,256]{2,1,0:T(8,128)(2,1)S(1)} %collective-permute-done.2.near_ref, ...), custom_call_target="tpu_custom_call" | custom-call | flops 8000000000 | bytes 2162688 | tf_op jit(solution)/shard_map/pallas_call | solution.py:256
  32.0 1.1 %shard_map.40 = bf16[1040,256]{1,0:T(8,128)(2,1)S(1)} custom-call(s32[2,3]{1,0:T(2,128)S(1)} %fusion.1.code_ref, bf16[1024,768]{1,0:T(8,128)(2,1)S(1)} %get-tuple-element.15.refs_0_, bf16[1024,768]{1,0:T(8,128)(2,1)S(1)} %get-tuple-element.16.refs_1_, bf16[2,384,384]{2,1,0:T(8,128)(2,1)S(1)} %get-tuple-element.17.refs_2_, ...), custom_call_target="tpu_custom_call" | custom-call | flops 800000000 | bytes 532480 | tf_op jit(solution)/shard_map/pallas_call | solution.py:277
  33.1 2.0 %shard_map.41 = (bf16[1040,256]{1,0:T(8,128)(2,1)S(1)}, f32[272,256]{1,0:T(8,128)S(1)}, f32[256,256]{1,0:T(8,128)S(1)}, f32[256,256]{1,0:T(8,128)S(1)}, f32[256,256]{1,0:T(8,128)S(1)}) custom-call(s32[2,3]{1,0:T(2,128)S(1)} %fusion.1.code_ref, bf16[1024,768]{1,0:T(8,128)(2,1)S(1)} %get-tuple-element.15.refs_0_, ...), custom_call_target="tpu_custom_call" | custom-call | flops 1600000000 | bytes 1597440 | tf_op jit(solution)/shard_map/pallas_call | solution.py:277
  35.1 0.4 collective-permute-start.5
  35.5 2.1 %collective-permute-start.6 = (bf16[1040,256]{1,0:T(8,128)(2,1)S(1)}, bf16[1040,256]{1,0:T(8,128)(2,1)S(1)}, u32[]{:S(2)}, u32[]{:S(2)}) collective-permute-start(bf16[1040,256]{1,0:T(8,128)(2,1)S(1)} %shard_map.40), channel_id=1, source_target_pairs={{0,0},{7,7},{1,2},{2,1},{3,4},{4,3},{5,6},{6,5},{8,8},{15,15},{9,1... | collective-permute-start | bytes 1597448 | tf_op jit(solution)/shard_map/ppermute | solution.py:31
  37.6 0.0 collective-permute-done.5
  37.6 8.5 %collective-permute-done.6 = bf16[1040,256]{1,0:T(8,128)(2,1)S(1)} collective-permute-done((bf16[1040,256]{1,0:T(8,128)(2,1)S(1)}, bf16[1040,256]{1,0:T(8,128)(2,1)S(1)}, u32[]{:S(2)}, u32[]{:S(2)}) %collective-permute-start.6) | collective-permute-done | bytes 532512 | tf_op jit(solution)/shard_map/ppermute | solution.py:31
  46.1 0.2 add_convert_fusion.1
  46.3 1.6 %collective-permute-start.13 = (bf16[256,256]{1,0:T(8,128)(2,1)S(1)}, bf16[256,256]{1,0:T(8,128)(2,1)S(1)}, u32[]{:S(2)}, u32[]{:S(2)}) collective-permute-start(bf16[256,256]{1,0:T(8,128)(2,1)S(1)} %get-tuple-element.25), channel_id=1, source_target_pairs={{0,8},{8,0},{16,24},{24,16},{1,9},{9,1},{17,25},{25,17},{2,10},{10... | collective-permute-start | bytes 393224 | tf_op jit(solution)/shard_map/ppermute | solution.py:36
  47.9 0.5 collective-permute-start.11
  48.4 0.5 collective-permute-start.9
  48.9 1.5 %collective-permute-start.7 = (bf16[256,256]{1,0:T(8,128)(2,1)S(1)}, bf16[256,256]{1,0:T(8,128)(2,1)S(1)}, u32[]{:S(2)}, u32[]{:S(2)}) collective-permute-start(bf16[256,256]{1,0:T(8,128)(2,1)S(1)} %get-tuple-element.28), channel_id=1, source_target_pairs={{0,16},{8,24},{16,0},{24,8},{1,17},{9,25},{17,1},{25,9},{2,18},{10... | collective-permute-start | bytes 393224 | tf_op jit(solution)/shard_map/ppermute | solution.py:36
  50.5 2.3 %collective-permute-done.13 = bf16[256,256]{1,0:T(8,128)(2,1)S(1)} collective-permute-done((bf16[256,256]{1,0:T(8,128)(2,1)S(1)}, bf16[256,256]{1,0:T(8,128)(2,1)S(1)}, u32[]{:S(2)}, u32[]{:S(2)}) %collective-permute-start.13) | collective-permute-done | bytes 131104 | tf_op jit(solution)/shard_map/ppermute | solution.py:36
  52.8 0.1 collective-permute-start.14
  52.9 1.3 %collective-permute-done.11 = bf16[256,256]{1,0:T(8,128)(2,1)S(1)} collective-permute-done((bf16[256,256]{1,0:T(8,128)(2,1)S(1)}, bf16[256,256]{1,0:T(8,128)(2,1)S(1)}, u32[]{:S(2)}, u32[]{:S(2)}) %collective-permute-start.11) | collective-permute-done | bytes 131104 | tf_op jit(solution)/shard_map/ppermute | solution.py:36
  54.3 0.7 %collective-permute-start.12 = (bf16[256,256]{1,0:T(8,128)(2,1)S(1)}, bf16[256,256]{1,0:T(8,128)(2,1)S(1)}, u32[]{:S(2)}, u32[]{:S(2)}) collective-permute-start(bf16[256,256]{1,0:T(8,128)(2,1)S(1)} %add_convert_fusion.2.sent_ref), channel_id=1, source_target_pairs={{0,8},{8,0},{16,24},{24,16},{1,9},{9,1},{17,25},{25,17},{2,10},{10... | collective-permute-start | bytes 393224 | tf_op jit(solution)/shard_map/ppermute | solution.py:36
  55.0 0.0 collective-permute-done.9
  55.0 1.6 %collective-permute-start.10 = (bf16[256,256]{1,0:T(8,128)(2,1)S(1)}, bf16[256,256]{1,0:T(8,128)(2,1)S(1)}, u32[]{:S(2)}, u32[]{:S(2)}) collective-permute-start(bf16[256,256]{1,0:T(8,128)(2,1)S(1)} %add_convert_fusion.4.sent_ref), channel_id=1, source_target_pairs={{0,16},{8,24},{16,0},{24,8},{1,17},{9,25},{17,1},{25,9},{2,18},{10... | collective-permute-start | bytes 393224 | tf_op jit(solution)/shard_map/ppermute | solution.py:36
  56.6 0.5 collective-permute-done.7
  57.1 0.6 collective-permute-start.8
  57.7 2.2 %collective-permute-done.14.got_ref = bf16[256,256]{1,0:T(8,128)(2,1)S(1)} collective-permute-done((bf16[256,256]{1,0:T(8,128)(2,1)S(1)}, bf16[256,256]{1,0:T(8,128)(2,1)S(1)}, u32[]{:S(2)}, u32[]{:S(2)}) %collective-permute-start.14) | collective-permute-done | bytes 131104 | tf_op jit(solution)/shard_map/ppermute | solution.py:36
  59.9 0.7 %finish.4.rest_0_ = f32[1024,256]{1,0:T(8,128)} custom-call(bf16[256,256]{1,0:T(8,128)(2,1)S(1)} %add_convert_fusion.sent_ref, bf16[256,256]{1,0:T(8,128)(2,1)S(1)} %collective-permute-done.14.got_ref, f32[1,256]{1,0:T(1,128)S(1)} %fusion.3.cover_ref), custom_call_target="tpu_custom_call" | custom-call | tf_op jit(solution)/shard_map/finish/pallas_call | solution.py:211
  60.6 0.0 collective-permute-done.12.got_ref
  60.6 0.8 %finish.5.rest_0_ = f32[1024,256]{1,0:T(8,128)} custom-call(bf16[256,256]{1,0:T(8,128)(2,1)S(1)} %add_convert_fusion.2.sent_ref, bf16[256,256]{1,0:T(8,128)(2,1)S(1)} %collective-permute-done.12.got_ref, f32[1,256]{1,0:T(1,128)S(1)} %fusion.3.cover_ref, f32[1024,256]{1,0:T(8,128)} %finish.4.rest_0_), custom_call_target="tpu_custom_call", output_to_operand_aliasing={{}: (3, {})} | custom-call | tf_op jit(solution)/shard_map/finish/pallas_call | solution.py:211
  61.4 0.2 collective-permute-done.10.got_ref
  61.6 0.7 %finish.6.rest_0_ = f32[1024,256]{1,0:T(8,128)} custom-call(bf16[256,256]{1,0:T(8,128)(2,1)S(1)} %add_convert_fusion.4.sent_ref, bf16[256,256]{1,0:T(8,128)(2,1)S(1)} %collective-permute-done.10.got_ref, f32[1,256]{1,0:T(1,128)S(1)} %fusion.3.cover_ref, f32[1024,256]{1,0:T(8,128)} %finish.5.rest_0_), custom_call_target="tpu_custom_call", output_to_operand_aliasing={{}: (3, {})} | custom-call | tf_op jit(solution)/shard_map/finish/pallas_call | solution.py:211
  62.4 0.0 collective-permute-done.8.got_ref
  62.4 0.8 %finish.7 = f32[1024,256]{1,0:T(8,128)} custom-call(bf16[256,256]{1,0:T(8,128)(2,1)S(1)} %add_convert_fusion.6.sent_ref, bf16[256,256]{1,0:T(8,128)(2,1)S(1)} %collective-permute-done.8.got_ref, f32[1,256]{1,0:T(1,128)S(1)} %fusion.3.cover_ref, f32[1024,256]{1,0:T(8,128)} %finish.6.rest_0_), custom_call_target="tpu_custom_call", output_to_operand_aliasing={{}: (3, {})} | custom-call | tf_op jit(solution)/shard_map/finish/pallas_call | solution.py:211
  (6 shorter events, 0.2 us)
Async XLA Ops:
  0.0 11.3 %copy-start = (bf16[1024,256]{1,0:T(8,128)(2,1)S(1)}, bf16[1024,256]{1,0:T(8,128)(2,1)}, u32[]{:S(2)}) copy-start(bf16[1024,256]{1,0:T(8,128)(2,1)} %own_ref.1) | copy-start | bytes 1572868
  0.0 9.4 %copy-start.1 = (s32[2,3]{1,0:T(2,128)S(1)}, s32[2,3]{1,0:T(2,128)}, u32[]{:S(2)}) copy-start(s32[2,3]{1,0:T(2,128)} %param.5) | copy-start | bytes 76
  0.0 16.9 %collective-permute-start.2 = (bf16[2,1024,256]{2,1,0:T(8,128)(2,1)}, bf16[2,1024,256]{2,1,0:T(8,128)(2,1)S(1)}, u32[]{:S(2)}, u32[]{:S(2)}) collective-permute-start(bf16[2,1024,256]{2,1,0:T(8,128)(2,1)} %param.3), channel_id=1, source_target_pairs={{0,1},{1,0},{2,3},{3,2},{4,5},{5,4},{6,7},{7,6},{8,9},{9,8},{10,11... | collective-permute-start | bytes 3145736 | tf_op jit(solution)/shard_map/ppermute | solution.py:23
  0.0 9.4 %collective-permute-start = (bf16[1024,256]{1,0:T(8,128)(2,1)}, bf16[1024,256]{1,0:T(8,128)(2,1)}, u32[]{:S(2)}, u32[]{:S(2)}) collective-permute-start(bf16[1024,256]{1,0:T(8,128)(2,1)} %own_ref.1), channel_id=1, source_target_pairs={{0,1},{1,0},{2,3},{3,2},{4,5},{5,4},{6,7},{7,6},{8,9},{9,8},{10,11... | collective-permute-start | bytes 1572872 | tf_op jit(solution)/shard_map/ppermute | solution.py:23
  0.5 10.8 %collective-permute-start.1 = (bf16[1024,256]{1,0:T(8,128)(2,1)}, bf16[1024,256]{1,0:T(8,128)(2,1)}, u32[]{:S(2)}, u32[]{:S(2)}) collective-permute-start(bf16[1024,256]{1,0:T(8,128)(2,1)} %own_ref.1), channel_id=1, source_target_pairs={{0,0},{7,7},{1,2},{2,1},{3,4},{4,3},{5,6},{6,5},{8,8},{15,15},{9,1... | collective-permute-start | bytes 1572872 | tf_op jit(solution)/shard_map/ppermute | solution.py:31
  3.8 13.1 %collective-permute-start.4 = (bf16[1024,256]{1,0:T(8,128)(2,1)S(1)}, bf16[1024,256]{1,0:T(8,128)(2,1)}, u32[]{:S(2)}, u32[]{:S(2)}) collective-permute-start(bf16[1024,256]{1,0:T(8,128)(2,1)S(1)} %get-tuple-element.29.own_ref), channel_id=1, source_target_pairs={{0,0},{7,7},{1,2},{2,1},{3,4},{4,3},{5,6},{6,5},{8,8},{15,15},{9,1... | collective-permute-start | bytes 1572872 | tf_op jit(solution)/shard_map/ppermute | solution.py:31
  7.4 17.3 %collective-permute-start.3 = (bf16[1024,256]{1,0:T(8,128)(2,1)S(1)}, bf16[1024,256]{1,0:T(8,128)(2,1)S(1)}, u32[]{:S(2)}, u32[]{:S(2)}) collective-permute-start(bf16[1024,256]{1,0:T(8,128)(2,1)S(1)} %get-tuple-element.30.own_ref), channel_id=1, source_target_pairs={{0,0},{7,7},{1,2},{2,1},{3,4},{4,3},{5,6},{6,5},{8,8},{15,15},{9,1... | collective-permute-start | bytes 1572872 | tf_op jit(solution)/shard_map/ppermute | solution.py:31
  35.1 2.5 %collective-permute-start.5 = (bf16[1040,256]{1,0:T(8,128)(2,1)S(1)}, bf16[1040,256]{1,0:T(8,128)(2,1)S(1)}, u32[]{:S(2)}, u32[]{:S(2)}) collective-permute-start(bf16[1040,256]{1,0:T(8,128)(2,1)S(1)} %get-tuple-element.21), channel_id=1, source_target_pairs={{0,1},{1,0},{2,3},{3,2},{4,5},{5,4},{6,7},{7,6},{8,9},{9,8},{10,11... | collective-permute-start | bytes 1597448 | tf_op jit(solution)/shard_map/ppermute | solution.py:23
  35.5 10.6 %collective-permute-start.6 = (bf16[1040,256]{1,0:T(8,128)(2,1)S(1)}, bf16[1040,256]{1,0:T(8,128)(2,1)S(1)}, u32[]{:S(2)}, u32[]{:S(2)}) collective-permute-start(bf16[1040,256]{1,0:T(8,128)(2,1)S(1)} %shard_map.40), channel_id=1, source_target_pairs={{0,0},{7,7},{1,2},{2,1},{3,4},{4,3},{5,6},{6,5},{8,8},{15,15},{9,1... | collective-permute-start | bytes 1597448 | tf_op jit(solution)/shard_map/ppermute | solution.py:31
  46.3 6.4 %collective-permute-start.13 = (bf16[256,256]{1,0:T(8,128)(2,1)S(1)}, bf16[256,256]{1,0:T(8,128)(2,1)S(1)}, u32[]{:S(2)}, u32[]{:S(2)}) collective-permute-start(bf16[256,256]{1,0:T(8,128)(2,1)S(1)} %get-tuple-element.25), channel_id=1, source_target_pairs={{0,8},{8,0},{16,24},{24,16},{1,9},{9,1},{17,25},{25,17},{2,10},{10... | collective-permute-start | bytes 393224 | tf_op jit(solution)/shard_map/ppermute | solution.py:36
  47.9 6.4 %collective-permute-start.11 = (bf16[256,256]{1,0:T(8,128)(2,1)S(1)}, bf16[256,256]{1,0:T(8,128)(2,1)S(1)}, u32[]{:S(2)}, u32[]{:S(2)}) collective-permute-start(bf16[256,256]{1,0:T(8,128)(2,1)S(1)} %get-tuple-element.26), channel_id=1, source_target_pairs={{0,16},{8,24},{16,0},{24,8},{1,17},{9,25},{17,1},{25,9},{2,18},{10... | collective-permute-start | bytes 393224 | tf_op jit(solution)/shard_map/ppermute | solution.py:36
  48.4 6.6 %collective-permute-start.9 = (bf16[256,256]{1,0:T(8,128)(2,1)S(1)}, bf16[256,256]{1,0:T(8,128)(2,1)S(1)}, u32[]{:S(2)}, u32[]{:S(2)}) collective-permute-start(bf16[256,256]{1,0:T(8,128)(2,1)S(1)} %get-tuple-element.27), channel_id=1, source_target_pairs={{0,8},{8,0},{16,24},{24,16},{1,9},{9,1},{17,25},{25,17},{2,10},{10... | collective-permute-start | bytes 393224 | tf_op jit(solution)/shard_map/ppermute | solution.py:36
  48.9 8.1 %collective-permute-start.7 = (bf16[256,256]{1,0:T(8,128)(2,1)S(1)}, bf16[256,256]{1,0:T(8,128)(2,1)S(1)}, u32[]{:S(2)}, u32[]{:S(2)}) collective-permute-start(bf16[256,256]{1,0:T(8,128)(2,1)S(1)} %get-tuple-element.28), channel_id=1, source_target_pairs={{0,16},{8,24},{16,0},{24,8},{1,17},{9,25},{17,1},{25,9},{2,18},{10... | collective-permute-start | bytes 393224 | tf_op jit(solution)/shard_map/ppermute | solution.py:36
  52.8 7.1 %collective-permute-start.14 = (bf16[256,256]{1,0:T(8,128)(2,1)S(1)}, bf16[256,256]{1,0:T(8,128)(2,1)S(1)}, u32[]{:S(2)}, u32[]{:S(2)}) collective-permute-start(bf16[256,256]{1,0:T(8,128)(2,1)S(1)} %add_convert_fusion.sent_ref), channel_id=1, source_target_pairs={{0,16},{8,24},{16,0},{24,8},{1,17},{9,25},{17,1},{25,9},{2,18},{10... | collective-permute-start | bytes 393224 | tf_op jit(solution)/shard_map/ppermute | solution.py:36
  54.3 6.3 %collective-permute-start.12 = (bf16[256,256]{1,0:T(8,128)(2,1)S(1)}, bf16[256,256]{1,0:T(8,128)(2,1)S(1)}, u32[]{:S(2)}, u32[]{:S(2)}) collective-permute-start(bf16[256,256]{1,0:T(8,128)(2,1)S(1)} %add_convert_fusion.2.sent_ref), channel_id=1, source_target_pairs={{0,8},{8,0},{16,24},{24,16},{1,9},{9,1},{17,25},{25,17},{2,10},{10... | collective-permute-start | bytes 393224 | tf_op jit(solution)/shard_map/ppermute | solution.py:36
  55.0 6.6 %collective-permute-start.10 = (bf16[256,256]{1,0:T(8,128)(2,1)S(1)}, bf16[256,256]{1,0:T(8,128)(2,1)S(1)}, u32[]{:S(2)}, u32[]{:S(2)}) collective-permute-start(bf16[256,256]{1,0:T(8,128)(2,1)S(1)} %add_convert_fusion.4.sent_ref), channel_id=1, source_target_pairs={{0,16},{8,24},{16,0},{24,8},{1,17},{9,25},{17,1},{25,9},{2,18},{10... | collective-permute-start | bytes 393224 | tf_op jit(solution)/shard_map/ppermute | solution.py:36
  57.1 5.2 %collective-permute-start.8 = (bf16[256,256]{1,0:T(8,128)(2,1)S(1)}, bf16[256,256]{1,0:T(8,128)(2,1)S(1)}, u32[]{:S(2)}, u32[]{:S(2)}) collective-permute-start(bf16[256,256]{1,0:T(8,128)(2,1)S(1)} %add_convert_fusion.6.sent_ref), channel_id=1, source_target_pairs={{0,8},{8,0},{16,24},{24,16},{1,9},{9,1},{17,25},{25,17},{2,10},{10... | collective-permute-start | bytes 393224 | tf_op jit(solution)/shard_map/ppermute | solution.py:36

commit v5 on v4

--- a/solution.py
+++ b/solution.py
@@ -96,33 +96,20 @@
         next_ref[g] = (1.5 * now.astype(jnp.float32) - 0.5 * product).astype(jnp.bfloat16)
 
 
-def polar_kernel(subject, code_ref, tmpl_ref, own_ref, near_ref, far_ref, map_ref, cols_ref, odd_ref, gram_ref, *stage):
+def polar_kernel(subject, code_ref, tmpl_ref, own_ref, near_ref, far_ref, map_ref, cols_ref, odd_ref, gram_ref):
     lights, members = code_ref.shape
     width = members * BLOCK
     frames = own_ref.shape[0]
     codes = read_codes(code_ref)
-    arrival = None
-    if stage:
-        staged_ref, arrived = stage
-        arrival = pltpu.make_async_copy(far_ref, staged_ref, arrived)
-        arrival.start()
-        far_ref = staged_ref
-
-    def gather(sources):
-        for g in range(lights):
-            for i in range(members):
-                code = codes[g][i]
-                lo = g * width + i * BLOCK
-                for place, ref in sources:
-
-                    @pl.when(code // 2 == place)
-                    def _():
-                        cols_ref[:, lo : lo + BLOCK] = columns(ref, code % 2)
-
-    gather(((0, own_ref), (1, near_ref.at[subject])))
-    if arrival is not None:
-        arrival.wait()
-    gather(((2, far_ref),))
+    for g in range(lights):
+        for i in range(members):
+            code = codes[g][i]
+            lo = g * width + i * BLOCK
+            for place, ref in enumerate((own_ref, near_ref.at[subject], far_ref)):
+
+                @pl.when(code // 2 == place)
+                def _():
+                    cols_ref[:, lo : lo + BLOCK] = columns(ref, code % 2)
 
     first_ref = map_ref if NS_STEPS % 2 == 0 else odd_ref
     row = lax.broadcasted_iota(jnp.int32, (width, width), 0)
@@ -200,24 +187,33 @@
             at += 1
 
 
-def finish_kernel(subjects, sent_ref, got_ref, cover_ref, *rest):
-    total = sent_ref[...].astype(jnp.float32) + got_ref[...].astype(jnp.float32)
-    rest[-1][...] = total / cover_ref[...] / subjects
-
-
-def finished(result, piece, pair, cover, subjects):
-    rows, cols = pair[0].shape
-    placed = [] if result is None else [result]
+def finish_kernel(subjects, *refs):
+    *pairs, cover_ref, out_ref, tile_ref, sems = refs
+    rows = pairs[0].shape[0]
+    scale = 1.0 / (cover_ref[...] * subjects)
+    copies = []
+    for h in range(len(pairs) // 2):
+        total = pairs[2 * h][...].astype(jnp.float32) + pairs[2 * h + 1][...].astype(jnp.float32)
+        here = pl.ds(h * rows, rows)
+        tile_ref[here, :] = total * scale
+        copies.append(pltpu.make_async_copy(tile_ref.at[here], out_ref.at[here], sems.at[h]))
+        copies[-1].start()
+    for copy in copies:
+        copy.wait()
+
+
+def finished(pairs, cover, subjects):
+    rows, cols = pairs[0][0].shape
+    count = len(pairs)
     return pl.pallas_call(
         functools.partial(finish_kernel, subjects),
-        out_shape=jax.ShapeDtypeStruct((rows * PIECES, cols), jnp.float32),
-        in_specs=[vmem()] * 3 + [pl.BlockSpec(memory_space=pl.ANY)] * len(placed),
-        out_specs=pl.BlockSpec((rows, cols), lambda i: (piece, 0)),
-        grid=(1,),
-        input_output_aliases={3: 0} if placed else {},
+        out_shape=jax.ShapeDtypeStruct((rows * count, cols), jnp.float32),
+        in_specs=[vmem()] * (2 * count + 1),
+        out_specs=pl.BlockSpec(memory_space=pl.ANY),
+        scratch_shapes=[pltpu.VMEM((rows * count, cols), jnp.float32), pltpu.SemaphoreType.DMA((count,))],
         compiler_params=pltpu.CompilerParams(vmem_limit_bytes=LIMIT * MIB),
         name="finish",
-    )(*pair, cover, *placed)
+    )(*[value for pair in pairs for value in pair], cover)
 
 
 def body(series, template, sl_blocks):
@@ -230,6 +226,13 @@
     odd = position % 2
     far_real = jnp.logical_and(position + 2 * odd - 1 >= 0, position + 2 * odd - 1 < count)
 
+    window = sl_blocks - (position - 1) * blk_dev
+    side = window // blk_dev
+    place = jnp.where(side == 1, 0, jnp.where((side == 2) == (odd == 1), 2, 1))
+    code = (place * blk_dev + window % blk_dev).astype(jnp.int32)
+
+    code, template, series = lax.optimization_barrier((code, template, series))
+
     tmpl_far = swap_far(template)
     tmpl_near = swap_near(template)
     parts = [series[s] for s in range(subj_count)]
@@ -237,11 +240,6 @@
     for part in parts:
         far.append(swap_far(part))
     near = swap_near(series)
-
-    window = sl_blocks - (position - 1) * blk_dev
-    side = window // blk_dev
-    place = jnp.where(side == 1, 0, jnp.where((side == 2) == (odd == 1), 2, 1))
-    code = (place * blk_dev + window % blk_dev).astype(jnp.int32)
 
     tmpl_rows = call(
         template_kernel,
@@ -259,11 +257,10 @@
                 jax.ShapeDtypeStruct((lights, width, width), jnp.bfloat16),
                 jax.ShapeDtypeStruct((frames, lights * width), jnp.bfloat16),
             ),
-            [vmem()] * 4 + [pl.BlockSpec(memory_space=pl.ANY) if s > 0 else vmem()],
+            [vmem()] * 5,
             flops=8 * 10**9,
             limit=LIMIT,
-            scratch=[pltpu.VMEM((lights, width, width), jnp.bfloat16)] * 2
-            + ([pltpu.VMEM((frames, width_dev), jnp.bfloat16), pltpu.SemaphoreType.DMA] if s > 0 else []),
+            scratch=[pltpu.VMEM((lights, width, width), jnp.bfloat16)] * 2,
         )(code, tmpl_rows, parts[s], near, far[s])
         maps.append(polar)
         cols.append(gathered)
@@ -313,10 +310,7 @@
             pairs.append((sent, got))
     if not pairs:
         return jnp.concatenate(halves, axis=0) / per_vertex / (subj_count * subj_size)
-    result = None
-    for h, pair in enumerate(pairs):
-        result = finished(result, h, pair, per_vertex, subj_count * subj_size)
-    return result
+    return finished(pairs, per_vertex, subj_count * subj_size)
 
 
 def solution(mesh):

time: 63.6 us -> 63.6 us (level)
  the two profiles are of different devices: /device:TPU:20 before, /device:TPU:16 now
where the time goes in v5:
time: 63.6 us; the launch traced here: 63.4 us
  starting transfers between devices  21.8 us (34%)
  waiting for transfers between devices  19.5 us (31%)
  Pallas kernels  19.4 us (31%)
  local copies, waits for them, and re-layouts  1.27 us (2%)
  other arithmetic  1.14 us (2%)
    pallas_call x2, Pallas kernels, body(): call(functools.partial(polar_kernel, s), (jax.ShapeDtypeStruct((lights, w...  14.3 us
    ppermute x4, waiting for transfers between devices, swap_far(): return lax.ppermute(value, 'cortex', route)  13.4 us
    ppermute x4, starting transfers between devices, swap_far(): return lax.ppermute(value, 'cortex', route)  10 us
    ppermute x8, starting transfers between devices, swap_subj(): lax.ppermute(value, 'subj', [(i, i ^ distance) for i in range(count)])  9.66 us
    ppermute x8, waiting for transfers between devices, swap_subj(): lax.ppermute(value, 'subj', [(i, i ^ distance) for i in range(count)])  6.06 us
    pallas_call x2, Pallas kernels, mapped(): call(functools.partial(map_kernel, subj_count, places, splits), shapes, [...  3.13 us
    ppermute x3, starting transfers between devices, swap_near(): return lax.ppermute(value, 'cortex', [(i, i ^ 1) for i in range(count)])  2.13 us
  transfers between devices with their start and end apart: 15, of which 9 were waited for; matrix products, arithmetic and copies ran while one was open for 2% of the time, Pallas kernels for 13%

profile of v5, /device:TPU:16, one launch (start us, length us, event | category | flops | bytes accessed | tf_op | source)
XLA Modules:
  0.0 63.4 jit_solution(10663089040813183143)
XLA Ops:
  0.0 0.0 copy-start
  0.0 0.8 %fusion.1.code_ref = s32[2,3]{1,0:T(2,128)S(1)} fusion(s32[2,3]{1,0:T(2,128)} %param.5, pred[]{:T(512)S(6)} %eq.21, s32[]{:T(128)S(6)} %mul.34), kind=kLoop, calls=%fused_computation.18 | loop fusion | flops 162 | bytes 53 | tf_op jit(solution)/shard_map/add | solution.py:232
  0.8 0.1 collective-permute-start.2
  0.8 2.4 %collective-permute-start.1 = (bf16[1024,256]{1,0:T(8,128)(2,1)}, bf16[1024,256]{1,0:T(8,128)(2,1)S(1)}, u32[]{:S(2)}, u32[]{:S(2)}) collective-permute-start(bf16[1024,256]{1,0:T(8,128)(2,1)} %own_ref), channel_id=1, source_target_pairs={{0,0},{7,7},{1,2},{2,1},{3,4},{4,3},{5,6},{6,5},{8,8},{15,15},{9,1... | collective-permute-start | bytes 1572872 | tf_op jit(solution)/shard_map/ppermute | solution.py:31
  3.3 1.2 %collective-permute-start = (bf16[1024,256]{1,0:T(8,128)(2,1)}, bf16[1024,256]{1,0:T(8,128)(2,1)S(1)}, u32[]{:S(2)}, u32[]{:S(2)}) collective-permute-start(bf16[1024,256]{1,0:T(8,128)(2,1)} %own_ref), channel_id=1, source_target_pairs={{0,1},{1,0},{2,3},{3,2},{4,5},{5,4},{6,7},{7,6},{8,9},{9,8},{10,11... | collective-permute-start | bytes 1572872 | tf_op jit(solution)/shard_map/ppermute | solution.py:23
  4.5 1.3 %slice_bitcast_fusion = (bf16[1024,256]{1,0:T(8,128)(2,1)S(1)}, bf16[1024,256]{1,0:T(8,128)(2,1)S(1)}) fusion(bf16[2,1024,256]{2,1,0:T(8,128)(2,1)} %param.3), kind=kLoop, calls=%fused_computation | loop fusion | bytes 2097152 | tf_op jit(solution)/shard_map/squeeze | solution.py:238
  5.8 2.0 %collective-permute-start.4 = (bf16[1024,256]{1,0:T(8,128)(2,1)S(1)}, bf16[1024,256]{1,0:T(8,128)(2,1)S(1)}, u32[]{:S(2)}, u32[]{:S(2)}) collective-permute-start(bf16[1024,256]{1,0:T(8,128)(2,1)S(1)} %get-tuple-element.35.own_ref), channel_id=1, source_target_pairs={{0,0},{7,7},{1,2},{2,1},{3,4},{4,3},{5,6},{6,5},{8,8},{15,15},{9,1... | collective-permute-start | bytes 1572872 | tf_op jit(solution)/shard_map/ppermute | solution.py:31
  7.8 3.6 %collective-permute-start.3 = (bf16[1024,256]{1,0:T(8,128)(2,1)S(1)}, bf16[1024,256]{1,0:T(8,128)(2,1)S(1)}, u32[]{:S(2)}, u32[]{:S(2)}) collective-permute-start(bf16[1024,256]{1,0:T(8,128)(2,1)S(1)} %get-tuple-element.36.own_ref), channel_id=1, source_target_pairs={{0,0},{7,7},{1,2},{2,1},{3,4},{4,3},{5,6},{6,5},{8,8},{15,15},{9,1... | collective-permute-start | bytes 1572872 | tf_op jit(solution)/shard_map/ppermute | solution.py:31
  11.4 0.2 collective-permute-done.1.far_ref
  11.6 0.0 collective-permute-done.near_ref
  11.6 0.0 copy-done
  11.6 0.9 %shard_map.37.tmpl_ref = bf16[2,384,1024]{2,1,0:T(8,128)(2,1)S(1)} custom-call(s32[2,3]{1,0:T(2,128)S(1)} %fusion.1.code_ref, bf16[1024,256]{1,0:T(8,128)(2,1)S(1)} %copy-done, bf16[1024,256]{1,0:T(8,128)(2,1)S(1)} %collective-permute-done.near_ref, bf16[1024,256]{1,0:T(8,128)(2,1)S(1)} %collective-permute-done.1.far_ref), custom_call_target="tpu_custom_call" | custom-call | flops 1000000000 | bytes 1572864 | tf_op jit(solution)/shard_map/pallas_call | solution.py:244
  12.5 4.7 %collective-permute-done.4.far_ref = bf16[1024,256]{1,0:T(8,128)(2,1)S(1)} collective-permute-done((bf16[1024,256]{1,0:T(8,128)(2,1)S(1)}, bf16[1024,256]{1,0:T(8,128)(2,1)S(1)}, u32[]{:S(2)}, u32[]{:S(2)}) %collective-permute-start.4) | collective-permute-done | bytes 524320 | tf_op jit(solution)/shard_map/ppermute | solution.py:31
  17.2 0.0 collective-permute-done.2.near_ref
  17.2 7.1 %shard_map.39 = (bf16[2,384,384]{2,1,0:T(8,128)(2,1)S(1)}, bf16[1024,768]{1,0:T(8,128)(2,1)S(1)}) custom-call(s32[2,3]{1,0:T(2,128)S(1)} %fusion.1.code_ref, bf16[2,384,1024]{2,1,0:T(8,128)(2,1)S(1)} %shard_map.37.tmpl_ref, bf16[1024,256]{1,0:T(8,128)(2,1)S(1)} %get-tuple-element.35.own_ref, bf16[2,1024,256]{2,1,0:T(8,128)(2,1)S(1)} %collective-permute-done.2.near_ref, ...), custom_call_target="tpu_custom_call" | custom-call | flops 8000000000 | bytes 2162688 | tf_op jit(solution)/shard_map/pallas_call | solution.py:254
  24.3 0.0 collective-permute-done.3.far_ref
  24.3 7.2 %shard_map.38 = (bf16[2,384,384]{2,1,0:T(8,128)(2,1)S(1)}, bf16[1024,768]{1,0:T(8,128)(2,1)S(1)}) custom-call(s32[2,3]{1,0:T(2,128)S(1)} %fusion.1.code_ref, bf16[2,384,1024]{2,1,0:T(8,128)(2,1)S(1)} %shard_map.37.tmpl_ref, bf16[1024,256]{1,0:T(8,128)(2,1)S(1)} %get-tuple-element.36.own_ref, bf16[2,1024,256]{2,1,0:T(8,128)(2,1)S(1)} %collective-permute-done.2.near_ref, ...), custom_call_target="tpu_custom_call" | custom-call | flops 8000000000 | bytes 2162688 | tf_op jit(solution)/shard_map/pallas_call | solution.py:254
  31.5 1.1 %shard_map.40 = bf16[1040,256]{1,0:T(8,128)(2,1)S(1)} custom-call(s32[2,3]{1,0:T(2,128)S(1)} %fusion.1.code_ref, bf16[1024,768]{1,0:T(8,128)(2,1)S(1)} %get-tuple-element.21.refs_0_, bf16[1024,768]{1,0:T(8,128)(2,1)S(1)} %get-tuple-element.22.refs_1_, bf16[2,384,384]{2,1,0:T(8,128)(2,1)S(1)} %get-tuple-element.23.refs_2_, ...), custom_call_target="tpu_custom_call" | custom-call | flops 800000000 | bytes 532480 | tf_op jit(solution)/shard_map/pallas_call | solution.py:274
  32.7 2.0 %shard_map.41 = (bf16[1040,256]{1,0:T(8,128)(2,1)S(1)}, f32[272,256]{1,0:T(8,128)S(1)}, f32[256,256]{1,0:T(8,128)S(1)}, f32[256,256]{1,0:T(8,128)S(1)}, f32[256,256]{1,0:T(8,128)S(1)}) custom-call(s32[2,3]{1,0:T(2,128)S(1)} %fusion.1.code_ref, bf16[1024,768]{1,0:T(8,128)(2,1)S(1)} %get-tuple-element.21.refs_0_, ...), custom_call_target="tpu_custom_call" | custom-call | flops 1600000000 | bytes 1597440 | tf_op jit(solution)/shard_map/pallas_call | solution.py:274
  34.7 0.8 %collective-permute-start.5 = (bf16[1040,256]{1,0:T(8,128)(2,1)S(1)}, bf16[1040,256]{1,0:T(8,128)(2,1)S(1)}, u32[]{:S(2)}, u32[]{:S(2)}) collective-permute-start(bf16[1040,256]{1,0:T(8,128)(2,1)S(1)} %get-tuple-element.27), channel_id=1, source_target_pairs={{0,1},{1,0},{2,3},{3,2},{4,5},{5,4},{6,7},{7,6},{8,9},{9,8},{10,11... | collective-permute-start | bytes 1597448 | tf_op jit(solution)/shard_map/ppermute | solution.py:23
  35.5 2.0 %collective-permute-start.6 = (bf16[1040,256]{1,0:T(8,128)(2,1)S(1)}, bf16[1040,256]{1,0:T(8,128)(2,1)S(1)}, u32[]{:S(2)}, u32[]{:S(2)}) collective-permute-start(bf16[1040,256]{1,0:T(8,128)(2,1)S(1)} %shard_map.40), channel_id=1, source_target_pairs={{0,0},{7,7},{1,2},{2,1},{3,4},{4,3},{5,6},{6,5},{8,8},{15,15},{9,1... | collective-permute-start | bytes 1597448 | tf_op jit(solution)/shard_map/ppermute | solution.py:31
  37.5 0.0 collective-permute-done.5
  37.5 8.5 %collective-permute-done.6 = bf16[1040,256]{1,0:T(8,128)(2,1)S(1)} collective-permute-done((bf16[1040,256]{1,0:T(8,128)(2,1)S(1)}, bf16[1040,256]{1,0:T(8,128)(2,1)S(1)}, u32[]{:S(2)}, u32[]{:S(2)}) %collective-permute-start.6) | collective-permute-done | bytes 532512 | tf_op jit(solution)/shard_map/ppermute | solution.py:31
  46.1 0.2 add_convert_fusion.1
  46.3 1.6 %collective-permute-start.13 = (bf16[256,256]{1,0:T(8,128)(2,1)S(1)}, bf16[256,256]{1,0:T(8,128)(2,1)S(1)}, u32[]{:S(2)}, u32[]{:S(2)}) collective-permute-start(bf16[256,256]{1,0:T(8,128)(2,1)S(1)} %get-tuple-element.31), channel_id=1, source_target_pairs={{0,16},{8,24},{16,0},{24,8},{1,17},{9,25},{17,1},{25,9},{2,18},{10... | collective-permute-start | bytes 393224 | tf_op jit(solution)/shard_map/ppermute | solution.py:36
  47.9 1.5 %collective-permute-start.11 = (bf16[256,256]{1,0:T(8,128)(2,1)S(1)}, bf16[256,256]{1,0:T(8,128)(2,1)S(1)}, u32[]{:S(2)}, u32[]{:S(2)}) collective-permute-start(bf16[256,256]{1,0:T(8,128)(2,1)S(1)} %get-tuple-element.32), channel_id=1, source_target_pairs={{0,8},{8,0},{16,24},{24,16},{1,9},{9,1},{17,25},{25,17},{2,10},{10... | collective-permute-start | bytes 393224 | tf_op jit(solution)/shard_map/ppermute | solution.py:36
  49.4 0.5 collective-permute-start.9
  49.9 0.5 collective-permute-start.7
  50.4 1.8 %collective-permute-done.13 = bf16[256,256]{1,0:T(8,128)(2,1)S(1)} collective-permute-done((bf16[256,256]{1,0:T(8,128)(2,1)S(1)}, bf16[256,256]{1,0:T(8,128)(2,1)S(1)}, u32[]{:S(2)}, u32[]{:S(2)}) %collective-permute-start.13) | collective-permute-done | bytes 131104 | tf_op jit(solution)/shard_map/ppermute | solution.py:36
  52.3 2.1 %collective-permute-start.14 = (bf16[256,256]{1,0:T(8,128)(2,1)S(1)}, bf16[256,256]{1,0:T(8,128)(2,1)S(1)}, u32[]{:S(2)}, u32[]{:S(2)}) collective-permute-start(bf16[256,256]{1,0:T(8,128)(2,1)S(1)} %add_convert_fusion.refs_6_), channel_id=1, source_target_pairs={{0,8},{8,0},{16,24},{24,16},{1,9},{9,1},{17,25},{25,17},{2,10},{10... | collective-permute-start | bytes 393224 | tf_op jit(solution)/shard_map/ppermute | solution.py:36
  54.4 0.0 collective-permute-done.11
  54.4 1.6 %collective-permute-start.12 = (bf16[256,256]{1,0:T(8,128)(2,1)S(1)}, bf16[256,256]{1,0:T(8,128)(2,1)S(1)}, u32[]{:S(2)}, u32[]{:S(2)}) collective-permute-start(bf16[256,256]{1,0:T(8,128)(2,1)S(1)} %add_convert_fusion.2.refs_4_), channel_id=1, source_target_pairs={{0,16},{8,24},{16,0},{24,8},{1,17},{9,25},{17,1},{25,9},{2,18},{10... | collective-permute-start | bytes 393224 | tf_op jit(solution)/shard_map/ppermute | solution.py:36
  56.0 0.0 collective-permute-done.9
  56.0 0.6 collective-permute-start.10
  56.6 0.5 collective-permute-done.7
  57.1 1.3 %collective-permute-start.8 = (bf16[256,256]{1,0:T(8,128)(2,1)S(1)}, bf16[256,256]{1,0:T(8,128)(2,1)S(1)}, u32[]{:S(2)}, u32[]{:S(2)}) collective-permute-start(bf16[256,256]{1,0:T(8,128)(2,1)S(1)} %add_convert_fusion.6.refs_0_), channel_id=1, source_target_pairs={{0,16},{8,24},{16,0},{24,8},{1,17},{9,25},{17,1},{25,9},{2,18},{10... | collective-permute-start | bytes 393224 | tf_op jit(solution)/shard_map/ppermute | solution.py:36
  58.4 1.5 %collective-permute-done.14.refs_7_ = bf16[256,256]{1,0:T(8,128)(2,1)S(1)} collective-permute-done((bf16[256,256]{1,0:T(8,128)(2,1)S(1)}, bf16[256,256]{1,0:T(8,128)(2,1)S(1)}, u32[]{:S(2)}, u32[]{:S(2)}) %collective-permute-start.14) | collective-permute-done | bytes 131104 | tf_op jit(solution)/shard_map/ppermute | solution.py:36
  59.9 0.9 %collective-permute-done.12.refs_5_ = bf16[256,256]{1,0:T(8,128)(2,1)S(1)} collective-permute-done((bf16[256,256]{1,0:T(8,128)(2,1)S(1)}, bf16[256,256]{1,0:T(8,128)(2,1)S(1)}, u32[]{:S(2)}, u32[]{:S(2)}) %collective-permute-start.12) | collective-permute-done | bytes 131104 | tf_op jit(solution)/shard_map/ppermute | solution.py:36
  60.8 0.8 %collective-permute-done.10.refs_3_ = bf16[256,256]{1,0:T(8,128)(2,1)S(1)} collective-permute-done((bf16[256,256]{1,0:T(8,128)(2,1)S(1)}, bf16[256,256]{1,0:T(8,128)(2,1)S(1)}, u32[]{:S(2)}, u32[]{:S(2)}) %collective-permute-start.10) | collective-permute-done | bytes 131104 | tf_op jit(solution)/shard_map/ppermute | solution.py:36
  61.6 0.6 collective-permute-done.8.refs_1_
  62.2 1.0 %finish.1 = f32[1024,256]{1,0:T(8,128)} custom-call(bf16[256,256]{1,0:T(8,128)(2,1)S(1)} %add_convert_fusion.6.refs_0_, bf16[256,256]{1,0:T(8,128)(2,1)S(1)} %collective-permute-done.8.refs_1_, bf16[256,256]{1,0:T(8,128)(2,1)S(1)} %add_convert_fusion.4.refs_2_, bf16[256,256]{1,0:T(8,128)(2,1)S(1)} %collective-permute-done.10.refs_3_, ...), custom_call_target="tpu_custom_call" | custom-call | tf_op jit(solution)/shard_map/finish/pallas_call | solution.py:208
  (5 shorter events, 0.1 us)
Async XLA Ops:
  0.0 11.6 %copy-start = (bf16[1024,256]{1,0:T(8,128)(2,1)S(1)}, bf16[1024,256]{1,0:T(8,128)(2,1)}, u32[]{:S(2)}) copy-start(bf16[1024,256]{1,0:T(8,128)(2,1)} %own_ref) | copy-start | bytes 1572868
  0.8 16.4 %collective-permute-start.2 = (bf16[2,1024,256]{2,1,0:T(8,128)(2,1)}, bf16[2,1024,256]{2,1,0:T(8,128)(2,1)S(1)}, u32[]{:S(2)}, u32[]{:S(2)}) collective-permute-start(bf16[2,1024,256]{2,1,0:T(8,128)(2,1)} %param.3), channel_id=1, source_target_pairs={{0,1},{1,0},{2,3},{3,2},{4,5},{5,4},{6,7},{7,6},{8,9},{9,8},{10,11... | collective-permute-start | bytes 3145736 | tf_op jit(solution)/shard_map/ppermute | solution.py:23
  0.8 10.7 %collective-permute-start.1 = (bf16[1024,256]{1,0:T(8,128)(2,1)}, bf16[1024,256]{1,0:T(8,128)(2,1)S(1)}, u32[]{:S(2)}, u32[]{:S(2)}) collective-permute-start(bf16[1024,256]{1,0:T(8,128)(2,1)} %own_ref), channel_id=1, source_target_pairs={{0,0},{7,7},{1,2},{2,1},{3,4},{4,3},{5,6},{6,5},{8,8},{15,15},{9,1... | collective-permute-start | bytes 1572872 | tf_op jit(solution)/shard_map/ppermute | solution.py:31
  3.3 8.3 %collective-permute-start = (bf16[1024,256]{1,0:T(8,128)(2,1)}, bf16[1024,256]{1,0:T(8,128)(2,1)S(1)}, u32[]{:S(2)}, u32[]{:S(2)}) collective-permute-start(bf16[1024,256]{1,0:T(8,128)(2,1)} %own_ref), channel_id=1, source_target_pairs={{0,1},{1,0},{2,3},{3,2},{4,5},{5,4},{6,7},{7,6},{8,9},{9,8},{10,11... | collective-permute-start | bytes 1572872 | tf_op jit(solution)/shard_map/ppermute | solution.py:23
  5.8 11.4 %collective-permute-start.4 = (bf16[1024,256]{1,0:T(8,128)(2,1)S(1)}, bf16[1024,256]{1,0:T(8,128)(2,1)S(1)}, u32[]{:S(2)}, u32[]{:S(2)}) collective-permute-start(bf16[1024,256]{1,0:T(8,128)(2,1)S(1)} %get-tuple-element.35.own_ref), channel_id=1, source_target_pairs={{0,0},{7,7},{1,2},{2,1},{3,4},{4,3},{5,6},{6,5},{8,8},{15,15},{9,1... | collective-permute-start | bytes 1572872 | tf_op jit(solution)/shard_map/ppermute | solution.py:31
  7.8 16.5 %collective-permute-start.3 = (bf16[1024,256]{1,0:T(8,128)(2,1)S(1)}, bf16[1024,256]{1,0:T(8,128)(2,1)S(1)}, u32[]{:S(2)}, u32[]{:S(2)}) collective-permute-start(bf16[1024,256]{1,0:T(8,128)(2,1)S(1)} %get-tuple-element.36.own_ref), channel_id=1, source_target_pairs={{0,0},{7,7},{1,2},{2,1},{3,4},{4,3},{5,6},{6,5},{8,8},{15,15},{9,1... | collective-permute-start | bytes 1572872 | tf_op jit(solution)/shard_map/ppermute | solution.py:31
  34.7 2.9 %collective-permute-start.5 = (bf16[1040,256]{1,0:T(8,128)(2,1)S(1)}, bf16[1040,256]{1,0:T(8,128)(2,1)S(1)}, u32[]{:S(2)}, u32[]{:S(2)}) collective-permute-start(bf16[1040,256]{1,0:T(8,128)(2,1)S(1)} %get-tuple-element.27), channel_id=1, source_target_pairs={{0,1},{1,0},{2,3},{3,2},{4,5},{5,4},{6,7},{7,6},{8,9},{9,8},{10,11... | collective-permute-start | bytes 1597448 | tf_op jit(solution)/shard_map/ppermute | solution.py:23
  35.5 10.6 %collective-permute-start.6 = (bf16[1040,256]{1,0:T(8,128)(2,1)S(1)}, bf16[1040,256]{1,0:T(8,128)(2,1)S(1)}, u32[]{:S(2)}, u32[]{:S(2)}) collective-permute-start(bf16[1040,256]{1,0:T(8,128)(2,1)S(1)} %shard_map.40), channel_id=1, source_target_pairs={{0,0},{7,7},{1,2},{2,1},{3,4},{4,3},{5,6},{6,5},{8,8},{15,15},{9,1... | collective-permute-start | bytes 1597448 | tf_op jit(solution)/shard_map/ppermute | solution.py:31
  46.3 5.9 %collective-permute-start.13 = (bf16[256,256]{1,0:T(8,128)(2,1)S(1)}, bf16[256,256]{1,0:T(8,128)(2,1)S(1)}, u32[]{:S(2)}, u32[]{:S(2)}) collective-permute-start(bf16[256,256]{1,0:T(8,128)(2,1)S(1)} %get-tuple-element.31), channel_id=1, source_target_pairs={{0,16},{8,24},{16,0},{24,8},{1,17},{9,25},{17,1},{25,9},{2,18},{10... | collective-permute-start | bytes 393224 | tf_op jit(solution)/shard_map/ppermute | solution.py:36
  47.9 6.4 %collective-permute-start.11 = (bf16[256,256]{1,0:T(8,128)(2,1)S(1)}, bf16[256,256]{1,0:T(8,128)(2,1)S(1)}, u32[]{:S(2)}, u32[]{:S(2)}) collective-permute-start(bf16[256,256]{1,0:T(8,128)(2,1)S(1)} %get-tuple-element.32), channel_id=1, source_target_pairs={{0,8},{8,0},{16,24},{24,16},{1,9},{9,1},{17,25},{25,17},{2,10},{10... | collective-permute-start | bytes 393224 | tf_op jit(solution)/shard_map/ppermute | solution.py:36
  49.4 6.6 %collective-permute-start.9 = (bf16[256,256]{1,0:T(8,128)(2,1)S(1)}, bf16[256,256]{1,0:T(8,128)(2,1)S(1)}, u32[]{:S(2)}, u32[]{:S(2)}) collective-permute-start(bf16[256,256]{1,0:T(8,128)(2,1)S(1)} %get-tuple-element.33), channel_id=1, source_target_pairs={{0,16},{8,24},{16,0},{24,8},{1,17},{9,25},{17,1},{25,9},{2,18},{10... | collective-permute-start | bytes 393224 | tf_op jit(solution)/shard_map/ppermute | solution.py:36
  49.9 7.2 %collective-permute-start.7 = (bf16[256,256]{1,0:T(8,128)(2,1)S(1)}, bf16[256,256]{1,0:T(8,128)(2,1)S(1)}, u32[]{:S(2)}, u32[]{:S(2)}) collective-permute-start(bf16[256,256]{1,0:T(8,128)(2,1)S(1)} %get-tuple-element.34), channel_id=1, source_target_pairs={{0,8},{8,0},{16,24},{24,16},{1,9},{9,1},{17,25},{25,17},{2,10},{10... | collective-permute-start | bytes 393224 | tf_op jit(solution)/shard_map/ppermute | solution.py:36
  52.3 7.6 %collective-permute-start.14 = (bf16[256,256]{1,0:T(8,128)(2,1)S(1)}, bf16[256,256]{1,0:T(8,128)(2,1)S(1)}, u32[]{:S(2)}, u32[]{:S(2)}) collective-permute-start(bf16[256,256]{1,0:T(8,128)(2,1)S(1)} %add_convert_fusion.refs_6_), channel_id=1, source_target_pairs={{0,8},{8,0},{16,24},{24,16},{1,9},{9,1},{17,25},{25,17},{2,10},{10... | collective-permute-start | bytes 393224 | tf_op jit(solution)/shard_map/ppermute | solution.py:36
  54.4 6.4 %collective-permute-start.12 = (bf16[256,256]{1,0:T(8,128)(2,1)S(1)}, bf16[256,256]{1,0:T(8,128)(2,1)S(1)}, u32[]{:S(2)}, u32[]{:S(2)}) collective-permute-start(bf16[256,256]{1,0:T(8,128)(2,1)S(1)} %add_convert_fusion.2.refs_4_), channel_id=1, source_target_pairs={{0,16},{8,24},{16,0},{24,8},{1,17},{9,25},{17,1},{25,9},{2,18},{10... | collective-permute-start | bytes 393224 | tf_op jit(solution)/shard_map/ppermute | solution.py:36
  56.0 5.6 %collective-permute-start.10 = (bf16[256,256]{1,0:T(8,128)(2,1)S(1)}, bf16[256,256]{1,0:T(8,128)(2,1)S(1)}, u32[]{:S(2)}, u32[]{:S(2)}) collective-permute-start(bf16[256,256]{1,0:T(8,128)(2,1)S(1)} %add_convert_fusion.4.refs_2_), channel_id=1, source_target_pairs={{0,8},{8,0},{16,24},{24,16},{1,9},{9,1},{17,25},{25,17},{2,10},{10... | collective-permute-start | bytes 393224 | tf_op jit(solution)/shard_map/ppermute | solution.py:36
  57.1 5.1 %collective-permute-start.8 = (bf16[256,256]{1,0:T(8,128)(2,1)S(1)}, bf16[256,256]{1,0:T(8,128)(2,1)S(1)}, u32[]{:S(2)}, u32[]{:S(2)}) collective-permute-start(bf16[256,256]{1,0:T(8,128)(2,1)S(1)} %add_convert_fusion.6.refs_0_), channel_id=1, source_target_pairs={{0,16},{8,24},{16,0},{24,8},{1,17},{9,25},{17,1},{25,9},{2,18},{10... | collective-permute-start | bytes 393224 | tf_op jit(solution)/shard_map/ppermute | solution.py:36

commit v6 on v5

--- a/solution.py
+++ b/solution.py
@@ -55,26 +55,36 @@
     )
 
 
-def read_codes(code_ref):
-    lights, members = code_ref.shape
-    return [[code_ref[g, j] for j in range(members)] for g in range(lights)]
+def read_codes(blocks_ref, blk_dev):
+    position = lax.axis_index("cortex")
+    odd = position % 2
+    codes = []
+    for g in range(blocks_ref.shape[0]):
+        codes.append([])
+        for j in range(blocks_ref.shape[1]):
+            window = blocks_ref[g, j] - (position - 1) * blk_dev
+            side = window // blk_dev
+            place = jnp.where(side == 1, 0, jnp.where(side == 2 * odd, 2, 1))
+            codes[g].append(place * blk_dev + window % blk_dev)
+    return codes
 
 
 def columns(ref, half):
     return ref[:, pl.ds(pl.multiple_of(half * BLOCK, BLOCK), BLOCK)]
 
 
-def template_kernel(code_ref, own_ref, near_ref, far_ref, out_ref):
-    lights, members = code_ref.shape
-    codes = read_codes(code_ref)
+def template_kernel(blocks_ref, own_ref, near_ref, far_ref, out_ref):
+    lights, members = blocks_ref.shape
+    blk_dev = own_ref.shape[1] // BLOCK
+    codes = read_codes(blocks_ref, blk_dev)
     for g in range(lights):
         for j in range(members):
             code = codes[g][j]
             for place, ref in enumerate((own_ref, near_ref, far_ref)):
 
-                @pl.when(code // 2 == place)
+                @pl.when(code // blk_dev == place)
                 def _():
-                    out_ref[g, j * BLOCK : (j + 1) * BLOCK, :] = columns(ref, code % 2).T
+                    out_ref[g, j * BLOCK : (j + 1) * BLOCK, :] = columns(ref, code % blk_dev).T
 
 
 def newton_schulz(now_ref, next_ref, gram_ref):
@@ -96,20 +106,21 @@
         next_ref[g] = (1.5 * now.astype(jnp.float32) - 0.5 * product).astype(jnp.bfloat16)
 
 
-def polar_kernel(subject, code_ref, tmpl_ref, own_ref, near_ref, far_ref, map_ref, cols_ref, odd_ref, gram_ref):
-    lights, members = code_ref.shape
+def polar_kernel(subject, blocks_ref, tmpl_ref, own_ref, near_ref, far_ref, map_ref, cols_ref, odd_ref, gram_ref):
+    lights, members = blocks_ref.shape
     width = members * BLOCK
     frames = own_ref.shape[0]
-    codes = read_codes(code_ref)
+    blk_dev = own_ref.shape[1] // BLOCK
+    codes = read_codes(blocks_ref, blk_dev)
     for g in range(lights):
         for i in range(members):
             code = codes[g][i]
             lo = g * width + i * BLOCK
             for place, ref in enumerate((own_ref, near_ref.at[subject], far_ref)):
 
-                @pl.when(code // 2 == place)
+                @pl.when(code // blk_dev == place)
                 def _():
-                    cols_ref[:, lo : lo + BLOCK] = columns(ref, code % 2)
+                    cols_ref[:, lo : lo + BLOCK] = columns(ref, code % blk_dev)
 
     first_ref = map_ref if NS_STEPS % 2 == 0 else odd_ref
     row = lax.broadcasted_iota(jnp.int32, (width, width), 0)
@@ -128,14 +139,14 @@
         newton_schulz(turns[step % 2], turns[1 - step % 2], gram_ref)
 
 
-def map_kernel(subj_count, places, splits, code_ref, *refs):
+def map_kernel(subj_count, blk_dev, places, splits, blocks_ref, *refs):
     cols_refs = refs[:subj_count]
     map_refs = refs[subj_count : 2 * subj_count]
     weight_ref = refs[-1]
     out_refs = refs[2 * subj_count : -1]
-    lights, members = code_ref.shape
+    lights, members = blocks_ref.shape
     width = members * BLOCK
-    codes = read_codes(code_ref)
+    codes = read_codes(blocks_ref, blk_dev)
     counts = []
     for p, place in enumerate(places):
         total = jnp.int32(0)
@@ -187,33 +198,37 @@
             at += 1
 
 
-def finish_kernel(subjects, *refs):
-    *pairs, cover_ref, out_ref, tile_ref, sems = refs
+def finish_kernel(subjects, count, above, *refs):
+    pairs, cover_ref = refs[: 2 * count], refs[2 * count]
+    out_ref, tile_ref, sems = refs[-3:]
     rows = pairs[0].shape[0]
     scale = 1.0 / (cover_ref[...] * subjects)
     copies = []
-    for h in range(len(pairs) // 2):
+    for h in range(count):
         total = pairs[2 * h][...].astype(jnp.float32) + pairs[2 * h + 1][...].astype(jnp.float32)
         here = pl.ds(h * rows, rows)
         tile_ref[here, :] = total * scale
-        copies.append(pltpu.make_async_copy(tile_ref.at[here], out_ref.at[here], sems.at[h]))
+        there = pl.ds((above + h) * rows, rows)
+        copies.append(pltpu.make_async_copy(tile_ref.at[here], out_ref.at[there], sems.at[h]))
         copies[-1].start()
     for copy in copies:
         copy.wait()
 
 
-def finished(pairs, cover, subjects):
+def finished(result, frames, above, pairs, cover, subjects):
     rows, cols = pairs[0][0].shape
     count = len(pairs)
+    placed = [] if result is None else [result]
     return pl.pallas_call(
-        functools.partial(finish_kernel, subjects),
-        out_shape=jax.ShapeDtypeStruct((rows * count, cols), jnp.float32),
-        in_specs=[vmem()] * (2 * count + 1),
+        functools.partial(finish_kernel, subjects, count, above),
+        out_shape=jax.ShapeDtypeStruct((frames, cols), jnp.float32),
+        in_specs=[vmem()] * (2 * count + 1) + [pl.BlockSpec(memory_space=pl.ANY)] * len(placed),
         out_specs=pl.BlockSpec(memory_space=pl.ANY),
         scratch_shapes=[pltpu.VMEM((rows * count, cols), jnp.float32), pltpu.SemaphoreType.DMA((count,))],
+        input_output_aliases={2 * count + 1: 0} if placed else {},
         compiler_params=pltpu.CompilerParams(vmem_limit_bytes=LIMIT * MIB),
         name="finish",
-    )(*[value for pair in pairs for value in pair], cover)
+    )(*[value for pair in pairs for value in pair], cover, *placed)
 
 
 def body(series, template, sl_blocks):
@@ -226,13 +241,6 @@
     odd = position % 2
     far_real = jnp.logical_and(position + 2 * odd - 1 >= 0, position + 2 * odd - 1 < count)
 
-    window = sl_blocks - (position - 1) * blk_dev
-    side = window // blk_dev
-    place = jnp.where(side == 1, 0, jnp.where((side == 2) == (odd == 1), 2, 1))
-    code = (place * blk_dev + window % blk_dev).astype(jnp.int32)
-
-    code, template, series = lax.optimization_barrier((code, template, series))
-
     tmpl_far = swap_far(template)
     tmpl_near = swap_near(template)
     parts = [series[s] for s in range(subj_count)]
@@ -247,7 +255,7 @@
         [vmem()] * 4,
         flops=10**9,
         limit=LIMIT,
-    )(code, template, tmpl_near, tmpl_far)
+    )(sl_blocks, template, tmpl_near, tmpl_far)
 
     maps, cols = [], []
     for s in range(subj_count):
@@ -261,31 +269,31 @@
             flops=8 * 10**9,
             limit=LIMIT,
             scratch=[pltpu.VMEM((lights, width, width), jnp.bfloat16)] * 2,
-        )(code, tmpl_rows, parts[s], near, far[s])
+        )(sl_blocks, tmpl_rows, parts[s], near, far[s])
         maps.append(polar)
         cols.append(gathered)
 
-    def mapped(places, splits, types):
+    def mapped(lists, places, splits, types):
         shapes = [
             jax.ShapeDtypeStruct((rows + (COUNT_ROWS if n == 0 else 0), width_dev), kind)
             for pieces, kind in zip(splits, types)
             for n, rows in enumerate(pieces)
         ]
         return call(
-            functools.partial(map_kernel, subj_count, places, splits),
+            functools.partial(map_kernel, subj_count, blk_dev, places, splits),
             shapes,
             [vmem()] * (1 + 2 * subj_count),
             flops=len(places) * 4 * 10**8,
             limit=LIMIT,
             scratch=[pltpu.VMEM((len(places) * BLOCK, subj_count * lights * width), jnp.bfloat16)],
-        )(code, *cols, *maps)
+        )(lists, *cols, *maps)
 
     blocks = list(range(blk_dev))
-    (to_far,) = mapped([2 * blk_dev + b for b in blocks], ((frames,),), (jnp.bfloat16,))
+    (to_far,) = mapped(sl_blocks, [2 * blk_dev + b for b in blocks], ((frames,),), (jnp.bfloat16,))
     from_far = swap_far(to_far)
-    code, _ = lax.optimization_barrier((code, to_far))
+    lists, _ = lax.optimization_barrier((sl_blocks, to_far))
     to_near, *own = mapped(
-        [blk_dev + b for b in blocks] + blocks, ((frames,), (frames // PIECES,) * PIECES), (jnp.bfloat16, jnp.float32)
+        lists, [blk_dev + b for b in blocks] + blocks, ((frames,), (frames // PIECES,) * PIECES), (jnp.bfloat16, jnp.float32)
     )
     from_near = swap_near(to_near)
     keep = far_real.astype(jnp.float32)
@@ -310,7 +318,9 @@
             pairs.append((sent, got))
     if not pairs:
         return jnp.concatenate(halves, axis=0) / per_vertex / (subj_count * subj_size)
-    return finished(pairs, per_vertex, subj_count * subj_size)
+    subjects = subj_count * subj_size
+    result = finished(None, frames, 0, pairs[:-1], per_vertex, subjects)
+    return finished(result, frames, PIECES - 1, pairs[-1:], per_vertex, subjects)
 
 
 def solution(mesh):

time: 63.6 us -> 61.3 us (0.964)
  the two profiles are of different devices: /device:TPU:16 before, /device:TPU:12 now
where the time goes in v6:
time: 61.3 us; the launch traced here: 61.1 us
  starting transfers between devices  20.7 us (34%)
  Pallas kernels  20.2 us (33%)
  waiting for transfers between devices  18.2 us (30%)
  local copies, waits for them, and re-layouts  1.28 us (2%)
    pallas_call x2, Pallas kernels, body(): call(functools.partial(polar_kernel, s), (jax.ShapeDtypeStruct((lights, w...  14.4 us
    ppermute x4, waiting for transfers between devices, swap_far(): return lax.ppermute(value, 'cortex', route)  11.4 us
    ppermute x4, starting transfers between devices, swap_far(): return lax.ppermute(value, 'cortex', route)  9.63 us
    ppermute x8, starting transfers between devices, swap_subj(): lax.ppermute(value, 'subj', [(i, i ^ distance) for i in range(count)])  8.89 us
    ppermute x8, waiting for transfers between devices, swap_subj(): lax.ppermute(value, 'subj', [(i, i ^ distance) for i in range(count)])  6.86 us
    pallas_call x2, Pallas kernels, mapped(): call(functools.partial(map_kernel, subj_count, blk_dev, places, splits),...  3.18 us
    ppermute x3, starting transfers between devices, swap_near(): return lax.ppermute(value, 'cortex', [(i, i ^ 1) for i in range(count)])  2.13 us
    pallas_call x2, Pallas kernels, finished(): pl.pallas_call(functools.partial(finish_kernel, subjects, count, above),...  1.69 us
  transfers between devices with their start and end apart: 15, of which 7 were waited for; matrix products, arithmetic and copies ran while one was open for 2% of the time, Pallas kernels for 18%

profile of v6, /device:TPU:12, one launch (start us, length us, event | category | flops | bytes accessed | tf_op | source)
XLA Modules:
  0.0 61.1 jit_solution(12806528501599608260)
XLA Ops:
  0.0 0.0 copy-start.1
  0.0 0.0 copy-start
  0.0 0.0 collective-permute-start.2
  0.0 0.5 collective-permute-start
  0.5 2.0 %collective-permute-start.1 = (bf16[1024,256]{1,0:T(8,128)(2,1)}, bf16[1024,256]{1,0:T(8,128)(2,1)S(1)}, u32[]{:S(2)}, u32[]{:S(2)}) collective-permute-start(bf16[1024,256]{1,0:T(8,128)(2,1)} %own_ref.1), channel_id=1, source_target_pairs={{0,0},{7,7},{1,2},{2,1},{3,4},{4,3},{5,6},{6,5},{8,8},{15,15},{9,1... | collective-permute-start | bytes 1572872 | tf_op jit(solution)/shard_map/ppermute | solution.py:31
  2.5 1.3 %slice_bitcast_fusion = (bf16[1024,256]{1,0:T(8,128)(2,1)S(1)}, bf16[1024,256]{1,0:T(8,128)(2,1)S(1)}) fusion(bf16[2,1024,256]{2,1,0:T(8,128)(2,1)} %param.3), kind=kLoop, calls=%fused_computation | loop fusion | bytes 2097152 | tf_op jit(solution)/shard_map/squeeze | solution.py:246
  3.8 3.5 %collective-permute-start.3 = (bf16[1024,256]{1,0:T(8,128)(2,1)S(1)}, bf16[1024,256]{1,0:T(8,128)(2,1)S(1)}, u32[]{:S(2)}, u32[]{:S(2)}) collective-permute-start(bf16[1024,256]{1,0:T(8,128)(2,1)S(1)} %get-tuple-element.30.own_ref), channel_id=1, source_target_pairs={{0,0},{7,7},{1,2},{2,1},{3,4},{4,3},{5,6},{6,5},{8,8},{15,15},{9,1... | collective-permute-start | bytes 1572872 | tf_op jit(solution)/shard_map/ppermute | solution.py:31
  7.4 2.0 %collective-permute-start.4 = (bf16[1024,256]{1,0:T(8,128)(2,1)S(1)}, bf16[1024,256]{1,0:T(8,128)(2,1)S(1)}, u32[]{:S(2)}, u32[]{:S(2)}) collective-permute-start(bf16[1024,256]{1,0:T(8,128)(2,1)S(1)} %get-tuple-element.29.own_ref), channel_id=1, source_target_pairs={{0,0},{7,7},{1,2},{2,1},{3,4},{4,3},{5,6},{6,5},{8,8},{15,15},{9,1... | collective-permute-start | bytes 1572872 | tf_op jit(solution)/shard_map/ppermute | solution.py:31
  9.4 0.0 collective-permute-done.near_ref
  9.4 1.8 %collective-permute-done.1.far_ref = bf16[1024,256]{1,0:T(8,128)(2,1)S(1)} collective-permute-done((bf16[1024,256]{1,0:T(8,128)(2,1)}, bf16[1024,256]{1,0:T(8,128)(2,1)S(1)}, u32[]{:S(2)}, u32[]{:S(2)}) %collective-permute-start.1) | collective-permute-done | bytes 524320 | tf_op jit(solution)/shard_map/ppermute | solution.py:31
  11.2 0.0 copy-done.1
  11.2 0.0 copy-done
  11.2 1.0 %shard_map.37.tmpl_ref = bf16[2,384,1024]{2,1,0:T(8,128)(2,1)S(1)} custom-call(s32[2,3]{1,0:T(2,128)S(1)} %copy-done, bf16[1024,256]{1,0:T(8,128)(2,1)S(1)} %copy-done.1, bf16[1024,256]{1,0:T(8,128)(2,1)S(1)} %collective-permute-done.near_ref, bf16[1024,256]{1,0:T(8,128)(2,1)S(1)} %collective-permute-done.1.far_ref), custom_call_target="tpu_custom_call" | custom-call | flops 1000000000 | bytes 1572864 | tf_op jit(solution)/shard_map/pallas_call | solution.py:252
  12.2 4.7 %collective-permute-done.3.far_ref = bf16[1024,256]{1,0:T(8,128)(2,1)S(1)} collective-permute-done((bf16[1024,256]{1,0:T(8,128)(2,1)S(1)}, bf16[1024,256]{1,0:T(8,128)(2,1)S(1)}, u32[]{:S(2)}, u32[]{:S(2)}) %collective-permute-start.3) | collective-permute-done | bytes 524320 | tf_op jit(solution)/shard_map/ppermute | solution.py:31
  16.8 0.0 collective-permute-done.2.near_ref
  16.8 7.1 %shard_map.38 = (bf16[2,384,384]{2,1,0:T(8,128)(2,1)S(1)}, bf16[1024,768]{1,0:T(8,128)(2,1)S(1)}) custom-call(s32[2,3]{1,0:T(2,128)S(1)} %copy-done, bf16[2,384,1024]{2,1,0:T(8,128)(2,1)S(1)} %shard_map.37.tmpl_ref, bf16[1024,256]{1,0:T(8,128)(2,1)S(1)} %get-tuple-element.30.own_ref, bf16[2,1024,256]{2,1,0:T(8,128)(2,1)S(1)} %collective-permute-done.2.near_ref, ...), custom_call_target="tpu_custom_call" | custom-call | flops 8000000000 | bytes 2162688 | tf_op jit(solution)/shard_map/pallas_call | solution.py:262
  23.9 0.0 collective-permute-done.4.far_ref
  24.0 7.3 %shard_map.39 = (bf16[2,384,384]{2,1,0:T(8,128)(2,1)S(1)}, bf16[1024,768]{1,0:T(8,128)(2,1)S(1)}) custom-call(s32[2,3]{1,0:T(2,128)S(1)} %copy-done, bf16[2,384,1024]{2,1,0:T(8,128)(2,1)S(1)} %shard_map.37.tmpl_ref, bf16[1024,256]{1,0:T(8,128)(2,1)S(1)} %get-tuple-element.29.own_ref, bf16[2,1024,256]{2,1,0:T(8,128)(2,1)S(1)} %collective-permute-done.2.near_ref, ...), custom_call_target="tpu_custom_call" | custom-call | flops 8000000000 | bytes 2162688 | tf_op jit(solution)/shard_map/pallas_call | solution.py:262
  31.3 1.2 %shard_map.40 = bf16[1040,256]{1,0:T(8,128)(2,1)S(1)} custom-call(s32[2,3]{1,0:T(2,128)S(1)} %copy-done, bf16[1024,768]{1,0:T(8,128)(2,1)S(1)} %get-tuple-element.15.refs_0_, bf16[1024,768]{1,0:T(8,128)(2,1)S(1)} %get-tuple-element.16.refs_1_, bf16[2,384,384]{2,1,0:T(8,128)(2,1)S(1)} %get-tuple-element.17.refs_2_, ...), custom_call_target="tpu_custom_call" | custom-call | flops 800000000 | bytes 532480 | tf_op jit(solution)/shard_map/pallas_call | solution.py:282
  32.4 2.0 %collective-permute-start.6 = (bf16[1040,256]{1,0:T(8,128)(2,1)S(1)}, bf16[1040,256]{1,0:T(8,128)(2,1)S(1)}, u32[]{:S(2)}, u32[]{:S(2)}) collective-permute-start(bf16[1040,256]{1,0:T(8,128)(2,1)S(1)} %shard_map.40), channel_id=1, source_target_pairs={{0,0},{7,7},{1,2},{2,1},{3,4},{4,3},{5,6},{6,5},{8,8},{15,15},{9,1... | collective-permute-start | bytes 1597448 | tf_op jit(solution)/shard_map/ppermute | solution.py:31
  34.5 2.0 %shard_map.41 = (bf16[1040,256]{1,0:T(8,128)(2,1)S(1)}, f32[272,256]{1,0:T(8,128)S(1)}, f32[256,256]{1,0:T(8,128)S(1)}, f32[256,256]{1,0:T(8,128)S(1)}, f32[256,256]{1,0:T(8,128)S(1)}) custom-call(s32[2,3]{1,0:T(2,128)S(1)} %copy-done, bf16[1024,768]{1,0:T(8,128)(2,1)S(1)} %get-tuple-element.15.refs_0_, bf16[1024,768]{1,0:T(8,128)(2,1)S(1)} %get-tuple-element.16.refs_1_, ...), custom_call_target="tpu_custom_call" | custom-call | flops 1600000000 | bytes 1597440 | tf_op jit(solution)/shard_map/pallas_call | solution.py:282
  36.5 1.6 %collective-permute-start.5 = (bf16[1040,256]{1,0:T(8,128)(2,1)S(1)}, bf16[1040,256]{1,0:T(8,128)(2,1)S(1)}, u32[]{:S(2)}, u32[]{:S(2)}) collective-permute-start(bf16[1040,256]{1,0:T(8,128)(2,1)S(1)} %get-tuple-element.21), channel_id=1, source_target_pairs={{0,1},{1,0},{2,3},{3,2},{4,5},{5,4},{6,7},{7,6},{8,9},{9,8},{10,11... | collective-permute-start | bytes 1597448 | tf_op jit(solution)/shard_map/ppermute | solution.py:23
  38.1 4.9 %collective-permute-done.6 = bf16[1040,256]{1,0:T(8,128)(2,1)S(1)} collective-permute-done((bf16[1040,256]{1,0:T(8,128)(2,1)S(1)}, bf16[1040,256]{1,0:T(8,128)(2,1)S(1)}, u32[]{:S(2)}, u32[]{:S(2)}) %collective-permute-start.6) | collective-permute-done | bytes 532512 | tf_op jit(solution)/shard_map/ppermute | solution.py:31
  43.0 0.0 collective-permute-done.5
  43.0 0.2 add_convert_fusion.1
  43.3 0.6 collective-permute-start.7
  43.9 1.5 %collective-permute-start.9 = (bf16[256,256]{1,0:T(8,128)(2,1)S(1)}, bf16[256,256]{1,0:T(8,128)(2,1)S(1)}, u32[]{:S(2)}, u32[]{:S(2)}) collective-permute-start(bf16[256,256]{1,0:T(8,128)(2,1)S(1)} %get-tuple-element.27), channel_id=1, source_target_pairs={{0,8},{8,0},{16,24},{24,16},{1,9},{9,1},{17,25},{25,17},{2,10},{10... | collective-permute-start | bytes 393224 | tf_op jit(solution)/shard_map/ppermute | solution.py:36
  45.3 1.5 %collective-permute-start.11 = (bf16[256,256]{1,0:T(8,128)(2,1)S(1)}, bf16[256,256]{1,0:T(8,128)(2,1)S(1)}, u32[]{:S(2)}, u32[]{:S(2)}) collective-permute-start(bf16[256,256]{1,0:T(8,128)(2,1)S(1)} %get-tuple-element.26), channel_id=1, source_target_pairs={{0,16},{8,24},{16,0},{24,8},{1,17},{9,25},{17,1},{25,9},{2,18},{10... | collective-permute-start | bytes 393224 | tf_op jit(solution)/shard_map/ppermute | solution.py:36
  46.9 0.5 collective-permute-start.13
  47.4 2.3 %collective-permute-done.7 = bf16[256,256]{1,0:T(8,128)(2,1)S(1)} collective-permute-done((bf16[256,256]{1,0:T(8,128)(2,1)S(1)}, bf16[256,256]{1,0:T(8,128)(2,1)S(1)}, u32[]{:S(2)}, u32[]{:S(2)}) %collective-permute-start.7) | collective-permute-done | bytes 131104 | tf_op jit(solution)/shard_map/ppermute | solution.py:36
  49.7 1.6 %collective-permute-start.8 = (bf16[256,256]{1,0:T(8,128)(2,1)S(1)}, bf16[256,256]{1,0:T(8,128)(2,1)S(1)}, u32[]{:S(2)}, u32[]{:S(2)}) collective-permute-start(bf16[256,256]{1,0:T(8,128)(2,1)S(1)} %add_convert_fusion.6.refs_0_), channel_id=1, source_target_pairs={{0,8},{8,0},{16,24},{24,16},{1,9},{9,1},{17,25},{25,17},{2,10},{10... | collective-permute-start | bytes 393224 | tf_op jit(solution)/shard_map/ppermute | solution.py:36
  51.3 0.0 collective-permute-done.9
  51.3 0.6 collective-permute-start.10
  51.9 0.0 collective-permute-done.11
  51.9 1.8 %collective-permute-start.12 = (bf16[256,256]{1,0:T(8,128)(2,1)S(1)}, bf16[256,256]{1,0:T(8,128)(2,1)S(1)}, u32[]{:S(2)}, u32[]{:S(2)}) collective-permute-start(bf16[256,256]{1,0:T(8,128)(2,1)S(1)} %add_convert_fusion.2.refs_2_), channel_id=1, source_target_pairs={{0,8},{8,0},{16,24},{24,16},{1,9},{9,1},{17,25},{25,17},{2,10},{10... | collective-permute-start | bytes 393224 | tf_op jit(solution)/shard_map/ppermute | solution.py:36
  53.8 0.0 collective-permute-done.13
  53.8 0.8 %collective-permute-start.14 = (bf16[256,256]{1,0:T(8,128)(2,1)S(1)}, bf16[256,256]{1,0:T(8,128)(2,1)S(1)}, u32[]{:S(2)}, u32[]{:S(2)}) collective-permute-start(bf16[256,256]{1,0:T(8,128)(2,1)S(1)} %add_convert_fusion.refs_4_), channel_id=1, source_target_pairs={{0,16},{8,24},{16,0},{24,8},{1,17},{9,25},{17,1},{25,9},{2,18},{10... | collective-permute-start | bytes 393224 | tf_op jit(solution)/shard_map/ppermute | solution.py:36
  54.7 2.7 %collective-permute-done.10.refs_1_ = bf16[256,256]{1,0:T(8,128)(2,1)S(1)} collective-permute-done((bf16[256,256]{1,0:T(8,128)(2,1)S(1)}, bf16[256,256]{1,0:T(8,128)(2,1)S(1)}, u32[]{:S(2)}, u32[]{:S(2)}) %collective-permute-start.10) | collective-permute-done | bytes 131104 | tf_op jit(solution)/shard_map/ppermute | solution.py:36
  57.3 0.5 collective-permute-done.12.refs_3_
  57.8 1.4 %collective-permute-done.14.refs_5_ = bf16[256,256]{1,0:T(8,128)(2,1)S(1)} collective-permute-done((bf16[256,256]{1,0:T(8,128)(2,1)S(1)}, bf16[256,256]{1,0:T(8,128)(2,1)S(1)}, u32[]{:S(2)}, u32[]{:S(2)}) %collective-permute-start.14) | collective-permute-done | bytes 131104 | tf_op jit(solution)/shard_map/ppermute | solution.py:36
  59.2 0.9 %finish.2.refs_3_ = f32[1024,256]{1,0:T(8,128)} custom-call(bf16[256,256]{1,0:T(8,128)(2,1)S(1)} %add_convert_fusion.4.refs_0_, bf16[256,256]{1,0:T(8,128)(2,1)S(1)} %collective-permute-done.10.refs_1_, bf16[256,256]{1,0:T(8,128)(2,1)S(1)} %add_convert_fusion.2.refs_2_, bf16[256,256]{1,0:T(8,128)(2,1)S(1)} %collective-permute-done.12.refs_3_, ...), custom_call_target="tpu_custom_call" | custom-call | tf_op jit(solution)/shard_map/finish/pallas_call | solution.py:222
  60.1 0.0 collective-permute-done.8.refs_1_
  60.1 0.8 %finish.3 = f32[1024,256]{1,0:T(8,128)} custom-call(bf16[256,256]{1,0:T(8,128)(2,1)S(1)} %add_convert_fusion.6.refs_0_, bf16[256,256]{1,0:T(8,128)(2,1)S(1)} %collective-permute-done.8.refs_1_, f32[1,256]{1,0:T(1,128)S(1)} %fusion.1.refs_6_.refs_2_, f32[1024,256]{1,0:T(8,128)} %finish.2.refs_3_), custom_call_target="tpu_custom_call", output_to_operand_aliasing={{}: (3, {})} | custom-call | tf_op jit(solution)/shard_map/finish/pallas_call | solution.py:222
  (5 shorter events, 0.1 us)
Async XLA Ops:
  0.0 11.2 %copy-start.1 = (bf16[1024,256]{1,0:T(8,128)(2,1)S(1)}, bf16[1024,256]{1,0:T(8,128)(2,1)}, u32[]{:S(2)}) copy-start(bf16[1024,256]{1,0:T(8,128)(2,1)} %own_ref.1) | copy-start | bytes 1572868
  0.0 11.2 %copy-start = (s32[2,3]{1,0:T(2,128)S(1)}, s32[2,3]{1,0:T(2,128)}, u32[]{:S(2)}) copy-start(s32[2,3]{1,0:T(2,128)} %blocks_ref.8) | copy-start | bytes 76
  0.0 16.8 %collective-permute-start.2 = (bf16[2,1024,256]{2,1,0:T(8,128)(2,1)}, bf16[2,1024,256]{2,1,0:T(8,128)(2,1)S(1)}, u32[]{:S(2)}, u32[]{:S(2)}) collective-permute-start(bf16[2,1024,256]{2,1,0:T(8,128)(2,1)} %param.3), channel_id=1, source_target_pairs={{0,1},{1,0},{2,3},{3,2},{4,5},{5,4},{6,7},{7,6},{8,9},{9,8},{10,11... | collective-permute-start | bytes 3145736 | tf_op jit(solution)/shard_map/ppermute | solution.py:23
  0.0 9.4 %collective-permute-start = (bf16[1024,256]{1,0:T(8,128)(2,1)}, bf16[1024,256]{1,0:T(8,128)(2,1)S(1)}, u32[]{:S(2)}, u32[]{:S(2)}) collective-permute-start(bf16[1024,256]{1,0:T(8,128)(2,1)} %own_ref.1), channel_id=1, source_target_pairs={{0,1},{1,0},{2,3},{3,2},{4,5},{5,4},{6,7},{7,6},{8,9},{9,8},{10,11... | collective-permute-start | bytes 1572872 | tf_op jit(solution)/shard_map/ppermute | solution.py:23
  0.5 10.7 %collective-permute-start.1 = (bf16[1024,256]{1,0:T(8,128)(2,1)}, bf16[1024,256]{1,0:T(8,128)(2,1)S(1)}, u32[]{:S(2)}, u32[]{:S(2)}) collective-permute-start(bf16[1024,256]{1,0:T(8,128)(2,1)} %own_ref.1), channel_id=1, source_target_pairs={{0,0},{7,7},{1,2},{2,1},{3,4},{4,3},{5,6},{6,5},{8,8},{15,15},{9,1... | collective-permute-start | bytes 1572872 | tf_op jit(solution)/shard_map/ppermute | solution.py:31
  3.8 13.0 %collective-permute-start.3 = (bf16[1024,256]{1,0:T(8,128)(2,1)S(1)}, bf16[1024,256]{1,0:T(8,128)(2,1)S(1)}, u32[]{:S(2)}, u32[]{:S(2)}) collective-permute-start(bf16[1024,256]{1,0:T(8,128)(2,1)S(1)} %get-tuple-element.30.own_ref), channel_id=1, source_target_pairs={{0,0},{7,7},{1,2},{2,1},{3,4},{4,3},{5,6},{6,5},{8,8},{15,15},{9,1... | collective-permute-start | bytes 1572872 | tf_op jit(solution)/shard_map/ppermute | solution.py:31
  7.4 16.6 %collective-permute-start.4 = (bf16[1024,256]{1,0:T(8,128)(2,1)S(1)}, bf16[1024,256]{1,0:T(8,128)(2,1)S(1)}, u32[]{:S(2)}, u32[]{:S(2)}) collective-permute-start(bf16[1024,256]{1,0:T(8,128)(2,1)S(1)} %get-tuple-element.29.own_ref), channel_id=1, source_target_pairs={{0,0},{7,7},{1,2},{2,1},{3,4},{4,3},{5,6},{6,5},{8,8},{15,15},{9,1... | collective-permute-start | bytes 1572872 | tf_op jit(solution)/shard_map/ppermute | solution.py:31
  32.4 10.6 %collective-permute-start.6 = (bf16[1040,256]{1,0:T(8,128)(2,1)S(1)}, bf16[1040,256]{1,0:T(8,128)(2,1)S(1)}, u32[]{:S(2)}, u32[]{:S(2)}) collective-permute-start(bf16[1040,256]{1,0:T(8,128)(2,1)S(1)} %shard_map.40), channel_id=1, source_target_pairs={{0,0},{7,7},{1,2},{2,1},{3,4},{4,3},{5,6},{6,5},{8,8},{15,15},{9,1... | collective-permute-start | bytes 1597448 | tf_op jit(solution)/shard_map/ppermute | solution.py:31
  36.5 6.5 %collective-permute-start.5 = (bf16[1040,256]{1,0:T(8,128)(2,1)S(1)}, bf16[1040,256]{1,0:T(8,128)(2,1)S(1)}, u32[]{:S(2)}, u32[]{:S(2)}) collective-permute-start(bf16[1040,256]{1,0:T(8,128)(2,1)S(1)} %get-tuple-element.21), channel_id=1, source_target_pairs={{0,1},{1,0},{2,3},{3,2},{4,5},{5,4},{6,7},{7,6},{8,9},{9,8},{10,11... | collective-permute-start | bytes 1597448 | tf_op jit(solution)/shard_map/ppermute | solution.py:23
  43.3 6.4 %collective-permute-start.7 = (bf16[256,256]{1,0:T(8,128)(2,1)S(1)}, bf16[256,256]{1,0:T(8,128)(2,1)S(1)}, u32[]{:S(2)}, u32[]{:S(2)}) collective-permute-start(bf16[256,256]{1,0:T(8,128)(2,1)S(1)} %get-tuple-element.28), channel_id=1, source_target_pairs={{0,16},{8,24},{16,0},{24,8},{1,17},{9,25},{17,1},{25,9},{2,18},{10... | collective-permute-start | bytes 393224 | tf_op jit(solution)/shard_map/ppermute | solution.py:36
  43.9 7.5 %collective-permute-start.9 = (bf16[256,256]{1,0:T(8,128)(2,1)S(1)}, bf16[256,256]{1,0:T(8,128)(2,1)S(1)}, u32[]{:S(2)}, u32[]{:S(2)}) collective-permute-start(bf16[256,256]{1,0:T(8,128)(2,1)S(1)} %get-tuple-element.27), channel_id=1, source_target_pairs={{0,8},{8,0},{16,24},{24,16},{1,9},{9,1},{17,25},{25,17},{2,10},{10... | collective-permute-start | bytes 393224 | tf_op jit(solution)/shard_map/ppermute | solution.py:36
  45.3 6.6 %collective-permute-start.11 = (bf16[256,256]{1,0:T(8,128)(2,1)S(1)}, bf16[256,256]{1,0:T(8,128)(2,1)S(1)}, u32[]{:S(2)}, u32[]{:S(2)}) collective-permute-start(bf16[256,256]{1,0:T(8,128)(2,1)S(1)} %get-tuple-element.26), channel_id=1, source_target_pairs={{0,16},{8,24},{16,0},{24,8},{1,17},{9,25},{17,1},{25,9},{2,18},{10... | collective-permute-start | bytes 393224 | tf_op jit(solution)/shard_map/ppermute | solution.py:36
  46.9 6.9 %collective-permute-start.13 = (bf16[256,256]{1,0:T(8,128)(2,1)S(1)}, bf16[256,256]{1,0:T(8,128)(2,1)S(1)}, u32[]{:S(2)}, u32[]{:S(2)}) collective-permute-start(bf16[256,256]{1,0:T(8,128)(2,1)S(1)} %get-tuple-element.25), channel_id=1, source_target_pairs={{0,8},{8,0},{16,24},{24,16},{1,9},{9,1},{17,25},{25,17},{2,10},{10... | collective-permute-start | bytes 393224 | tf_op jit(solution)/shard_map/ppermute | solution.py:36
  49.7 10.4 %collective-permute-start.8 = (bf16[256,256]{1,0:T(8,128)(2,1)S(1)}, bf16[256,256]{1,0:T(8,128)(2,1)S(1)}, u32[]{:S(2)}, u32[]{:S(2)}) collective-permute-start(bf16[256,256]{1,0:T(8,128)(2,1)S(1)} %add_convert_fusion.6.refs_0_), channel_id=1, source_target_pairs={{0,8},{8,0},{16,24},{24,16},{1,9},{9,1},{17,25},{25,17},{2,10},{10... | collective-permute-start | bytes 393224 | tf_op jit(solution)/shard_map/ppermute | solution.py:36
  51.3 6.0 %collective-permute-start.10 = (bf16[256,256]{1,0:T(8,128)(2,1)S(1)}, bf16[256,256]{1,0:T(8,128)(2,1)S(1)}, u32[]{:S(2)}, u32[]{:S(2)}) collective-permute-start(bf16[256,256]{1,0:T(8,128)(2,1)S(1)} %add_convert_fusion.4.refs_0_), channel_id=1, source_target_pairs={{0,16},{8,24},{16,0},{24,8},{1,17},{9,25},{17,1},{25,9},{2,18},{10... | collective-permute-start | bytes 393224 | tf_op jit(solution)/shard_map/ppermute | solution.py:36
  51.9 5.8 %collective-permute-start.12 = (bf16[256,256]{1,0:T(8,128)(2,1)S(1)}, bf16[256,256]{1,0:T(8,128)(2,1)S(1)}, u32[]{:S(2)}, u32[]{:S(2)}) collective-permute-start(bf16[256,256]{1,0:T(8,128)(2,1)S(1)} %add_convert_fusion.2.refs_2_), channel_id=1, source_target_pairs={{0,8},{8,0},{16,24},{24,16},{1,9},{9,1},{17,25},{25,17},{2,10},{10... | collective-permute-start | bytes 393224 | tf_op jit(solution)/shard_map/ppermute | solution.py:36
  53.8 5.4 %collective-permute-start.14 = (bf16[256,256]{1,0:T(8,128)(2,1)S(1)}, bf16[256,256]{1,0:T(8,128)(2,1)S(1)}, u32[]{:S(2)}, u32[]{:S(2)}) collective-permute-start(bf16[256,256]{1,0:T(8,128)(2,1)S(1)} %add_convert_fusion.refs_4_), channel_id=1, source_target_pairs={{0,16},{8,24},{16,0},{24,8},{1,17},{9,25},{17,1},{25,9},{2,18},{10... | collective-permute-start | bytes 393224 | tf_op jit(solution)/shard_map/ppermute | solution.py:36

commit v7 on v6

--- a/solution.py
+++ b/solution.py
@@ -231,6 +231,18 @@
     )(*[value for pair in pairs for value in pair], cover, *placed)
 
 
+def last_kernel(subj_count, blk_dev, places, splits, blocks_ref, tmpl_ref, own_ref, near_ref, far_ref, *refs):
+    before = subj_count - 1
+    cols_refs, map_refs = refs[:before], refs[before : 2 * before]
+    map_ref, cols_ref, *tile_refs = refs[2 * before : -3]
+    odd_ref, gram_ref, weight_ref = refs[-3:]
+    polar_kernel(before, blocks_ref, tmpl_ref, own_ref, near_ref, far_ref, map_ref, cols_ref, odd_ref, gram_ref)
+    map_kernel(
+        subj_count, blk_dev, places, splits, blocks_ref,
+        *cols_refs, cols_ref, *map_refs, map_ref, *tile_refs, weight_ref,
+    )
+
+
 def body(series, template, sl_blocks):
     subj_count, frames, width_dev = series.shape
     lights, members = sl_blocks.shape
@@ -258,18 +270,30 @@
     )(sl_blocks, template, tmpl_near, tmpl_far)
 
     maps, cols = [], []
+    blocks = list(range(blk_dev))
+    shapes = [
+        jax.ShapeDtypeStruct((lights, width, width), jnp.bfloat16),
+        jax.ShapeDtypeStruct((frames, lights * width), jnp.bfloat16),
+    ]
+    scratch = [pltpu.VMEM((lights, width, width), jnp.bfloat16)] * 2
     for s in range(subj_count):
-        polar, gathered = call(
-            functools.partial(polar_kernel, s),
-            (
-                jax.ShapeDtypeStruct((lights, width, width), jnp.bfloat16),
-                jax.ShapeDtypeStruct((frames, lights * width), jnp.bfloat16),
-            ),
-            [vmem()] * 5,
-            flops=8 * 10**9,
-            limit=LIMIT,
-            scratch=[pltpu.VMEM((lights, width, width), jnp.bfloat16)] * 2,
-        )(sl_blocks, tmpl_rows, parts[s], near, far[s])
+        halo = (sl_blocks, tmpl_rows, parts[s], near, far[s])
+        last = s == subj_count - 1
+        if last:
+            far_places = [2 * blk_dev + b for b in blocks]
+            polar, gathered, to_far = call(
+                functools.partial(last_kernel, subj_count, blk_dev, far_places, ((frames,),)),
+                shapes + [jax.ShapeDtypeStruct((frames + COUNT_ROWS, width_dev), jnp.bfloat16)],
+                [vmem()] * (5 + 2 * s),
+                flops=8 * 10**9,
+                limit=LIMIT,
+                scratch=scratch
+                + [pltpu.VMEM((blk_dev * BLOCK, subj_count * lights * width), jnp.bfloat16)],
+            )(*halo, *cols, *maps)
+        else:
+            polar, gathered = call(
+                functools.partial(polar_kernel, s), shapes, [vmem()] * 5, flops=8 * 10**9, limit=LIMIT, scratch=scratch
+            )(*halo)
         maps.append(polar)
         cols.append(gathered)
 
@@ -288,8 +312,6 @@
             scratch=[pltpu.VMEM((len(places) * BLOCK, subj_count * lights * width), jnp.bfloat16)],
         )(lists, *cols, *maps)
 
-    blocks = list(range(blk_dev))
-    (to_far,) = mapped(sl_blocks, [2 * blk_dev + b for b in blocks], ((frames,),), (jnp.bfloat16,))
     from_far = swap_far(to_far)
     lists, _ = lax.optimization_barrier((sl_blocks, to_far))
     to_near, *own = mapped(
@@ -302,12 +324,14 @@
         return mine + from_near[lo:hi].astype(jnp.float32) + keep * from_far[lo:hi].astype(jnp.float32)
 
     rows = frames // PIECES
-    per_vertex = joined(own[0][rows : rows + 1], frames, frames + 1)
-    halves = [joined(own[h][:rows], h * rows, (h + 1) * rows) for h in range(PIECES)]
+    halves = [joined(own[0][:rows], 0, rows).astype(jnp.bfloat16)]
+    halves[0], from_far, from_near = lax.optimization_barrier((halves[0], from_far, from_near))
+    halves += [joined(own[h][:rows], h * rows, (h + 1) * rows) for h in range(1, PIECES)]
     subj_size = lax.axis_size("subj")
     distances = []
     while 2 ** len(distances) < subj_size:
         distances.append(2 ** len(distances))
+    per_vertex = joined(own[0][rows : rows + 1], frames, frames + 1)
     pairs = []
     for step in range(len(distances)):
         pairs = []

time: 61.3 us -> 61.1 us (level)
  the two profiles are of different devices: /device:TPU:12 before, /device:TPU:16 now
where the time goes in v7:
time: 61.1 us; the launch traced here: 60.9 us
  starting transfers between devices  21.2 us (35%)
  Pallas kernels  20.1 us (33%)
  waiting for transfers between devices  17.7 us (29%)
  local copies, waits for them, and re-layouts  1.28 us (2%)
    ppermute x4, waiting for transfers between devices, swap_far(): return lax.ppermute(value, 'cortex', route)  11.4 us
    ppermute x4, starting transfers between devices, swap_far(): return lax.ppermute(value, 'cortex', route)  9.91 us
    ppermute x8, starting transfers between devices, swap_subj(): lax.ppermute(value, 'subj', [(i, i ^ distance) for i in range(count)])  9.41 us
    pallas_call x1, Pallas kernels, body(): call(functools.partial(last_kernel, subj_count, blk_dev, far_places, ((fr...  8.34 us
    pallas_call x1, Pallas kernels, body(): call(functools.partial(polar_kernel, s), shapes, [vmem()] * 5, flops=8 *...  7.1 us
    ppermute x8, waiting for transfers between devices, swap_subj(): lax.ppermute(value, 'subj', [(i, i ^ distance) for i in range(count)])  6.34 us
    pallas_call x1, Pallas kernels, mapped(): call(functools.partial(map_kernel, subj_count, blk_dev, places, splits),...  1.99 us
    ppermute x3, starting transfers between devices, swap_near(): return lax.ppermute(value, 'cortex', [(i, i ^ 1) for i in range(count)])  1.85 us
  transfers between devices with their start and end apart: 15, of which 8 were waited for; matrix products, arithmetic and copies ran while one was open for 2% of the time, Pallas kernels for 18%

profile of v7, /device:TPU:16, one launch (start us, length us, event | category | flops | bytes accessed | tf_op | source)
XLA Modules:
  0.0 60.9 jit_solution(6701734018960253624)
XLA Ops:
  0.0 0.0 copy-start
  0.0 0.0 copy-start.1
  0.0 0.0 collective-permute-start.2
  0.0 0.5 collective-permute-start
  0.5 2.0 %collective-permute-start.1 = (bf16[1024,256]{1,0:T(8,128)(2,1)}, bf16[1024,256]{1,0:T(8,128)(2,1)S(1)}, u32[]{:S(2)}, u32[]{:S(2)}) collective-permute-start(bf16[1024,256]{1,0:T(8,128)(2,1)} %own_ref.1), channel_id=1, source_target_pairs={{0,0},{7,7},{1,2},{2,1},{3,4},{4,3},{5,6},{6,5},{8,8},{15,15},{9,1... | collective-permute-start | bytes 1572872 | tf_op jit(solution)/shard_map/ppermute | solution.py:31
  2.5 1.3 %slice_bitcast_fusion = (bf16[1024,256]{1,0:T(8,128)(2,1)S(1)}, bf16[1024,256]{1,0:T(8,128)(2,1)S(1)}) fusion(bf16[2,1024,256]{2,1,0:T(8,128)(2,1)} %param.3), kind=kLoop, calls=%fused_computation | loop fusion | bytes 2097152 | tf_op jit(solution)/shard_map/squeeze | solution.py:258
  3.8 3.5 %collective-permute-start.4 = (bf16[1024,256]{1,0:T(8,128)(2,1)S(1)}, bf16[1024,256]{1,0:T(8,128)(2,1)S(1)}, u32[]{:S(2)}, u32[]{:S(2)}) collective-permute-start(bf16[1024,256]{1,0:T(8,128)(2,1)S(1)} %get-tuple-element.36.own_ref), channel_id=1, source_target_pairs={{0,0},{7,7},{1,2},{2,1},{3,4},{4,3},{5,6},{6,5},{8,8},{15,15},{9,1... | collective-permute-start | bytes 1572872 | tf_op jit(solution)/shard_map/ppermute | solution.py:31
  7.4 2.0 %collective-permute-start.3 = (bf16[1024,256]{1,0:T(8,128)(2,1)S(1)}, bf16[1024,256]{1,0:T(8,128)(2,1)S(1)}, u32[]{:S(2)}, u32[]{:S(2)}) collective-permute-start(bf16[1024,256]{1,0:T(8,128)(2,1)S(1)} %get-tuple-element.37.own_ref), channel_id=1, source_target_pairs={{0,0},{7,7},{1,2},{2,1},{3,4},{4,3},{5,6},{6,5},{8,8},{15,15},{9,1... | collective-permute-start | bytes 1572872 | tf_op jit(solution)/shard_map/ppermute | solution.py:31
  9.4 0.0 collective-permute-done.near_ref
  9.4 1.8 %collective-permute-done.1.far_ref = bf16[1024,256]{1,0:T(8,128)(2,1)S(1)} collective-permute-done((bf16[1024,256]{1,0:T(8,128)(2,1)}, bf16[1024,256]{1,0:T(8,128)(2,1)S(1)}, u32[]{:S(2)}, u32[]{:S(2)}) %collective-permute-start.1) | collective-permute-done | bytes 524320 | tf_op jit(solution)/shard_map/ppermute | solution.py:31
  11.2 0.0 copy-done
  11.2 0.0 copy-done.1
  11.2 1.0 %shard_map.37.tmpl_ref = bf16[2,384,1024]{2,1,0:T(8,128)(2,1)S(1)} custom-call(s32[2,3]{1,0:T(2,128)S(1)} %copy-done.1, bf16[1024,256]{1,0:T(8,128)(2,1)S(1)} %copy-done, bf16[1024,256]{1,0:T(8,128)(2,1)S(1)} %collective-permute-done.near_ref, bf16[1024,256]{1,0:T(8,128)(2,1)S(1)} %collective-permute-done.1.far_ref), custom_call_target="tpu_custom_call" | custom-call | flops 1000000000 | bytes 1572864 | tf_op jit(solution)/shard_map/pallas_call | solution.py:264
  12.2 4.7 %collective-permute-done.4.far_ref = bf16[1024,256]{1,0:T(8,128)(2,1)S(1)} collective-permute-done((bf16[1024,256]{1,0:T(8,128)(2,1)S(1)}, bf16[1024,256]{1,0:T(8,128)(2,1)S(1)}, u32[]{:S(2)}, u32[]{:S(2)}) %collective-permute-start.4) | collective-permute-done | bytes 524320 | tf_op jit(solution)/shard_map/ppermute | solution.py:31
  16.8 0.0 collective-permute-done.2.near_ref
  16.8 7.1 %shard_map.38 = (bf16[2,384,384]{2,1,0:T(8,128)(2,1)S(1)}, bf16[1024,768]{1,0:T(8,128)(2,1)S(1)}) custom-call(s32[2,3]{1,0:T(2,128)S(1)} %copy-done.1, bf16[2,384,1024]{2,1,0:T(8,128)(2,1)S(1)} %shard_map.37.tmpl_ref, bf16[1024,256]{1,0:T(8,128)(2,1)S(1)} %get-tuple-element.36.own_ref, bf16[2,1024,256]{2,1,0:T(8,128)(2,1)S(1)} %collective-permute-done.2.near_ref, ...), custom_call_target="tpu_custom_call" | custom-call | flops 8000000000 | bytes 2162688 | tf_op jit(solution)/shard_map/pallas_call | solution.py:294
  23.9 0.0 collective-permute-done.3.far_ref
  24.0 8.3 %shard_map.39 = (bf16[2,384,384]{2,1,0:T(8,128)(2,1)S(1)}, bf16[1024,768]{1,0:T(8,128)(2,1)S(1)}, bf16[1040,256]{1,0:T(8,128)(2,1)S(1)}) custom-call(s32[2,3]{1,0:T(2,128)S(1)} %copy-done.1, bf16[2,384,1024]{2,1,0:T(8,128)(2,1)S(1)} %shard_map.37.tmpl_ref, bf16[1024,256]{1,0:T(8,128)(2,1)S(1)} %get-tuple-element.37.own_ref, ...), custom_call_target="tpu_custom_call" | custom-call | flops 8000000000 | bytes 2695168 | tf_op jit(solution)/shard_map/pallas_call | solution.py:284
  32.3 2.3 %collective-permute-start.6 = (bf16[1040,256]{1,0:T(8,128)(2,1)S(1)}, bf16[1040,256]{1,0:T(8,128)(2,1)S(1)}, u32[]{:S(2)}, u32[]{:S(2)}) collective-permute-start(bf16[1040,256]{1,0:T(8,128)(2,1)S(1)} %get-tuple-element.21), channel_id=1, source_target_pairs={{0,0},{7,7},{1,2},{2,1},{3,4},{4,3},{5,6},{6,5},{8,8},{15,15},{9,1... | collective-permute-start | bytes 1597448 | tf_op jit(solution)/shard_map/ppermute | solution.py:31
  34.6 2.0 %shard_map.40 = (bf16[1040,256]{1,0:T(8,128)(2,1)S(1)}, f32[272,256]{1,0:T(8,128)S(1)}, f32[256,256]{1,0:T(8,128)S(1)}, f32[256,256]{1,0:T(8,128)S(1)}, f32[256,256]{1,0:T(8,128)S(1)}) custom-call(s32[2,3]{1,0:T(2,128)S(1)} %copy-done.1, bf16[1024,768]{1,0:T(8,128)(2,1)S(1)} %get-tuple-element.19.refs_0_, bf16[1024,768]{1,0:T(8,128)(2,1)S(1)} %get-tuple-element.23.refs_1_, ...), custom_call_target="tpu_custom_call" | custom-call | flops 1600000000 | bytes 1597440 | tf_op jit(solution)/shard_map/pallas_call | solution.py:306
  36.6 1.3 %collective-permute-start.5 = (bf16[1040,256]{1,0:T(8,128)(2,1)S(1)}, bf16[1040,256]{1,0:T(8,128)(2,1)S(1)}, u32[]{:S(2)}, u32[]{:S(2)}) collective-permute-start(bf16[1040,256]{1,0:T(8,128)(2,1)S(1)} %get-tuple-element.27), channel_id=1, source_target_pairs={{0,1},{1,0},{2,3},{3,2},{4,5},{5,4},{6,7},{7,6},{8,9},{9,8},{10,11... | collective-permute-start | bytes 1597448 | tf_op jit(solution)/shard_map/ppermute | solution.py:23
  38.0 4.9 %collective-permute-done.6 = bf16[1040,256]{1,0:T(8,128)(2,1)S(1)} collective-permute-done((bf16[1040,256]{1,0:T(8,128)(2,1)S(1)}, bf16[1040,256]{1,0:T(8,128)(2,1)S(1)}, u32[]{:S(2)}, u32[]{:S(2)}) %collective-permute-start.6) | collective-permute-done | bytes 532512 | tf_op jit(solution)/shard_map/ppermute | solution.py:31
  42.9 0.0 collective-permute-done.5
  42.9 0.1 add_convert_fusion.7
  43.0 0.2 add_convert_fusion.1
  43.1 1.6 %collective-permute-start.7 = (bf16[256,256]{1,0:T(8,128)(2,1)S(1)}, bf16[256,256]{1,0:T(8,128)(2,1)S(1)}, u32[]{:S(2)}, u32[]{:S(2)}) collective-permute-start(bf16[256,256]{1,0:T(8,128)(2,1)S(1)} %get-tuple-element.35), channel_id=1, source_target_pairs={{0,16},{8,24},{16,0},{24,8},{1,17},{9,25},{17,1},{25,9},{2,18},{10... | collective-permute-start | bytes 393224 | tf_op jit(solution)/shard_map/ppermute | solution.py:36
  44.7 1.5 %collective-permute-start.9 = (bf16[256,256]{1,0:T(8,128)(2,1)S(1)}, bf16[256,256]{1,0:T(8,128)(2,1)S(1)}, u32[]{:S(2)}, u32[]{:S(2)}) collective-permute-start(bf16[256,256]{1,0:T(8,128)(2,1)S(1)} %add_convert_fusion.7), channel_id=1, source_target_pairs={{0,8},{8,0},{16,24},{24,16},{1,9},{9,1},{17,25},{25,17},{2,10},{10... | collective-permute-start | bytes 393224 | tf_op jit(solution)/shard_map/ppermute | solution.py:36
  46.2 0.5 collective-permute-start.11
  46.7 0.5 collective-permute-start.13
  47.3 2.1 %collective-permute-done.7 = bf16[256,256]{1,0:T(8,128)(2,1)S(1)} collective-permute-done((bf16[256,256]{1,0:T(8,128)(2,1)S(1)}, bf16[256,256]{1,0:T(8,128)(2,1)S(1)}, u32[]{:S(2)}, u32[]{:S(2)}) %collective-permute-start.7) | collective-permute-done | bytes 131104 | tf_op jit(solution)/shard_map/ppermute | solution.py:36
  49.4 1.8 %collective-permute-start.8 = (bf16[256,256]{1,0:T(8,128)(2,1)S(1)}, bf16[256,256]{1,0:T(8,128)(2,1)S(1)}, u32[]{:S(2)}, u32[]{:S(2)}) collective-permute-start(bf16[256,256]{1,0:T(8,128)(2,1)S(1)} %add_convert_fusion.5.refs_0_), channel_id=1, source_target_pairs={{0,8},{8,0},{16,24},{24,16},{1,9},{9,1},{17,25},{25,17},{2,10},{10... | collective-permute-start | bytes 393224 | tf_op jit(solution)/shard_map/ppermute | solution.py:36
  51.2 0.0 collective-permute-done.9
  51.2 1.6 %collective-permute-start.10 = (bf16[256,256]{1,0:T(8,128)(2,1)S(1)}, bf16[256,256]{1,0:T(8,128)(2,1)S(1)}, u32[]{:S(2)}, u32[]{:S(2)}) collective-permute-start(bf16[256,256]{1,0:T(8,128)(2,1)S(1)} %add_convert_fusion.4.refs_0_), channel_id=1, source_target_pairs={{0,16},{8,24},{16,0},{24,8},{1,17},{9,25},{17,1},{25,9},{2,18},{10... | collective-permute-start | bytes 393224 | tf_op jit(solution)/shard_map/ppermute | solution.py:36
  52.8 0.0 collective-permute-done.11
  52.8 0.6 collective-permute-start.12
  53.4 0.5 collective-permute-done.13
  53.9 1.3 %collective-permute-start.14 = (bf16[256,256]{1,0:T(8,128)(2,1)S(1)}, bf16[256,256]{1,0:T(8,128)(2,1)S(1)}, u32[]{:S(2)}, u32[]{:S(2)}) collective-permute-start(bf16[256,256]{1,0:T(8,128)(2,1)S(1)} %add_convert_fusion.refs_4_), channel_id=1, source_target_pairs={{0,16},{8,24},{16,0},{24,8},{1,17},{9,25},{17,1},{25,9},{2,18},{10... | collective-permute-start | bytes 393224 | tf_op jit(solution)/shard_map/ppermute | solution.py:36
  55.2 1.9 %collective-permute-done.10.refs_1_ = bf16[256,256]{1,0:T(8,128)(2,1)S(1)} collective-permute-done((bf16[256,256]{1,0:T(8,128)(2,1)S(1)}, bf16[256,256]{1,0:T(8,128)(2,1)S(1)}, u32[]{:S(2)}, u32[]{:S(2)}) %collective-permute-start.10) | collective-permute-done | bytes 131104 | tf_op jit(solution)/shard_map/ppermute | solution.py:36
  57.2 1.5 %collective-permute-done.12.refs_3_ = bf16[256,256]{1,0:T(8,128)(2,1)S(1)} collective-permute-done((bf16[256,256]{1,0:T(8,128)(2,1)S(1)}, bf16[256,256]{1,0:T(8,128)(2,1)S(1)}, u32[]{:S(2)}, u32[]{:S(2)}) %collective-permute-start.12) | collective-permute-done | bytes 131104 | tf_op jit(solution)/shard_map/ppermute | solution.py:36
  58.6 0.4 collective-permute-done.14.refs_5_
  59.1 0.9 %finish.2.refs_3_ = f32[1024,256]{1,0:T(8,128)} custom-call(bf16[256,256]{1,0:T(8,128)(2,1)S(1)} %add_convert_fusion.4.refs_0_, bf16[256,256]{1,0:T(8,128)(2,1)S(1)} %collective-permute-done.10.refs_1_, bf16[256,256]{1,0:T(8,128)(2,1)S(1)} %add_convert_fusion.2.refs_2_, bf16[256,256]{1,0:T(8,128)(2,1)S(1)} %collective-permute-done.12.refs_3_, ...), custom_call_target="tpu_custom_call" | custom-call | tf_op jit(solution)/shard_map/finish/pallas_call | solution.py:222
  60.0 0.0 collective-permute-done.8.refs_1_
  60.0 0.8 %finish.3 = f32[1024,256]{1,0:T(8,128)} custom-call(bf16[256,256]{1,0:T(8,128)(2,1)S(1)} %add_convert_fusion.5.refs_0_, bf16[256,256]{1,0:T(8,128)(2,1)S(1)} %collective-permute-done.8.refs_1_, f32[1,256]{1,0:T(1,128)S(1)} %multiply_add_fusion.refs_6_.refs_2_, f32[1024,256]{1,0:T(8,128)} %finish.2.refs_3_), custom_call_target="tpu_custom_call", output_to_operand_aliasing={{}: (3, {})} | custom-call | tf_op jit(solution)/shard_map/finish/pallas_call | solution.py:222
  (5 shorter events, 0.1 us)
Async XLA Ops:
  0.0 11.2 %copy-start = (bf16[1024,256]{1,0:T(8,128)(2,1)S(1)}, bf16[1024,256]{1,0:T(8,128)(2,1)}, u32[]{:S(2)}) copy-start(bf16[1024,256]{1,0:T(8,128)(2,1)} %own_ref.1) | copy-start | bytes 1572868
  0.0 11.2 %copy-start.1 = (s32[2,3]{1,0:T(2,128)S(1)}, s32[2,3]{1,0:T(2,128)}, u32[]{:S(2)}) copy-start(s32[2,3]{1,0:T(2,128)} %blocks_ref.6) | copy-start | bytes 76
  0.0 16.8 %collective-permute-start.2 = (bf16[2,1024,256]{2,1,0:T(8,128)(2,1)}, bf16[2,1024,256]{2,1,0:T(8,128)(2,1)S(1)}, u32[]{:S(2)}, u32[]{:S(2)}) collective-permute-start(bf16[2,1024,256]{2,1,0:T(8,128)(2,1)} %param.3), channel_id=1, source_target_pairs={{0,1},{1,0},{2,3},{3,2},{4,5},{5,4},{6,7},{7,6},{8,9},{9,8},{10,11... | collective-permute-start | bytes 3145736 | tf_op jit(solution)/shard_map/ppermute | solution.py:23
  0.0 9.4 %collective-permute-start = (bf16[1024,256]{1,0:T(8,128)(2,1)}, bf16[1024,256]{1,0:T(8,128)(2,1)S(1)}, u32[]{:S(2)}, u32[]{:S(2)}) collective-permute-start(bf16[1024,256]{1,0:T(8,128)(2,1)} %own_ref.1), channel_id=1, source_target_pairs={{0,1},{1,0},{2,3},{3,2},{4,5},{5,4},{6,7},{7,6},{8,9},{9,8},{10,11... | collective-permute-start | bytes 1572872 | tf_op jit(solution)/shard_map/ppermute | solution.py:23
  0.5 10.7 %collective-permute-start.1 = (bf16[1024,256]{1,0:T(8,128)(2,1)}, bf16[1024,256]{1,0:T(8,128)(2,1)S(1)}, u32[]{:S(2)}, u32[]{:S(2)}) collective-permute-start(bf16[1024,256]{1,0:T(8,128)(2,1)} %own_ref.1), channel_id=1, source_target_pairs={{0,0},{7,7},{1,2},{2,1},{3,4},{4,3},{5,6},{6,5},{8,8},{15,15},{9,1... | collective-permute-start | bytes 1572872 | tf_op jit(solution)/shard_map/ppermute | solution.py:31
  3.8 13.0 %collective-permute-start.4 = (bf16[1024,256]{1,0:T(8,128)(2,1)S(1)}, bf16[1024,256]{1,0:T(8,128)(2,1)S(1)}, u32[]{:S(2)}, u32[]{:S(2)}) collective-permute-start(bf16[1024,256]{1,0:T(8,128)(2,1)S(1)} %get-tuple-element.36.own_ref), channel_id=1, source_target_pairs={{0,0},{7,7},{1,2},{2,1},{3,4},{4,3},{5,6},{6,5},{8,8},{15,15},{9,1... | collective-permute-start | bytes 1572872 | tf_op jit(solution)/shard_map/ppermute | solution.py:31
  7.4 16.6 %collective-permute-start.3 = (bf16[1024,256]{1,0:T(8,128)(2,1)S(1)}, bf16[1024,256]{1,0:T(8,128)(2,1)S(1)}, u32[]{:S(2)}, u32[]{:S(2)}) collective-permute-start(bf16[1024,256]{1,0:T(8,128)(2,1)S(1)} %get-tuple-element.37.own_ref), channel_id=1, source_target_pairs={{0,0},{7,7},{1,2},{2,1},{3,4},{4,3},{5,6},{6,5},{8,8},{15,15},{9,1... | collective-permute-start | bytes 1572872 | tf_op jit(solution)/shard_map/ppermute | solution.py:31
  32.3 10.6 %collective-permute-start.6 = (bf16[1040,256]{1,0:T(8,128)(2,1)S(1)}, bf16[1040,256]{1,0:T(8,128)(2,1)S(1)}, u32[]{:S(2)}, u32[]{:S(2)}) collective-permute-start(bf16[1040,256]{1,0:T(8,128)(2,1)S(1)} %get-tuple-element.21), channel_id=1, source_target_pairs={{0,0},{7,7},{1,2},{2,1},{3,4},{4,3},{5,6},{6,5},{8,8},{15,15},{9,1... | collective-permute-start | bytes 1597448 | tf_op jit(solution)/shard_map/ppermute | solution.py:31
  36.6 6.3 %collective-permute-start.5 = (bf16[1040,256]{1,0:T(8,128)(2,1)S(1)}, bf16[1040,256]{1,0:T(8,128)(2,1)S(1)}, u32[]{:S(2)}, u32[]{:S(2)}) collective-permute-start(bf16[1040,256]{1,0:T(8,128)(2,1)S(1)} %get-tuple-element.27), channel_id=1, source_target_pairs={{0,1},{1,0},{2,3},{3,2},{4,5},{5,4},{6,7},{7,6},{8,9},{9,8},{10,11... | collective-permute-start | bytes 1597448 | tf_op jit(solution)/shard_map/ppermute | solution.py:23
  43.1 6.2 %collective-permute-start.7 = (bf16[256,256]{1,0:T(8,128)(2,1)S(1)}, bf16[256,256]{1,0:T(8,128)(2,1)S(1)}, u32[]{:S(2)}, u32[]{:S(2)}) collective-permute-start(bf16[256,256]{1,0:T(8,128)(2,1)S(1)} %get-tuple-element.35), channel_id=1, source_target_pairs={{0,16},{8,24},{16,0},{24,8},{1,17},{9,25},{17,1},{25,9},{2,18},{10... | collective-permute-start | bytes 393224 | tf_op jit(solution)/shard_map/ppermute | solution.py:36
  44.7 6.4 %collective-permute-start.9 = (bf16[256,256]{1,0:T(8,128)(2,1)S(1)}, bf16[256,256]{1,0:T(8,128)(2,1)S(1)}, u32[]{:S(2)}, u32[]{:S(2)}) collective-permute-start(bf16[256,256]{1,0:T(8,128)(2,1)S(1)} %add_convert_fusion.7), channel_id=1, source_target_pairs={{0,8},{8,0},{16,24},{24,16},{1,9},{9,1},{17,25},{25,17},{2,10},{10... | collective-permute-start | bytes 393224 | tf_op jit(solution)/shard_map/ppermute | solution.py:36
  46.2 6.6 %collective-permute-start.11 = (bf16[256,256]{1,0:T(8,128)(2,1)S(1)}, bf16[256,256]{1,0:T(8,128)(2,1)S(1)}, u32[]{:S(2)}, u32[]{:S(2)}) collective-permute-start(bf16[256,256]{1,0:T(8,128)(2,1)S(1)} %get-tuple-element.34), channel_id=1, source_target_pairs={{0,16},{8,24},{16,0},{24,8},{1,17},{9,25},{17,1},{25,9},{2,18},{10... | collective-permute-start | bytes 393224 | tf_op jit(solution)/shard_map/ppermute | solution.py:36
  46.7 7.2 %collective-permute-start.13 = (bf16[256,256]{1,0:T(8,128)(2,1)S(1)}, bf16[256,256]{1,0:T(8,128)(2,1)S(1)}, u32[]{:S(2)}, u32[]{:S(2)}) collective-permute-start(bf16[256,256]{1,0:T(8,128)(2,1)S(1)} %get-tuple-element.33), channel_id=1, source_target_pairs={{0,8},{8,0},{16,24},{24,16},{1,9},{9,1},{17,25},{25,17},{2,10},{10... | collective-permute-start | bytes 393224 | tf_op jit(solution)/shard_map/ppermute | solution.py:36
  49.4 10.6 %collective-permute-start.8 = (bf16[256,256]{1,0:T(8,128)(2,1)S(1)}, bf16[256,256]{1,0:T(8,128)(2,1)S(1)}, u32[]{:S(2)}, u32[]{:S(2)}) collective-permute-start(bf16[256,256]{1,0:T(8,128)(2,1)S(1)} %add_convert_fusion.5.refs_0_), channel_id=1, source_target_pairs={{0,8},{8,0},{16,24},{24,16},{1,9},{9,1},{17,25},{25,17},{2,10},{10... | collective-permute-start | bytes 393224 | tf_op jit(solution)/shard_map/ppermute | solution.py:36
  51.2 6.0 %collective-permute-start.10 = (bf16[256,256]{1,0:T(8,128)(2,1)S(1)}, bf16[256,256]{1,0:T(8,128)(2,1)S(1)}, u32[]{:S(2)}, u32[]{:S(2)}) collective-permute-start(bf16[256,256]{1,0:T(8,128)(2,1)S(1)} %add_convert_fusion.4.refs_0_), channel_id=1, source_target_pairs={{0,16},{8,24},{16,0},{24,8},{1,17},{9,25},{17,1},{25,9},{2,18},{10... | collective-permute-start | bytes 393224 | tf_op jit(solution)/shard_map/ppermute | solution.py:36
  52.8 5.8 %collective-permute-start.12 = (bf16[256,256]{1,0:T(8,128)(2,1)S(1)}, bf16[256,256]{1,0:T(8,128)(2,1)S(1)}, u32[]{:S(2)}, u32[]{:S(2)}) collective-permute-start(bf16[256,256]{1,0:T(8,128)(2,1)S(1)} %add_convert_fusion.2.refs_2_), channel_id=1, source_target_pairs={{0,8},{8,0},{16,24},{24,16},{1,9},{9,1},{17,25},{25,17},{2,10},{10... | collective-permute-start | bytes 393224 | tf_op jit(solution)/shard_map/ppermute | solution.py:36
  53.9 5.1 %collective-permute-start.14 = (bf16[256,256]{1,0:T(8,128)(2,1)S(1)}, bf16[256,256]{1,0:T(8,128)(2,1)S(1)}, u32[]{:S(2)}, u32[]{:S(2)}) collective-permute-start(bf16[256,256]{1,0:T(8,128)(2,1)S(1)} %add_convert_fusion.refs_4_), channel_id=1, source_target_pairs={{0,16},{8,24},{16,0},{24,8},{1,17},{9,25},{17,1},{25,9},{2,18},{10... | collective-permute-start | bytes 393224 | tf_op jit(solution)/shard_map/ppermute | solution.py:36
